TPU v7x, 8 devices: a whole 2x2x1 slice. The times are simulated.
8 devices in a mesh: bz: 2 (over z, y), by: 2 (over x), bx: 2 (over core).
Axes of the slice: x: 2, y: 2, z: 1, core: 2. Of those that a mesh axis runs over, the one named last changes fastest.
Arguments:
- positions: float32 [13824, 3], P(('bz', 'by', 'bx'))
- velocities: float32 [13824, 3], P(('bz', 'by', 'bx'))
- forces: float32 [13824, 3], P(('bz', 'by', 'bx'))
- atom_ids: int32 [13824], P(('bz', 'by', 'bx'))
- valid_mask: int32 [13824], P(('bz', 'by', 'bx'))
Outputs:
- output 1: float32 [13824, 3], P(('bz', 'by', 'bx'))
- output 2: float32 [13824, 3], P(('bz', 'by', 'bx'))
- output 3: float32 [13824, 3], P(('bz', 'by', 'bx'))
- output 4: int32 [13824], P(('bz', 'by', 'bx'))
- output 5: int32 [13824], P(('bz', 'by', 'bx'))
- output 6: float32 [], replicated
All inputs are finite; a program needn't handle non-finite values.
Results may differ from a plain program's by a relative error of at most 0.001.
Values sent between devices are 32-bit elements.
A program may use at most 1 GiB of HBM per device.

v0:
```python
import jax
import jax.numpy as jnp
from jax import lax
from jax.sharding import PartitionSpec as P

TIME_STEP = 0.005
RCUT = 2.5
DENSITY = 0.8442
SPACING = (1.0 / DENSITY) ** (1.0 / 3.0)
GHOST_LAYERS = 2
FAR_AWAY = 1.0e4
BIG_KEY = 2147483647
BRICK_AXES = ("bz", "by", "bx")


def pair_terms(dist_sq, pair_mask):
    safe_sq = jnp.where(pair_mask, dist_sq, 1.0)
    inv_r2 = 1.0 / safe_sq
    inv_r6 = inv_r2 * inv_r2 * inv_r2
    pair_dist = jnp.sqrt(safe_sq)
    cut_inv6 = RCUT ** -6
    u_cut = 4.0 * (cut_inv6 * cut_inv6 - cut_inv6)
    du_cut = (-48.0 * cut_inv6 * cut_inv6 + 24.0 * cut_inv6) / RCUT
    energy = 4.0 * (inv_r6 * inv_r6 - inv_r6) - u_cut - (pair_dist - RCUT) * du_cut
    f_over_r = (48.0 * inv_r6 * inv_r6 - 24.0 * inv_r6) * inv_r2 + du_cut / pair_dist
    return jnp.where(pair_mask, energy, 0.0), jnp.where(pair_mask, f_over_r, 0.0)


def shift_pairs(axis_sizes, offset):
    size_z, size_y, size_x = axis_sizes
    perm_pairs = []
    for src_z in range(size_z):
        for src_y in range(size_y):
            for src_x in range(size_x):
                dst_index = (((src_z + offset[2]) % size_z) * size_y + (src_y + offset[1]) % size_y) * size_x + (src_x + offset[0]) % size_x
                perm_pairs.append(((src_z * size_y + src_y) * size_x + src_x, dst_index))
    return perm_pairs


def pack_rows(values, keep, capacity, fill):
    slot_rank = jnp.cumsum(keep.astype(jnp.int32)) - 1
    dest_slot = jnp.where(keep, slot_rank, capacity)
    base = jnp.full((capacity,) + values.shape[1:], fill, values.dtype)
    return base.at[dest_slot].set(values, mode="drop")


def solution(mesh):
    size_x = mesh.shape["bx"]
    size_y = mesh.shape["by"]
    size_z = mesh.shape["bz"]
    axis_sizes = (size_z, size_y, size_x)
    offsets = [(step_x, step_y, step_z) for step_z in (-1, 0, 1) for step_y in (-1, 0, 1) for step_x in (-1, 0, 1) if (step_x, step_y, step_z) != (0, 0, 0)]
    row_spec = P(BRICK_AXES, None)
    flat_spec = P(BRICK_AXES)

    def run(positions, velocities, forces, atom_ids, valid_mask):
        capacity = positions.shape[0] // (size_x * size_y * size_z)
        sites = int(round(capacity ** (1.0 / 3.0)))
        brick_side = sites * SPACING
        box_len = jnp.array([size_x, size_y, size_z], jnp.float32) * brick_side
        mig_caps = []
        for offset in offsets:
            moved_dims = sum(abs(component) for component in offset)
            mig_caps.append([(sites - 2) ** 2, sites - 2, 1][moved_dims - 1])
        mig_starts = []
        running = 0
        for mig_cap in mig_caps:
            mig_starts.append(running)
            running = running + mig_cap
        mig_total = running
        start_table = jnp.array(mig_starts[:13] + [0] + mig_starts[13:], jnp.int32)
        ghost_caps = [GHOST_LAYERS * sites * sites, GHOST_LAYERS * sites * (sites + 2 * GHOST_LAYERS), GHOST_LAYERS * (sites + 2 * GHOST_LAYERS) ** 2]

        def local_step(pos_rows, vel_rows, frc_rows, id_rows, valid_rows):
            brick_lo = jnp.stack([lax.axis_index("bx"), lax.axis_index("by"), lax.axis_index("bz")]).astype(jnp.float32) * brick_side
            is_live = valid_rows == 1
            v_half = vel_rows + 0.5 * TIME_STEP * frc_rows
            moved_pos = pos_rows + TIME_STEP * v_half
            moved_pos = moved_pos - box_len * jnp.floor(moved_pos / box_len)
            rel_pos = moved_pos - (brick_lo + 0.5 * brick_side)
            rel_pos = rel_pos - box_len * jnp.floor(rel_pos / box_len + 0.5)
            brick_step = jnp.clip(jnp.floor(rel_pos / brick_side + 0.5).astype(jnp.int32), -1, 1)
            dir_code = (brick_step[:, 2] + 1) * 9 + (brick_step[:, 1] + 1) * 3 + brick_step[:, 0] + 1
            leaving = is_live & (dir_code != 13)
            staying = is_live & (dir_code == 13)
            onehot = (dir_code[:, None] == jnp.arange(27)[None, :]) & leaving[:, None]
            onehot_int = onehot.astype(jnp.int32)
            dir_rank = jnp.sum((jnp.cumsum(onehot_int, axis=0) - 1) * onehot_int, axis=1)
            mig_slot = jnp.where(leaving, start_table[dir_code] + dir_rank, mig_total)
            payload = jnp.concatenate([moved_pos, v_half], axis=1)
            out_rows = jnp.zeros((mig_total, 6), jnp.float32).at[mig_slot].set(payload, mode="drop")
            out_ids = jnp.full((mig_total,), -1, jnp.int32).at[mig_slot].set(id_rows, mode="drop")
            recv_rows = []
            recv_ids = []
            for offset, mig_start, mig_cap in zip(offsets, mig_starts, mig_caps):
                perm_pairs = shift_pairs(axis_sizes, offset)
                recv_rows.append(lax.ppermute(out_rows[mig_start:mig_start + mig_cap], BRICK_AXES, perm_pairs))
                recv_ids.append(lax.ppermute(out_ids[mig_start:mig_start + mig_cap], BRICK_AXES, perm_pairs))
            arrived_ids = jnp.concatenate(recv_ids)
            arrived_rows = jnp.concatenate(recv_rows)
            merge_keys = jnp.concatenate([jnp.where(staying, id_rows, BIG_KEY), jnp.where(arrived_ids >= 0, arrived_ids, BIG_KEY)])
            merge_rows = jnp.concatenate([payload, arrived_rows])
            sorted_all = lax.sort([merge_keys] + [merge_rows[:, col_idx] for col_idx in range(6)], num_keys=1)
            own_keys = sorted_all[0][:capacity]
            own_live = own_keys < BIG_KEY
            own_data = jnp.where(own_live[:, None], jnp.stack(sorted_all[1:], axis=1)[:capacity], 0.0)
            own_pos = own_data[:, :3]
            own_vel = own_data[:, 3:]
            own_ids = jnp.where(own_live, own_keys, 0)
            pool_pos = jnp.where(own_live[:, None], own_pos, FAR_AWAY)
            pool_live = own_live
            unit_rows = jnp.eye(3, dtype=jnp.float32)
            for dim_idx, axis_name, ghost_cap in zip(range(3), ("bx", "by", "bz"), ghost_caps):
                axis_len = mesh.shape[axis_name]
                axis_coord = lax.axis_index(axis_name)
                local_coord = pool_pos[:, dim_idx] - brick_lo[dim_idx]
                up_shift = jnp.where(axis_coord == axis_len - 1, -box_len[dim_idx], 0.0) * unit_rows[dim_idx]
                down_shift = jnp.where(axis_coord == 0, box_len[dim_idx], 0.0) * unit_rows[dim_idx]
                send_up = pack_rows(pool_pos + up_shift, pool_live & (local_coord >= brick_side - RCUT), ghost_cap, FAR_AWAY)
                send_down = pack_rows(pool_pos + down_shift, pool_live & (local_coord < RCUT), ghost_cap, FAR_AWAY)
                from_below = lax.ppermute(send_up, axis_name, [(src_idx, (src_idx + 1) % axis_len) for src_idx in range(axis_len)])
                from_above = lax.ppermute(send_down, axis_name, [(src_idx, (src_idx - 1) % axis_len) for src_idx in range(axis_len)])
                new_ghosts = jnp.concatenate([from_below, from_above])
                pool_pos = jnp.concatenate([pool_pos, new_ghosts])
                pool_live = jnp.concatenate([pool_live, new_ghosts[:, 0] < 0.5 * FAR_AWAY])
            own_rows = pool_pos[:capacity]
            pair_delta = own_rows[:, None, :] - pool_pos[None, :, :]
            dist_sq = jnp.sum(pair_delta * pair_delta, axis=-1)
            not_self = jnp.arange(capacity)[:, None] != jnp.arange(pool_pos.shape[0])[None, :]
            pair_mask = own_live[:, None] & pool_live[None, :] & not_self & (dist_sq < RCUT * RCUT)
            pair_energy, f_over_r = pair_terms(dist_sq, pair_mask)
            new_frc = jnp.sum(f_over_r[:, :, None] * pair_delta, axis=1)
            energy = lax.psum(0.5 * jnp.sum(pair_energy), BRICK_AXES)
            new_vel = own_vel + 0.5 * TIME_STEP * new_frc
            return own_pos, new_vel, new_frc, own_ids, own_live.astype(jnp.int32), energy

        stepper = jax.shard_map(local_step, mesh=mesh, in_specs=(row_spec, row_spec, row_spec, flat_spec, flat_spec), out_specs=(row_spec, row_spec, row_spec, flat_spec, flat_spec, P()), check_vma=False)
        return stepper(positions, velocities, forces, atom_ids, valid_mask)

    return run
```

profile of v0, /device:TPU:0, one launch (start us, length us, event | category | flops | bytes accessed | tf_op | source)
XLA Modules:
  0.0 334.4 jit_solution(323756084514153535)
XLA Ops:
  3.0 7.7 %reduce-window.56 = s32[27,14,128]{2,1,0:T(8,128)S(1)} reduce-window(s32[27,14,128]{2,1,0:T(8,128)S(1)} %reshape.348, s32[]{:T(128)} %constant.50.clone.1), window={size=1x1x128 pad=0_0x0_0x127_0}, to_apply=%region_0.1 | reduce-window | flops 6144768 | bytes 387076 | tf_op jit(solution)/shard_map/reduce-window | solution.py:138
  11.5 8.9 %scatter_custom_fusion = s32[728]{0:T(1024)S(1)} fusion(s32[1728]{0:T(1024)S(1)} %compare_select_fusion.13, s32[1728]{0:T(1024)} %param.10, s32[]{:T(128)} %constant.37.clone.1), kind=kCustom, calls=%fused_computation.182 | custom fusion | bytes 3424 | tf_op jit(solution)/shard_map/scatter | solution.py:92
  20.5 4.3 %collective-permute-start.24 = (s32[10]{0:T(128)S(1)}, s32[10]{0:T(128)S(1)}, u32[]{:S(2)}, u32[]{:S(2)}) collective-permute-start(s32[10]{0:T(128)S(1)} %get-tuple-element.124), channel_id=1, source_target_pairs={{0,6},{1,7},{2,4},{3,5},{4,2},{5,3},{6,0},{7,1}} | collective-permute-start | bytes 128 | tf_op jit(solution)/shard_map/ppermute | solution.py:98
  24.8 1.7 collective-permute-start.20
  26.9 8.1 %scatter_custom_fusion.1 = f32[728,6]{1,0:T(8,128)S(1)} fusion(s32[1728]{0:T(1024)S(1)} %compare_select_fusion.13, f32[1728,6]{1,0:T(8,128)S(1)} %copy.176, f32[]{:T(128)} %constant.54.clone.1), kind=kCustom, calls=%fused_computation.36 | custom fusion | bytes 17476 | tf_op jit(solution)/shard_map/scatter | solution.py:91
  35.1 2.6 collective-permute-start.49
  39.4 2.6 collective-permute-start.43
  43.3 2.6 collective-permute-start.32
  47.2 2.6 collective-permute-start.26
  51.1 1.7 collective-permute-start.48
  52.9 2.6 collective-permute-done.50
  55.6 1.5 collective-permute-start.44
  57.2 1.4 collective-permute-done.46
  58.7 1.4 collective-permute-done.44
  67.0 2.3 collective-permute-done.33
  69.4 1.4 collective-permute-start.27
  70.9 1.4 collective-permute-done.29
  74.6 3.2 collective-permute-done.25
  78.4 3.3 collective-permute-done.23
  82.3 3.3 collective-permute-done.19
  86.2 3.3 collective-permute-done.17
  90.1 3.3 collective-permute-done.8
  94.0 3.3 collective-permute-done.6
  97.9 3.3 collective-permute-done.2
  101.8 3.3 collective-permute-done
  105.2 1.7 collective-permute-start.14
  107.0 1.7 collective-permute-start.9
  108.7 1.4 collective-permute-start.7
  110.1 1.7 collective-permute-start.3
  111.9 1.5 collective-permute-start.1
  113.9 1.5 collective-permute-start.15
  116.9 1.5 collective-permute-start.4
  119.0 1.4 collective-permute-start.41
  122.0 5.1 %concatenate.62 = s32[728]{0:T(1024)S(1)} concatenate(s32[1]{0:T(128)} %collective-permute-done, s32[10]{0:T(128)S(1)} %collective-permute-done.1, s32[1]{0:T(128)} %collective-permute-done.2, s32[10]{0:T(128)S(1)} %collective-permute-done.3, s32[100]{0:T(128)S(1)} %collective-permute-done.4, s32[10]{0:T(128)S(1)} %collective-permute-done.5, s32[1]{0:T(128)} %collective-permute-done.6, ...), dimensions={0} | concatenate | bytes 5824 | tf_op jit(solution)/shard_map/concatenate | solution.py:99
  128.6 2.6 collective-permute-done.30
  131.6 7.0 %sort.63 = (s32[2456]{0:T(1024)S(1)}, f32[2456]{0:T(1024)S(1)}, f32[2456]{0:T(1024)S(1)}, f32[2456]{0:T(1024)S(1)}, f32[2456]{0:T(1024)S(1)}, /*index=5*/f32[2456]{0:T(1024)S(1)}, f32[2456]{0:T(1024)S(1)}, s32[2456]{0:T(1024)}) sort(s32[2456]{0:T(1024)S(1)} %pad_add_fusion.1, f32[2456]{0:T(1024)S(1)} %get-tuple-element.32, f32[2456]{0:T(1024)S(1)} %get-tuple-element.31, ...), dimensions={0}, to_apply=%region_5.6 | sort | flops 29472 | bytes 157184 | tf_op jit(solution)/shard_map/sort | solution.py:103
  142.4 7.9 %scatter_custom_fusion.2 = f32[288,3]{1,0:T(8,128)S(1)} fusion(s32[1728]{0:T(1024)S(1)} %compare_select_fusion.12, f32[1728,3]{1,0:T(8,128)S(1)} %copy.203, f32[]{:T(128)} %constant.55.clone.1), kind=kCustom, calls=%fused_computation.51 | custom fusion | bytes 3460 | tf_op jit(solution)/shard_map/scatter | solution.py:44
  150.7 8.1 %scatter_custom_fusion.3 = f32[288,3]{1,0:T(8,128)S(1)} fusion(s32[1728]{0:T(1024)S(1)} %compare_select_fusion.11, f32[1728,3]{1,0:T(8,128)S(1)} %copy.204, f32[]{:T(128)} %constant.55.clone.1), kind=kCustom, calls=%fused_computation.49 | custom fusion | bytes 3460 | tf_op jit(solution)/shard_map/scatter | solution.py:44
  163.7 9.8 %scatter_custom_fusion.5 = f32[384,3]{1,0:T(8,128)S(1)} fusion(s32[2304]{0:T(1024)S(1)} %get-tuple-element.35, f32[2304,3]{1,0:T(8,128)S(1)} %copy.210, f32[]{:T(128)} %constant.55.clone.1), kind=kCustom, calls=%fused_computation.43 | custom fusion | bytes 4612 | tf_op jit(solution)/shard_map/scatter | solution.py:44
  174.9 9.8 %scatter_custom_fusion.4 = f32[384,3]{1,0:T(8,128)S(1)} fusion(s32[2304]{0:T(1024)S(1)} %get-tuple-element.36, f32[2304,3]{1,0:T(8,128)S(1)} %copy.209, f32[]{:T(128)} %constant.55.clone.1), kind=kCustom, calls=%fused_computation.45 | custom fusion | bytes 4612 | tf_op jit(solution)/shard_map/scatter | solution.py:44
  185.8 5.8 %collective-permute-done.54 = f32[384,3]{1,0:T(8,128)S(1)} collective-permute-done((f32[384,3]{1,0:T(8,128)S(1)}, f32[384,3]{1,0:T(8,128)S(1)}, u32[]{:S(2)}, u32[]{:S(2)}) %collective-permute-start.54) | collective-permute-done | bytes 4640 | tf_op jit(solution)/shard_map/ppermute | solution.py:121
  195.4 8.2 %scatter_custom_fusion.7 = f32[512,3]{1,0:T(8,128)S(1)} fusion(s32[3072]{0:T(1024)S(1)} %bitcast.93, f32[3072,3]{1,0:T(8,128)S(1)} %copy.218, f32[]{:T(128)} %constant.55.clone.1), kind=kCustom, calls=%fused_computation.38 | custom fusion | bytes 6148 | tf_op jit(solution)/shard_map/scatter | solution.py:44
  205.2 8.4 %scatter_custom_fusion.6 = f32[512,3]{1,0:T(8,128)S(1)} fusion(s32[3072]{0:T(1024)S(1)} %bitcast.92, f32[3072,3]{1,0:T(8,128)S(1)} %copy.217, f32[]{:T(128)} %constant.55.clone.1), kind=kCustom, calls=%fused_computation.40 | custom fusion | bytes 6148 | tf_op jit(solution)/shard_map/scatter | solution.py:44
  214.7 6.1 %collective-permute-done.56 = f32[512,3]{1,0:T(8,128)S(1)} collective-permute-done((f32[512,3]{1,0:T(8,128)S(1)}, f32[512,3]{1,0:T(8,128)S(1)}, u32[]{:S(2)}, u32[]{:S(2)}) %collective-permute-start.56) | collective-permute-done | bytes 6176 | tf_op jit(solution)/shard_map/ppermute | solution.py:121
  221.1 35.1 %fusion = f32[1728,4096]{1,0:T(8,128)} fusion(f32[4096,3]{0,1:T(4,128)S(1)} %concatenate.79, f32[1728,3]{0,1:T(4,128)S(1)} %get-tuple-element.70), kind=kLoop, calls=%fused_computation.10 | loop fusion | flops 56623104 | bytes 28381440 | tf_op jit(solution)/shard_map/reduce_sum | solution.py:128
  256.2 38.6 %fusion.10 = (f32[]{:T(128)}, f32[1728,4096]{1,0:T(8,128)}) fusion(f32[1728,4096]{1,0:T(8,128)} %fusion, pred[4096]{0:T(1024)(128)(4,1)S(1)} %concatenate.78, pred[1728]{0:T(1024)(128)(4,1)S(1)} %get-tuple-element.64), kind=kLoop, calls=%fused_computation.23 | loop fusion | flops 184025088 | bytes 56628932 | tf_op jit(solution)/shard_map/reduce_sum | solution.py:133
  296.1 22.2 %psum.7 = f32[]{:T(128)} all-reduce(f32[]{:T(128)S(6)} %mul.210), channel_id=1, replica_groups=mesh['bz'=2,'by'=2,'bx'=2] {'bz','by','bx'}, use_global_device_ids=true, to_apply=%region_27.28 | all-reduce | flops 1 | bytes 8 | tf_op jit(solution)/shard_map/psum | solution.py:133
  318.3 15.5 %fusion.1 = f32[1728,3]{0,1:T(4,128)S(1)} fusion(f32[1728,4096]{1,0:T(8,128)} %get-tuple-element.83, f32[4096,3]{0,1:T(4,128)S(1)} %concatenate.79, f32[1728,3]{0,1:T(4,128)S(1)} %get-tuple-element.70), kind=kLoop, calls=%fused_computation.11 | loop fusion | flops 63695808 | bytes 28402176 | tf_op jit(solution)/shard_map/reduce_sum | solution.py:132
  (225 shorter events, 48.3 us)
Async XLA Ops:
  20.5 84.6 %collective-permute-start.24 = (s32[10]{0:T(128)S(1)}, s32[10]{0:T(128)S(1)}, u32[]{:S(2)}, u32[]{:S(2)}) collective-permute-start(s32[10]{0:T(128)S(1)} %get-tuple-element.124), channel_id=1, source_target_pairs={{0,6},{1,7},{2,4},{3,5},{4,2},{5,3},{6,0},{7,1}} | collective-permute-start | bytes 128 | tf_op jit(solution)/shard_map/ppermute | solution.py:98
  24.8 82.1 %collective-permute-start.22 = (s32[10]{0:T(128)S(1)}, s32[10]{0:T(128)S(1)}, u32[]{:S(2)}, u32[]{:S(2)}) collective-permute-start(s32[10]{0:T(128)S(1)} %get-tuple-element.125), channel_id=1, source_target_pairs={{0,5},{1,4},{2,7},{3,6},{4,1},{5,0},{6,3},{7,2}} | collective-permute-start | bytes 128 | tf_op jit(solution)/shard_map/ppermute | solution.py:98
  24.8 82.1 %collective-permute-start.20 = (s32[10]{0:T(128)S(1)}, s32[10]{0:T(128)S(1)}, u32[]{:S(2)}, u32[]{:S(2)}) collective-permute-start(s32[10]{0:T(128)S(1)} %get-tuple-element.126), channel_id=1, source_target_pairs={{0,5},{1,4},{2,7},{3,6},{4,1},{5,0},{6,3},{7,2}} | collective-permute-start | bytes 128 | tf_op jit(solution)/shard_map/ppermute | solution.py:98
  35.1 4.1 %collective-permute-start.51 = (f32[1,6]{1,0:T(1,128)S(1)}, f32[1,6]{1,0:T(1,128)S(1)}, u32[]{:S(2)}, u32[]{:S(2)}) collective-permute-start(f32[1,6]{1,0:T(1,128)S(1)} %get-tuple-element.84), channel_id=1, source_target_pairs={{0,7},{1,6},{2,5},{3,4},{4,3},{5,2},{6,1},{7,0}} | collective-permute-start | bytes 80 | tf_op jit(solution)/shard_map/ppermute | solution.py:97
  35.1 4.3 %collective-permute-start.49 = (f32[1,6]{1,0:T(1,128)S(1)}, f32[1,6]{1,0:T(1,128)S(1)}, u32[]{:S(2)}, u32[]{:S(2)}) collective-permute-start(f32[1,6]{1,0:T(1,128)S(1)} %get-tuple-element.85), channel_id=1, source_target_pairs={{0,7},{1,6},{2,5},{3,4},{4,3},{5,2},{6,1},{7,0}} | collective-permute-start | bytes 80 | tf_op jit(solution)/shard_map/ppermute | solution.py:97
  39.2 3.9 %collective-permute-start.45 = (f32[1,6]{1,0:T(1,128)S(1)}, f32[1,6]{1,0:T(1,128)S(1)}, u32[]{:S(2)}, u32[]{:S(2)}) collective-permute-start(f32[1,6]{1,0:T(1,128)S(1)} %get-tuple-element.86), channel_id=1, source_target_pairs={{0,7},{1,6},{2,5},{3,4},{4,3},{5,2},{6,1},{7,0}} | collective-permute-start | bytes 80 | tf_op jit(solution)/shard_map/ppermute | solution.py:97
  39.4 3.9 %collective-permute-start.43 = (f32[1,6]{1,0:T(1,128)S(1)}, f32[1,6]{1,0:T(1,128)S(1)}, u32[]{:S(2)}, u32[]{:S(2)}) collective-permute-start(f32[1,6]{1,0:T(1,128)S(1)} %get-tuple-element.87), channel_id=1, source_target_pairs={{0,7},{1,6},{2,5},{3,4},{4,3},{5,2},{6,1},{7,0}} | collective-permute-start | bytes 80 | tf_op jit(solution)/shard_map/ppermute | solution.py:97
  43.2 3.9 %collective-permute-start.34 = (f32[1,6]{1,0:T(1,128)S(1)}, f32[1,6]{1,0:T(1,128)S(1)}, u32[]{:S(2)}, u32[]{:S(2)}) collective-permute-start(f32[1,6]{1,0:T(1,128)S(1)} %get-tuple-element.88), channel_id=1, source_target_pairs={{0,7},{1,6},{2,5},{3,4},{4,3},{5,2},{6,1},{7,0}} | collective-permute-start | bytes 80 | tf_op jit(solution)/shard_map/ppermute | solution.py:97
  43.3 3.9 %collective-permute-start.32 = (f32[1,6]{1,0:T(1,128)S(1)}, f32[1,6]{1,0:T(1,128)S(1)}, u32[]{:S(2)}, u32[]{:S(2)}) collective-permute-start(f32[1,6]{1,0:T(1,128)S(1)} %get-tuple-element.89), channel_id=1, source_target_pairs={{0,7},{1,6},{2,5},{3,4},{4,3},{5,2},{6,1},{7,0}} | collective-permute-start | bytes 80 | tf_op jit(solution)/shard_map/ppermute | solution.py:97
  47.1 3.9 %collective-permute-start.28 = (f32[1,6]{1,0:T(1,128)S(1)}, f32[1,6]{1,0:T(1,128)S(1)}, u32[]{:S(2)}, u32[]{:S(2)}) collective-permute-start(f32[1,6]{1,0:T(1,128)S(1)} %get-tuple-element.90), channel_id=1, source_target_pairs={{0,7},{1,6},{2,5},{3,4},{4,3},{5,2},{6,1},{7,0}} | collective-permute-start | bytes 80 | tf_op jit(solution)/shard_map/ppermute | solution.py:97
  47.2 3.9 %collective-permute-start.26 = (f32[1,6]{1,0:T(1,128)S(1)}, f32[1,6]{1,0:T(1,128)S(1)}, u32[]{:S(2)}, u32[]{:S(2)}) collective-permute-start(f32[1,6]{1,0:T(1,128)S(1)} %get-tuple-element.91), channel_id=1, source_target_pairs={{0,7},{1,6},{2,5},{3,4},{4,3},{5,2},{6,1},{7,0}} | collective-permute-start | bytes 80 | tf_op jit(solution)/shard_map/ppermute | solution.py:97
  51.0 4.5 %collective-permute-start.50 = (f32[10,6]{1,0:T(8,128)S(1)}, f32[10,6]{1,0:T(8,128)S(1)}, u32[]{:S(2)}, u32[]{:S(2)}) collective-permute-start(f32[10,6]{1,0:T(8,128)S(1)} %get-tuple-element.92), channel_id=1, source_target_pairs={{0,6},{1,7},{2,4},{3,5},{4,2},{5,3},{6,0},{7,1}} | collective-permute-start | bytes 728 | tf_op jit(solution)/shard_map/ppermute | solution.py:97
  51.1 4.5 %collective-permute-start.48 = (f32[10,6]{1,0:T(8,128)S(1)}, f32[10,6]{1,0:T(8,128)S(1)}, u32[]{:S(2)}, u32[]{:S(2)}) collective-permute-start(f32[10,6]{1,0:T(8,128)S(1)} %get-tuple-element.93), channel_id=1, source_target_pairs={{0,5},{1,4},{2,7},{3,6},{4,1},{5,0},{6,3},{7,2}} | collective-permute-start | bytes 728 | tf_op jit(solution)/shard_map/ppermute | solution.py:97
  55.6 4.6 %collective-permute-start.44 = (f32[10,6]{1,0:T(8,128)S(1)}, f32[10,6]{1,0:T(8,128)S(1)}, u32[]{:S(2)}, u32[]{:S(2)}) collective-permute-start(f32[10,6]{1,0:T(8,128)S(1)} %get-tuple-element.95), channel_id=1, source_target_pairs={{0,6},{1,7},{2,4},{3,5},{4,2},{5,3},{6,0},{7,1}} | collective-permute-start | bytes 728 | tf_op jit(solution)/shard_map/ppermute | solution.py:97
  64.8 4.5 %collective-permute-start.33 = (f32[10,6]{1,0:T(8,128)S(1)}, f32[10,6]{1,0:T(8,128)S(1)}, u32[]{:S(2)}, u32[]{:S(2)}) collective-permute-start(f32[10,6]{1,0:T(8,128)S(1)} %get-tuple-element.100), channel_id=1, source_target_pairs={{0,6},{1,7},{2,4},{3,5},{4,2},{5,3},{6,0},{7,1}} | collective-permute-start | bytes 728 | tf_op jit(solution)/shard_map/ppermute | solution.py:97
  69.4 4.5 %collective-permute-start.27 = (f32[10,6]{1,0:T(8,128)S(1)}, f32[10,6]{1,0:T(8,128)S(1)}, u32[]{:S(2)}, u32[]{:S(2)}) collective-permute-start(f32[10,6]{1,0:T(8,128)S(1)} %get-tuple-element.103), channel_id=1, source_target_pairs={{0,6},{1,7},{2,4},{3,5},{4,2},{5,3},{6,0},{7,1}} | collective-permute-start | bytes 728 | tf_op jit(solution)/shard_map/ppermute | solution.py:97
  72.4 36.3 %collective-permute-start.18 = (s32[10]{0:T(128)S(1)}, s32[10]{0:T(128)S(1)}, u32[]{:S(2)}, u32[]{:S(2)}) collective-permute-start(s32[10]{0:T(128)S(1)} %get-tuple-element.127), channel_id=1, source_target_pairs={{0,6},{1,7},{2,4},{3,5},{4,2},{5,3},{6,0},{7,1}} | collective-permute-start | bytes 128 | tf_op jit(solution)/shard_map/ppermute | solution.py:98
  74.0 3.9 %collective-permute-start.25 = (s32[1]{0:T(128)}, s32[1]{0:T(128)}, u32[]{:S(2)}, u32[]{:S(2)}) collective-permute-start(s32[1]{0:T(128)} %get-tuple-element.116), channel_id=1, source_target_pairs={{0,7},{1,6},{2,5},{3,4},{4,3},{5,2},{6,1},{7,0}} | collective-permute-start | bytes 20 | tf_op jit(solution)/shard_map/ppermute | solution.py:98
  77.9 3.9 %collective-permute-start.23 = (s32[1]{0:T(128)}, s32[1]{0:T(128)}, u32[]{:S(2)}, u32[]{:S(2)}) collective-permute-start(s32[1]{0:T(128)} %get-tuple-element.117), channel_id=1, source_target_pairs={{0,7},{1,6},{2,5},{3,4},{4,3},{5,2},{6,1},{7,0}} | collective-permute-start | bytes 20 | tf_op jit(solution)/shard_map/ppermute | solution.py:98
  81.8 3.9 %collective-permute-start.19 = (s32[1]{0:T(128)}, s32[1]{0:T(128)}, u32[]{:S(2)}, u32[]{:S(2)}) collective-permute-start(s32[1]{0:T(128)} %get-tuple-element.118), channel_id=1, source_target_pairs={{0,7},{1,6},{2,5},{3,4},{4,3},{5,2},{6,1},{7,0}} | collective-permute-start | bytes 20 | tf_op jit(solution)/shard_map/ppermute | solution.py:98
  85.7 3.9 %collective-permute-start.17 = (s32[1]{0:T(128)}, s32[1]{0:T(128)}, u32[]{:S(2)}, u32[]{:S(2)}) collective-permute-start(s32[1]{0:T(128)} %get-tuple-element.119), channel_id=1, source_target_pairs={{0,7},{1,6},{2,5},{3,4},{4,3},{5,2},{6,1},{7,0}} | collective-permute-start | bytes 20 | tf_op jit(solution)/shard_map/ppermute | solution.py:98
  89.6 3.9 %collective-permute-start.8 = (s32[1]{0:T(128)}, s32[1]{0:T(128)}, u32[]{:S(2)}, u32[]{:S(2)}) collective-permute-start(s32[1]{0:T(128)} %get-tuple-element.120), channel_id=1, source_target_pairs={{0,7},{1,6},{2,5},{3,4},{4,3},{5,2},{6,1},{7,0}} | collective-permute-start | bytes 20 | tf_op jit(solution)/shard_map/ppermute | solution.py:98
  93.5 3.9 %collective-permute-start.6 = (s32[1]{0:T(128)}, s32[1]{0:T(128)}, u32[]{:S(2)}, u32[]{:S(2)}) collective-permute-start(s32[1]{0:T(128)} %get-tuple-element.121), channel_id=1, source_target_pairs={{0,7},{1,6},{2,5},{3,4},{4,3},{5,2},{6,1},{7,0}} | collective-permute-start | bytes 20 | tf_op jit(solution)/shard_map/ppermute | solution.py:98
  97.4 3.9 %collective-permute-start.2 = (s32[1]{0:T(128)}, s32[1]{0:T(128)}, u32[]{:S(2)}, u32[]{:S(2)}) collective-permute-start(s32[1]{0:T(128)} %get-tuple-element.122), channel_id=1, source_target_pairs={{0,7},{1,6},{2,5},{3,4},{4,3},{5,2},{6,1},{7,0}} | collective-permute-start | bytes 20 | tf_op jit(solution)/shard_map/ppermute | solution.py:98
  101.3 3.9 %collective-permute-start = (s32[1]{0:T(128)}, s32[1]{0:T(128)}, u32[]{:S(2)}, u32[]{:S(2)}) collective-permute-start(s32[1]{0:T(128)} %get-tuple-element.123), channel_id=1, source_target_pairs={{0,7},{1,6},{2,5},{3,4},{4,3},{5,2},{6,1},{7,0}} | collective-permute-start | bytes 20 | tf_op jit(solution)/shard_map/ppermute | solution.py:98
  105.2 5.0 %collective-permute-start.16 = (s32[10]{0:T(128)S(1)}, s32[10]{0:T(128)S(1)}, u32[]{:S(2)}, u32[]{:S(2)}) collective-permute-start(s32[10]{0:T(128)S(1)} %get-tuple-element.128), channel_id=1, source_target_pairs={{0,3},{1,2},{2,1},{3,0},{4,7},{5,6},{6,5},{7,4}} | collective-permute-start | bytes 128 | tf_op jit(solution)/shard_map/ppermute | solution.py:98
  105.2 5.0 %collective-permute-start.14 = (s32[10]{0:T(128)S(1)}, s32[10]{0:T(128)S(1)}, u32[]{:S(2)}, u32[]{:S(2)}) collective-permute-start(s32[10]{0:T(128)S(1)} %get-tuple-element.129), channel_id=1, source_target_pairs={{0,3},{1,2},{2,1},{3,0},{4,7},{5,6},{6,5},{7,4}} | collective-permute-start | bytes 128 | tf_op jit(solution)/shard_map/ppermute | solution.py:98
  106.9 5.0 %collective-permute-start.11 = (s32[10]{0:T(128)S(1)}, s32[10]{0:T(128)S(1)}, u32[]{:S(2)}, u32[]{:S(2)}) collective-permute-start(s32[10]{0:T(128)S(1)} %get-tuple-element.130), channel_id=1, source_target_pairs={{0,3},{1,2},{2,1},{3,0},{4,7},{5,6},{6,5},{7,4}} | collective-permute-start | bytes 128 | tf_op jit(solution)/shard_map/ppermute | solution.py:98
  107.0 6.4 %collective-permute-start.9 = (s32[10]{0:T(128)S(1)}, s32[10]{0:T(128)S(1)}, u32[]{:S(2)}, u32[]{:S(2)}) collective-permute-start(s32[10]{0:T(128)S(1)} %get-tuple-element.131), channel_id=1, source_target_pairs={{0,3},{1,2},{2,1},{3,0},{4,7},{5,6},{6,5},{7,4}} | collective-permute-start | bytes 128 | tf_op jit(solution)/shard_map/ppermute | solution.py:98
  108.7 5.2 %collective-permute-start.7 = (s32[10]{0:T(128)S(1)}, s32[10]{0:T(128)S(1)}, u32[]{:S(2)}, u32[]{:S(2)}) collective-permute-start(s32[10]{0:T(128)S(1)} %get-tuple-element.132), channel_id=1, source_target_pairs={{0,6},{1,7},{2,4},{3,5},{4,2},{5,3},{6,0},{7,1}} | collective-permute-start | bytes 128 | tf_op jit(solution)/shard_map/ppermute | solution.py:98
  110.1 5.3 %collective-permute-start.5 = (s32[10]{0:T(128)S(1)}, s32[10]{0:T(128)S(1)}, u32[]{:S(2)}, u32[]{:S(2)}) collective-permute-start(s32[10]{0:T(128)S(1)} %get-tuple-element.133), channel_id=1, source_target_pairs={{0,5},{1,4},{2,7},{3,6},{4,1},{5,0},{6,3},{7,2}} | collective-permute-start | bytes 128 | tf_op jit(solution)/shard_map/ppermute | solution.py:98
  110.1 5.3 %collective-permute-start.3 = (s32[10]{0:T(128)S(1)}, s32[10]{0:T(128)S(1)}, u32[]{:S(2)}, u32[]{:S(2)}) collective-permute-start(s32[10]{0:T(128)S(1)} %get-tuple-element.134), channel_id=1, source_target_pairs={{0,5},{1,4},{2,7},{3,6},{4,1},{5,0},{6,3},{7,2}} | collective-permute-start | bytes 128 | tf_op jit(solution)/shard_map/ppermute | solution.py:98
  111.9 4.5 %collective-permute-start.1 = (s32[10]{0:T(128)S(1)}, s32[10]{0:T(128)S(1)}, u32[]{:S(2)}, u32[]{:S(2)}) collective-permute-start(s32[10]{0:T(128)S(1)} %get-tuple-element.135), channel_id=1, source_target_pairs={{0,6},{1,7},{2,4},{3,5},{4,2},{5,3},{6,0},{7,1}} | collective-permute-start | bytes 128 | tf_op jit(solution)/shard_map/ppermute | solution.py:98
  113.9 4.5 %collective-permute-start.15 = (s32[100]{0:T(128)S(1)}, s32[100]{0:T(128)S(1)}, u32[]{:S(2)}, u32[]{:S(2)}) collective-permute-start(s32[100]{0:T(128)S(1)} %get-tuple-element.137), channel_id=1, source_target_pairs={{0,2},{1,3},{2,0},{3,1},{4,6},{5,7},{6,4},{7,5}} | collective-permute-start | bytes 1208 | tf_op jit(solution)/shard_map/ppermute | solution.py:98
  115.4 5.0 %collective-permute-start.12 = (s32[100]{0:T(128)S(1)}, s32[100]{0:T(128)S(1)}, u32[]{:S(2)}, u32[]{:S(2)}) collective-permute-start(s32[100]{0:T(128)S(1)} %get-tuple-element.139), channel_id=1, source_target_pairs={{0,1},{1,0},{2,3},{3,2},{4,5},{5,4},{6,7},{7,6}} | collective-permute-start | bytes 1208 | tf_op jit(solution)/shard_map/ppermute | solution.py:98
  116.4 4.1 %collective-permute-start.10 = (s32[100]{0:T(128)S(1)}, s32[100]{0:T(128)S(1)}, u32[]{:S(2)}, u32[]{:S(2)}) collective-permute-start(s32[100]{0:T(128)S(1)} %get-tuple-element.140), channel_id=1, source_target_pairs={{0,2},{1,3},{2,0},{3,1},{4,6},{5,7},{6,4},{7,5}} | collective-permute-start | bytes 1208 | tf_op jit(solution)/shard_map/ppermute | solution.py:98
  116.9 4.0 %collective-permute-start.4 = (s32[100]{0:T(128)S(1)}, s32[100]{0:T(128)S(1)}, u32[]{:S(2)}, u32[]{:S(2)}) collective-permute-start(s32[100]{0:T(128)S(1)} %get-tuple-element.141), channel_id=1, source_target_pairs={{0,4},{1,5},{2,6},{3,7},{4,0},{5,1},{6,2},{7,3}} | collective-permute-start | bytes 1208 | tf_op jit(solution)/shard_map/ppermute | solution.py:98
  118.4 8.6 %collective-permute-start.47 = (f32[100,6]{1,0:T(8,128)S(1)}, f32[100,6]{1,0:T(8,128)S(1)}, u32[]{:S(2)}, u32[]{:S(2)}) collective-permute-start(f32[100,6]{1,0:T(8,128)S(1)} %get-tuple-element.104), channel_id=1, source_target_pairs={{0,4},{1,5},{2,6},{3,7},{4,0},{5,1},{6,2},{7,3}} | collective-permute-start | bytes 7208 | tf_op jit(solution)/shard_map/ppermute | solution.py:97
  119.0 9.3 %collective-permute-start.41 = (f32[100,6]{1,0:T(8,128)S(1)}, f32[100,6]{1,0:T(8,128)S(1)}, u32[]{:S(2)}, u32[]{:S(2)}) collective-permute-start(f32[100,6]{1,0:T(8,128)S(1)} %get-tuple-element.105), channel_id=1, source_target_pairs={{0,2},{1,3},{2,0},{3,1},{4,6},{5,7},{6,4},{7,5}} | collective-permute-start | bytes 7208 | tf_op jit(solution)/shard_map/ppermute | solution.py:97
  120.4 7.9 %collective-permute-start.39 = (f32[100,6]{1,0:T(8,128)S(1)}, f32[100,6]{1,0:T(8,128)S(1)}, u32[]{:S(2)}, u32[]{:S(2)}) collective-permute-start(f32[100,6]{1,0:T(8,128)S(1)} %get-tuple-element.106), channel_id=1, source_target_pairs={{0,1},{1,0},{2,3},{3,2},{4,5},{5,4},{6,7},{7,6}} | collective-permute-start | bytes 7208 | tf_op jit(solution)/shard_map/ppermute | solution.py:97
  120.4 8.0 %collective-permute-start.38 = (f32[100,6]{1,0:T(8,128)S(1)}, f32[100,6]{1,0:T(8,128)S(1)}, u32[]{:S(2)}, u32[]{:S(2)}) collective-permute-start(f32[100,6]{1,0:T(8,128)S(1)} %get-tuple-element.107), channel_id=1, source_target_pairs={{0,1},{1,0},{2,3},{3,2},{4,5},{5,4},{6,7},{7,6}} | collective-permute-start | bytes 7208 | tf_op jit(solution)/shard_map/ppermute | solution.py:97
  120.9 7.6 %collective-permute-start.36 = (f32[100,6]{1,0:T(8,128)S(1)}, f32[100,6]{1,0:T(8,128)S(1)}, u32[]{:S(2)}, u32[]{:S(2)}) collective-permute-start(f32[100,6]{1,0:T(8,128)S(1)} %get-tuple-element.108), channel_id=1, source_target_pairs={{0,2},{1,3},{2,0},{3,1},{4,6},{5,7},{6,4},{7,5}} | collective-permute-start | bytes 7208 | tf_op jit(solution)/shard_map/ppermute | solution.py:97
  127.1 4.2 %collective-permute-start.30 = (f32[100,6]{1,0:T(8,128)S(1)}, f32[100,6]{1,0:T(8,128)S(1)}, u32[]{:S(2)}, u32[]{:S(2)}) collective-permute-start(f32[100,6]{1,0:T(8,128)S(1)} %get-tuple-element.109), channel_id=1, source_target_pairs={{0,4},{1,5},{2,6},{3,7},{4,0},{5,1},{6,2},{7,3}} | collective-permute-start | bytes 7208 | tf_op jit(solution)/shard_map/ppermute | solution.py:97
  150.3 9.0 %collective-permute-start.52 = (f32[288,3]{1,0:T(8,128)S(1)}, f32[288,3]{1,0:T(8,128)S(1)}, u32[]{:S(2)}, u32[]{:S(2)}) collective-permute-start(f32[288,3]{1,0:T(8,128)S(1)} %scatter_custom_fusion.2), channel_id=1, source_target_pairs={{0,1},{1,0},{2,3},{3,2},{4,5},{5,4},{6,7},{7,6}} | collective-permute-start | bytes 10376 | tf_op jit(solution)/shard_map/ppermute | solution.py:121
  173.5 12.3 %collective-permute-start.55 = (f32[384,3]{1,0:T(8,128)S(1)}, f32[384,3]{1,0:T(8,128)S(1)}, u32[]{:S(2)}, u32[]{:S(2)}) collective-permute-start(f32[384,3]{1,0:T(8,128)S(1)} %scatter_custom_fusion.5), channel_id=1, source_target_pairs={{0,2},{2,0},{1,3},{3,1},{4,6},{6,4},{5,7},{7,5}} | collective-permute-start | bytes 13832 | tf_op jit(solution)/shard_map/ppermute | solution.py:122
  184.7 6.9 %collective-permute-start.54 = (f32[384,3]{1,0:T(8,128)S(1)}, f32[384,3]{1,0:T(8,128)S(1)}, u32[]{:S(2)}, u32[]{:S(2)}) collective-permute-start(f32[384,3]{1,0:T(8,128)S(1)} %scatter_custom_fusion.4), channel_id=1, source_target_pairs={{0,2},{2,0},{1,3},{3,1},{4,6},{6,4},{5,7},{7,5}} | collective-permute-start | bytes 13832 | tf_op jit(solution)/shard_map/ppermute | solution.py:121
  203.6 11.0 %collective-permute-start.57 = (f32[512,3]{1,0:T(8,128)S(1)}, f32[512,3]{1,0:T(8,128)S(1)}, u32[]{:S(2)}, u32[]{:S(2)}) collective-permute-start(f32[512,3]{1,0:T(8,128)S(1)} %scatter_custom_fusion.7), channel_id=1, source_target_pairs={{0,4},{4,0},{1,5},{5,1},{2,6},{6,2},{3,7},{7,3}} | collective-permute-start | bytes 18440 | tf_op jit(solution)/shard_map/ppermute | solution.py:122
  213.6 7.2 %collective-permute-start.56 = (f32[512,3]{1,0:T(8,128)S(1)}, f32[512,3]{1,0:T(8,128)S(1)}, u32[]{:S(2)}, u32[]{:S(2)}) collective-permute-start(f32[512,3]{1,0:T(8,128)S(1)} %scatter_custom_fusion.6), channel_id=1, source_target_pairs={{0,4},{4,0},{1,5},{5,1},{2,6},{6,2},{3,7},{7,3}} | collective-permute-start | bytes 18440 | tf_op jit(solution)/shard_map/ppermute | solution.py:121
  (11 other events, 30.9 us)
where the time goes:
time: 335 us; the launch traced here: 334 us
  other arithmetic  116 us (35%)
  local copies, waits for them, and re-layouts  84.2 us (25%)
  waiting for transfers between devices  60.1 us (18%)
  starting transfers between devices  50.5 us (15%)
  blocking collectives  22.2 us (7%)
    scatter x6, local copies, waits for them, and re-layouts, pack_rows(): return base.at[dest_slot].set(values, mode='drop')  52.2 us
    reduce_sum x1, other arithmetic, local_step(): energy = lax.psum(0.5 * jnp.sum(pair_energy), BRICK_AXES)  38.6 us
    reduce_sum x1, other arithmetic, local_step(): dist_sq = jnp.sum(pair_delta * pair_delta, axis=-1)  35.1 us
    ppermute x26, waiting for transfers between devices, local_step(): lax.ppermute(out_ids[mig_start:mig_start + mig_cap], BRICK_AXES, perm_pairs)  27.1 us
    ppermute x26, starting transfers between devices, local_step(): lax.ppermute(out_ids[mig_start:mig_start + mig_cap], BRICK_AXES, perm_pairs)  24 us
    psum x1, blocking collectives, local_step(): energy = lax.psum(0.5 * jnp.sum(pair_energy), BRICK_AXES)  22.2 us
    ppermute x26, starting transfers between devices, local_step(): lax.ppermute(out_rows[mig_start:mig_start + mig_cap], BRICK_AXES, perm_pa...  21.9 us
    ppermute x26, waiting for transfers between devices, local_step(): lax.ppermute(out_rows[mig_start:mig_start + mig_cap], BRICK_AXES, perm_pa...  20.3 us
  transfers between devices with their start and end apart: 58, of which 26 were waited for; matrix products, arithmetic and copies ran while one was open for 13% of the time, Pallas kernels for 0%

commit v1 on v0

v1 whole, which is shorter than its diff:
```python
import functools

import jax
import jax.numpy as jnp
from jax import lax
from jax.experimental import pallas as pl
from jax.experimental.pallas import tpu as pltpu
from jax.sharding import PartitionSpec as P

TIME_STEP = 0.005
RCUT = 2.5
DENSITY = 0.8442
SPACING = (1.0 / DENSITY) ** (1.0 / 3.0)
SITES = 12
BRICK = SITES * SPACING
BOX = 2.0 * BRICK
BRICK_AXES = ("bz", "by", "bx")
CAP = SITES ** 3
KPAD = 1792
MESH_ID = pl.DeviceIdType.MESH
F32 = jnp.float32
BF16 = jnp.bfloat16
CUT6 = RCUT ** -6
U_CUT = 4.0 * (CUT6 * CUT6 - CUT6)
DU_CUT = (-48.0 * CUT6 * CUT6 + 24.0 * CUT6) / RCUT
DELTAS = [(d >> 2 & 1, d >> 1 & 1, d & 1) for d in range(1, 8)]
SHIFTS = [(dx, dy) for dy in range(-2, 3) for dx in range(-2, 3)]
NF = 7


def iota(shape, dim):
    return lax.broadcasted_iota(jnp.int32, shape, dim)


def split3(x):
    hi = x.astype(BF16).astype(F32)
    rest = x - hi
    mid = rest.astype(BF16).astype(F32)
    return hi, mid, rest - mid


def dot_nt(a, b):
    return lax.dot_general(a, b, (((1,), (1,)), ((), ())), preferred_element_type=F32)


def dot_nn(a, b):
    return lax.dot_general(a, b, (((1,), (0,)), ((), ())), preferred_element_type=F32)


def buf_shape(delta):
    return (NF * (8 if delta[0] else 16), 128 if delta[1] else 256)


def to_delta(g, delta):
    dz, dy, dx = delta
    if dx:
        xf = iota(g.shape, 1) & 15
        g = jnp.where(xf < 3, pltpu.roll(g, 244, 1), jnp.where(xf >= 13, pltpu.roll(g, 12, 1), 0.0))
    if dz:
        row = iota((8, 256), 0)
        g = jnp.where(row < 3, pltpu.roll(g[8:16], 4, 0), jnp.where(row >= 5, pltpu.roll(g[0:8], 4, 0), 0.0))
    if dy:
        lane = iota((g.shape[0], 128), 1)
        g = jnp.where(lane < 48, pltpu.roll(g[:, 128:], 64, 1), jnp.where(lane >= 80, pltpu.roll(g[:, :128], 64, 1), 0.0))
    return g


def from_delta(b, delta):
    dz, dy, _ = delta
    if dy:
        lane = iota(b.shape, 1)
        b = jnp.concatenate([jnp.where(lane < 48, b, 0.0), jnp.where(lane >= 80, b, 0.0)], axis=1)
    if dz:
        row = iota(b.shape, 0)
        b = jnp.concatenate([jnp.where(row < 3, b, 0.0), jnp.where(row >= 5, b, 0.0)], axis=0)
    return b


def kernel(pos_ref, vel_ref, frc_ref, id_ref, val_ref, opos_ref, ovel_ref, ofrc_ref, oid_ref, oval_ref, oen_ref, *scratch):
    sbufs = scratch[0:7]
    rbufs = scratch[7:14]
    atom_ref, g_ref, t_ref, q_ref, ebuf, send_sem, recv_sem, esend_sem, erecv_sem = scratch[14:]
    bz, by, bx = lax.axis_index("bz"), lax.axis_index("by"), lax.axis_index("bx")

    def partner(delta):
        return (lax.rem(bz + delta[0], 2), lax.rem(by + delta[1], 2), lax.rem(bx + delta[2], 2))

    barrier = pltpu.get_barrier_semaphore()
    for delta in DELTAS:
        pl.semaphore_signal(barrier, inc=1, device_id=partner(delta), device_id_type=MESH_ID)

    v_half = vel_ref[...] + (0.5 * TIME_STEP) * frc_ref[...]
    moved = pos_ref[...] + TIME_STEP * v_half
    moved = moved - BOX * jnp.floor(moved * (1.0 / BOX))
    axis_row = iota((3, 1), 0)
    coord = jnp.where(axis_row == 0, bx, jnp.where(axis_row == 1, by, bz)).astype(F32)
    brick_lo = coord * BRICK
    rel = moved - brick_lo
    rel = jnp.where(rel < -0.5 * BRICK, rel + BOX, jnp.where(rel >= 1.5 * BRICK, rel - BOX, rel))
    cell = jnp.floor(rel * (1.0 / SPACING)).astype(jnp.int32) + 2
    live = val_ref[...] == 1
    ids = id_ref[...]
    atom_ref[:, pl.ds(KPAD - 128, 128)] = jnp.zeros((atom_ref.shape[0], 128), F32)
    zi = jnp.where(live, cell[2:3, :], 0)
    lo = jnp.where(live, cell[1:2, :] * 16 + cell[0:1, :], 0)
    rows = list(split3(moved)) + list(split3(v_half))
    for k in range(6):
        atom_ref[8 * k:8 * k + 3, 0:CAP] = rows[k]
    atom_ref[48:49, 0:CAP] = (ids >> 7).astype(F32)
    atom_ref[49:50, 0:CAP] = (ids & 127).astype(F32)
    atom_ref[50:51, 0:CAP] = zi.astype(F32)
    atom_ref[51:52, 0:CAP] = lo.astype(F32)

    zrow = atom_ref[50:51, :]
    lrow = atom_ref[51:52, :]
    zmask = jnp.broadcast_to(zrow, (16, KPAD)) == iota((16, KPAD), 0).astype(F32)
    onehot = jnp.where(jnp.broadcast_to(lrow, (256, KPAD)) == iota((256, KPAD), 0).astype(F32), 1.0, 0.0).astype(BF16)

    def spread(row_idx):
        return jnp.where(zmask, jnp.broadcast_to(atom_ref[row_idx:row_idx + 1, :], (16, KPAD)), 0.0).astype(BF16)

    order = [8 * k + c for k in range(6) for c in range(3)] + [48, 49]
    lhs = jnp.concatenate([spread(i) for i in order], axis=0)
    binned = dot_nt(lhs, onehot)
    g_ref[0:48, :] = binned[0:48] + binned[48:96] + binned[96:144]
    g_ref[48:96, :] = binned[144:192] + binned[192:240] + binned[240:288]
    g_ref[96:112, :] = binned[288:304] * 128.0 + binned[304:320]

    for k, delta in enumerate(DELTAS):
        rz = 8 if delta[0] else 16
        for f in range(NF):
            sbufs[k][f * rz:(f + 1) * rz, :] = to_delta(g_ref[16 * f:16 * f + 16, :], delta)
    pl.semaphore_wait(barrier, 7)
    copies = []
    for k, delta in enumerate(DELTAS):
        copy = pltpu.make_async_remote_copy(src_ref=sbufs[k], dst_ref=rbufs[k], send_sem=send_sem.at[k], recv_sem=recv_sem.at[k], device_id=partner(delta), device_id_type=MESH_ID)
        copy.start()
        copies.append(copy)
    for copy in copies:
        copy.wait_recv()
    fields = []
    for f in range(NF):
        acc = g_ref[16 * f:16 * f + 16, :]
        for k, delta in enumerate(DELTAS):
            rz = 8 if delta[0] else 16
            acc = acc + from_delta(rbufs[k][f * rz:(f + 1) * rz, :], delta)
        fields.append(acc)

    present = fields[0] != 0.0
    lane = iota((16, 256), 1)
    frame = [lane & 15, lane >> 4, iota((16, 256), 0)]
    los = [bx, by, bz]
    local = []
    for c in range(3):
        u = fields[c] - los[c].astype(F32) * BRICK
        u = jnp.where(u < -0.5 * BRICK, u + BOX, jnp.where(u >= 1.5 * BRICK, u - BOX, u))
        local.append(jnp.where(present, u, 1000.0 + 10.0 * frame[c].astype(F32)))

    for s, (dx, dy) in enumerate(SHIFTS):
        for h in range(2):
            left = 32 + 96 * h + 16 * dy + dx
            for c in range(3):
                rolled = pltpu.roll(local[c], (256 - left) % 256, 1)
                t_ref[3 * s + c, pl.ds(h, 16, stride=2), :] = rolled[:, 0:128]
    for h in range(2):
        left = 32 + 96 * h
        for f in range(NF):
            rolled = pltpu.roll(fields[f], (256 - left) % 256, 1)
            q_ref[f, pl.ds(h, 16, stride=2), :] = rolled[:, 0:128]

    base = SHIFTS.index((0, 0))
    mine = [t_ref[3 * base + c, 4:28, :] for c in range(3)]

    def pair(carry, nbr):
        fx, fy, fz, sw, s6, sr, sn = carry
        ex, ey, ez = mine[0] - nbr[0], mine[1] - nbr[1], mine[2] - nbr[2]
        r2 = ex * ex + ey * ey + ez * ez
        near = r2 < RCUT * RCUT
        inv = jnp.where(near, lax.rsqrt(r2), 0.0)
        i2 = inv * inv
        i6 = i2 * i2 * i2
        w = i6 * (i6 - 0.5)
        fr = w * i2 + (DU_CUT / 48.0) * inv
        return (fx + fr * ex, fy + fr * ey, fz + fr * ez, sw + w, s6 + i6, sr + r2 * inv, sn + jnp.where(near, 1.0, 0.0))

    def load(s, dz):
        return [t_ref[3 * s + c, 4 + 2 * dz:28 + 2 * dz, :] for c in range(3)]

    carry = tuple(jnp.zeros((24, 128), F32) for _ in range(7))
    for s, (dx, dy) in enumerate(SHIFTS):
        twos = (abs(dx) == 2) + (abs(dy) == 2)
        if twos == 2:
            continue
        for dz in (range(-2, 3) if twos == 0 else range(-1, 2)):
            if (dx, dy, dz) != (0, 0, 0):
                carry = pair(carry, load(s, dz))
    low_x = (iota((24, 128), 1) & 15) < 8
    row24 = iota((24, 128), 0)
    low_y = (row24 & 1) == 0
    low_z = row24 < 12
    idx = SHIFTS.index
    for dz in range(-1, 2):
        a, b, c2, d = load(idx((-2, -2)), dz), load(idx((2, -2)), dz), load(idx((-2, 2)), dz), load(idx((2, 2)), dz)
        carry = pair(carry, [jnp.where(low_y, jnp.where(low_x, a[c], b[c]), jnp.where(low_x, c2[c], d[c])) for c in range(3)])
    for dy in range(-1, 2):
        a, b, c2, d = load(idx((-2, dy)), -2), load(idx((2, dy)), -2), load(idx((-2, dy)), 2), load(idx((2, dy)), 2)
        carry = pair(carry, [jnp.where(low_z, jnp.where(low_x, a[c], b[c]), jnp.where(low_x, c2[c], d[c])) for c in range(3)])
    for dx in range(-1, 2):
        a, b, c2, d = load(idx((dx, -2)), -2), load(idx((dx, 2)), -2), load(idx((dx, -2)), 2), load(idx((dx, 2)), 2)
        carry = pair(carry, [jnp.where(low_z, jnp.where(low_y, a[c], b[c]), jnp.where(low_y, c2[c], d[c])) for c in range(3)])
    force = [48.0 * carry[c] for c in range(3)]

    lane24 = iota((24, 128), 1)
    x24 = lane24 & 15
    own = (lane24 < 96) & (x24 >= 2) & (x24 < 14) & (q_ref[0, 4:28, :] != 0.0)
    energy = 4.0 * (carry[3] - 0.5 * carry[4]) - DU_CUT * carry[5] + (RCUT * DU_CUT - U_CUT) * carry[6]
    energy = jnp.where(own, 0.5 * energy, 0.0)
    me = bz * 4 + by * 2 + bx
    ebuf[me, :, :] = energy[0:8] + energy[8:16] + energy[16:24]
    ecopies = []
    for k, delta in enumerate(DELTAS):
        copy = pltpu.make_async_remote_copy(src_ref=ebuf.at[me], dst_ref=ebuf.at[me], send_sem=esend_sem.at[k], recv_sem=erecv_sem.at[k], device_id=partner(delta), device_id_type=MESH_ID)
        copy.start()
        ecopies.append(copy)

    idv = jnp.where(own, q_ref[6, 4:28, :], -1.0)
    id_int = idv.astype(jnp.int32)
    id_hi = jnp.where(own, id_int >> 7, -1).astype(F32)
    id_lo = jnp.where(own, id_int & 127, -1).astype(F32)

    def flat(x, n):
        return jnp.concatenate([jnp.broadcast_to(x[r:r + 1, :], (n, 128)) for r in range(24)], axis=1)

    hot_hi = jnp.where(flat(id_hi, 128) == iota((128, 3072), 0).astype(F32), 1.0, 0.0).astype(BF16)
    lo_eq = flat(id_lo, 128) == iota((128, 3072), 0).astype(F32)
    hot_lo = jnp.where(lo_eq, 1.0, 0.0).astype(BF16)
    table = dot_nt(hot_lo, hot_hi).astype(BF16)
    r128, c128 = iota((128, 128), 0), iota((128, 128), 1)
    below = dot_nn(jnp.where(c128 < r128, 1.0, 0.0).astype(BF16), table)
    total = dot_nn(jnp.ones((128, 128), BF16), table).astype(BF16)
    before = dot_nn(total, jnp.where(r128 < c128, 1.0, 0.0).astype(BF16))
    rank_tab = below + before
    tab_hi = jnp.floor(rank_tab * (1.0 / 256.0)) * 256.0
    tab_lo = rank_tab - tab_hi
    looked = dot_nn(tab_hi.astype(BF16), hot_hi) + dot_nn(tab_lo.astype(BF16), hot_hi)
    rank = jnp.sum(jnp.where(lo_eq, looked, 0.0), axis=0, keepdims=True)
    any_own = flat(jnp.where(own, 1.0, 0.0), 1) > 0.5
    rank_hi = jnp.floor(rank * (1.0 / 256.0))
    rank_lo = jnp.where(any_own, rank - 256.0 * rank_hi, -1.0)
    rank_hi = jnp.where(any_own, rank_hi, -1.0)

    hot_slot = jnp.where(jnp.broadcast_to(rank_lo, (256, 3072)) == iota((256, 3072), 0).astype(F32), 1.0, 0.0).astype(BF16)
    hi_mask = jnp.broadcast_to(rank_hi, (8, 3072)) == iota((8, 3072), 0).astype(F32)
    outs = []
    for c in range(3):
        outs += list(split3(q_ref[c, 4:28, :]))
    for c in range(3):
        outs += list(split3(q_ref[3 + c, 4:28, :] + (0.5 * TIME_STEP) * force[c]))
    for c in range(3):
        outs += list(split3(force[c]))
    outs += [id_hi, id_lo, jnp.where(own, 1.0, 0.0)]
    lhs = jnp.concatenate([jnp.where(hi_mask, flat(x, 8), 0.0) for x in outs], axis=0).astype(BF16)
    slots = dot_nt(lhs, hot_slot)

    def field(i):
        return slots[8 * i:8 * i + 8, :]

    def put(ref, row, x):
        for h in range(7):
            n = 256 if h < 6 else CAP - 1536
            ref[row:row + 1, 256 * h:256 * h + n] = x[h:h + 1, 0:n].astype(ref.dtype)

    for c in range(3):
        put(opos_ref, c, field(3 * c) + field(3 * c + 1) + field(3 * c + 2))
        put(ovel_ref, c, field(9 + 3 * c) + field(10 + 3 * c) + field(11 + 3 * c))
        put(ofrc_ref, c, field(18 + 3 * c) + field(19 + 3 * c) + field(20 + 3 * c))
    put(oid_ref, 0, field(27) * 128.0 + field(28))
    put(oval_ref, 0, field(29))

    for copy in ecopies:
        copy.wait_recv()
    acc = ebuf[0]
    for k in range(1, 8):
        acc = acc + ebuf[k]
    oen_ref[...] = jnp.sum(jnp.sum(acc, axis=0, keepdims=True), axis=1, keepdims=True)
    for copy in copies + ecopies:
        copy.wait_send()


def solution(mesh):
    row_spec = P(BRICK_AXES, None)
    flat_spec = P(BRICK_AXES)
    vmem = pl.BlockSpec(memory_space=pltpu.VMEM)

    def local_step(pos, vel, frc, ids, valid):
        f3 = jax.ShapeDtypeStruct((3, CAP), F32)
        i1 = jax.ShapeDtypeStruct((1, CAP), jnp.int32)
        outs = pl.pallas_call(
            kernel,
            out_shape=(f3, f3, f3, i1, i1, jax.ShapeDtypeStruct((1, 1), F32)),
            in_specs=[vmem] * 5,
            out_specs=(vmem,) * 6,
            scratch_shapes=[pltpu.VMEM(buf_shape(d), F32) for d in DELTAS] * 2 + [
                pltpu.VMEM((56, KPAD), F32),
                pltpu.VMEM((112, 256), F32),
                pltpu.VMEM((75, 32, 128), F32),
                pltpu.VMEM((NF, 32, 128), F32),
                pltpu.VMEM((8, 8, 128), F32),
                pltpu.SemaphoreType.DMA((7,)),
                pltpu.SemaphoreType.DMA((7,)),
                pltpu.SemaphoreType.DMA((7,)),
                pltpu.SemaphoreType.DMA((7,)),
            ],
            compiler_params=pltpu.CompilerParams(collective_id=0, has_side_effects=True),
        )(pos.T, vel.T, frc.T, ids[None, :], valid[None, :])
        return outs[0].T, outs[1].T, outs[2].T, outs[3][0], outs[4][0], outs[5][0, 0]

    return jax.shard_map(local_step, mesh=mesh, in_specs=(row_spec, row_spec, row_spec, flat_spec, flat_spec), out_specs=(row_spec, row_spec, row_spec, flat_spec, flat_spec, P()), check_vma=False)
```

time: 335 us -> 26 us (0.08)
  other arithmetic: 116 us -> 2.63 us
  local copies, waits for them, and re-layouts: 84.2 us -> 4.03 us
  waiting for transfers between devices: 60.1 us -> 0 us
  starting transfers between devices: 50.5 us -> 0 us
  blocking collectives: 22.2 us -> 0 us
  Pallas kernels: 0 us -> 16.5 us
    reduce_sum x4 -> x0, other arithmetic: 89.3 us -> none  [the longest x1 38.6 us: local_step(): energy = lax.psum(0.5 * jnp.sum(pair_energy), BRICK_AXES)]
    scatter x8 -> x0, local copies, waits for them, and re-layouts: 69.3 us -> none  [the longest x6 52.2 us: pack_rows(): return base.at[dest_slot].set(values, mode='drop')]
    ppermute x58 -> x0, waiting for transfers between devices: 60.1 us -> none  [the longest x26 27.1 us: local_step(): lax.ppermute(out_ids[mig_start:mig_start + mig_cap], BRICK_AXES, perm_pairs)]
    ppermute x58 -> x0, starting transfers between devices: 50.5 us -> none  [the longest x26 24 us: local_step(): lax.ppermute(out_ids[mig_start:mig_start + mig_cap], BRICK_AXES, perm_pairs)]
    psum x1 -> x0, blocking collectives: 22.2 us -> none  [local_step(): energy = lax.psum(0.5 * jnp.sum(pair_energy), BRICK_AXES)]
    pallas_call x0 -> x1, Pallas kernels: none -> 16.5 us  [local_step(): pl.pallas_call(kernel, out_shape=(f3, f3, f3, i1, i1, jax.ShapeDtypeStruc...]
    another operation x20 -> x0, other arithmetic: 9.94 us -> none  [run(): return stepper(positions, velocities, forces, atom_ids, valid_mask)]
    sort x1 -> x0, other arithmetic: 7.01 us -> none  [local_step(): lax.sort([merge_keys] + [merge_rows[:, col_idx] for col_idx in range(6)],...]
  transfers between devices with their start and end apart: 58 -> 0, of which waited for: 26 -> 0; matrix products, arithmetic and copies ran while one was open for 13% -> 0% of each run, Pallas kernels for 0% -> 0%
where the time goes in v1:
time: 26 us; the launch traced here: 25.5 us
  Pallas kernels  16.5 us (63%)
  local copies, waits for them, and re-layouts  4.03 us (16%)
  other arithmetic  2.63 us (10%)
  between operations  2.35 us (9%)
    pallas_call x1, Pallas kernels, local_step(): pl.pallas_call(kernel, out_shape=(f3, f3, f3, i1, i1, jax.ShapeDtypeStruc...  16.5 us
    pallas_call x2, other arithmetic, local_step(): pl.pallas_call(kernel, out_shape=(f3, f3, f3, i1, i1, jax.ShapeDtypeStruc...  2.63 us
    unnamed x11, local copies, waits for them, and re-layouts  2.13 us
    broadcast_in_dim x1, local copies, waits for them, and re-layouts, local_step(): ids[None, :]  1.3 us
    broadcast_in_dim x1, local copies, waits for them, and re-layouts, local_step(): valid[None, :]  0.6 us

profile of v1, /device:TPU:0, one launch (start us, length us, event | category | flops | bytes accessed | tf_op | source)
XLA Modules:
  0.0 25.5 jit_solution(2674357150435774409)
XLA Ops:
  0.6 0.0 copy-start.3
  0.6 1.3 %broadcast_in_dim.6.id_ref = s32[1,1728]{1,0:T(1,128)} reshape(s32[1728]{0:T(1024)} %param.8) | data formatting | bytes 13824 | tf_op jit(solution)/shard_map/broadcast_in_dim | solution.py:315
  1.9 0.0 copy-done.3
  1.9 0.6 %broadcast_in_dim.7.val_ref = s32[1,1728]{1,0:T(1,128)} reshape(s32[1728]{0:T(1024)S(1)} %copy-done.3) | data formatting | bytes 13824 | tf_op jit(solution)/shard_map/broadcast_in_dim | solution.py:315
  2.5 16.5 %shard_map.100 = (f32[3,1728]{1,0:T(4,128)}, f32[3,1728]{1,0:T(4,128)}, f32[3,1728]{1,0:T(4,128)}, s32[1,1728]{1,0:T(1,128)}, s32[1,1728]{1,0:T(1,128)}, /*index=5*/f32[1,1]{1,0:T(1,128)}) custom-call(f32[3,1728]{1,0:T(4,128)} %bitcast.10, f32[3,1728]{1,0:T(4,128)} %bitcast.11, f32[3,1728]{1,0:T(4,128)} %bitcast.12, s32[1,1728]{1,0:T(1,128)} %broadcast_in_dim.6.id_ref, ...), custom_call_target="tpu_custom_call" | custom-call | tf_op jit(solution)/shard_map/pallas_call | solution.py:298
  19.0 0.0 copy-start.2
  19.0 1.3 %reduce = s32[1728]{0:T(1024)} reduce(s32[1,1728]{1,0:T(1,128)} %get-tuple-element.15, s32[]{:T(128)} %constant), dimensions={0}, to_apply=%get-tuple-element.15.reduce_sub_computation | reduce | bytes 13828 | tf_op jit(solution)/shard_map/pallas_call | solution.py:298
  20.4 1.3 %reduce.1 = s32[1728]{0:T(1024)} reduce(s32[1,1728]{1,0:T(1,128)} %get-tuple-element.16, s32[]{:T(128)} %constant), dimensions={0}, to_apply=%get-tuple-element.16.reduce_sub_computation | reduce | bytes 13828 | tf_op jit(solution)/shard_map/pallas_call | solution.py:298
  21.7 0.0 copy-done.2
  21.7 0.0 copy-start.1
  21.7 0.6 %copy.15 = f32[1728,3]{0,1:T(4,128)} copy(f32[1728,3]{0,1:T(4,128)S(1)} %bitcast.9) | data formatting | bytes 41472
  22.3 0.1 copy-done.1
  22.4 0.0 copy-start
  22.4 0.6 %copy.16 = f32[1728,3]{0,1:T(4,128)} copy(f32[1728,3]{0,1:T(4,128)S(1)} %bitcast.8) | data formatting | bytes 41472
  23.1 0.1 copy-done
  23.2 0.6 %copy.17 = f32[1728,3]{0,1:T(4,128)} copy(f32[1728,3]{0,1:T(4,128)S(1)} %bitcast.7) | data formatting | bytes 41472
Async XLA Ops:
  0.6 1.3 %copy-start.3 = (s32[1728]{0:T(1024)S(1)}, s32[1728]{0:T(1024)}, u32[]{:S(2)}) copy-start(s32[1728]{0:T(1024)} %param.9) | copy-start | bytes 20740
  19.0 2.6 %copy-start.2 = (f32[3,1728]{1,0:T(4,128)S(1)}, f32[3,1728]{1,0:T(4,128)}, u32[]{:S(2)}) copy-start(f32[3,1728]{1,0:T(4,128)} %get-tuple-element.12) | copy-start | bytes 62212
  21.7 0.8 %copy-start.1 = (f32[3,1728]{1,0:T(4,128)S(1)}, f32[3,1728]{1,0:T(4,128)}, u32[]{:S(2)}) copy-start(f32[3,1728]{1,0:T(4,128)} %get-tuple-element.13) | copy-start | bytes 62212
  22.4 0.8 %copy-start = (f32[3,1728]{1,0:T(4,128)S(1)}, f32[3,1728]{1,0:T(4,128)}, u32[]{:S(2)}) copy-start(f32[3,1728]{1,0:T(4,128)} %get-tuple-element.14) | copy-start | bytes 62212

commit v2 on v1

--- a/solution.py
+++ b/solution.py
@@ -24,6 +24,7 @@
 U_CUT = 4.0 * (CUT6 * CUT6 - CUT6)
 DU_CUT = (-48.0 * CUT6 * CUT6 + 24.0 * CUT6) / RCUT
 DELTAS = [(d >> 2 & 1, d >> 1 & 1, d & 1) for d in range(1, 8)]
+SEND_ORDER = [(1, 1, 0), (1, 1, 1), (0, 1, 0), (1, 0, 0), (0, 1, 1), (1, 0, 1), (0, 0, 1)]
 SHIFTS = [(dx, dy) for dy in range(-2, 3) for dx in range(-2, 3)]
 NF = 7
 
@@ -47,8 +48,16 @@
     return lax.dot_general(a, b, (((1,), (0,)), ((), ())), preferred_element_type=F32)
 
 
-def buf_shape(delta):
-    return (NF * (8 if delta[0] else 16), 128 if delta[1] else 256)
+def tile_of(delta):
+    return 8 if delta[0] else 16, 128 if delta[1] else 256
+
+
+def pos_arrays(delta):
+    return 2 if delta[2] and (delta[0] or delta[1]) else 3
+
+
+def vel_arrays(delta):
+    return 1 if delta[0] or delta[1] else 4
 
 
 def to_delta(g, delta):
@@ -65,21 +74,72 @@
     return g
 
 
-def from_delta(b, delta):
+def wide(b):
+    lane = iota(b.shape, 1)
+    return jnp.concatenate([jnp.where(lane < 48, b, 0.0), jnp.where(lane >= 80, b, 0.0)], axis=1)
+
+
+def tall(b):
+    row = iota(b.shape, 0)
+    return jnp.concatenate([jnp.where(row < 3, b, 0.0), jnp.where(row >= 5, b, 0.0)], axis=0)
+
+
+def pack_pos(f, delta):
+    if pos_arrays(delta) == 3:
+        return f
+    return [f[0] + pltpu.roll(f[1], 6, 1), f[2]]
+
+
+def unpack_pos(a, delta):
+    if pos_arrays(delta) == 3:
+        return a
+    n = a[0].shape[1]
+    xf = iota(a[0].shape, 1) & 15
+    edge = (xf < 3) | (xf >= 13)
+    return [jnp.where(edge, a[0], 0.0), jnp.where(edge, pltpu.roll(a[0], n - 6, 1), 0.0), a[1]]
+
+
+def pack_vel(f, delta):
     dz, dy, _ = delta
+    if dz:
+        row = iota(f[0].shape, 0)
+        out = jnp.zeros_like(f[0])
+        for k in range(4):
+            out = jnp.where(row == 2 * k, jnp.broadcast_to(f[k][2:3], out.shape), out)
+            out = jnp.where(row == 2 * k + 1, jnp.broadcast_to(f[k][5:6], out.shape), out)
+        return [out]
     if dy:
-        lane = iota(b.shape, 1)
-        b = jnp.concatenate([jnp.where(lane < 48, b, 0.0), jnp.where(lane >= 80, b, 0.0)], axis=1)
+        group = iota(f[0].shape, 1) >> 4
+        out = jnp.where((group == 2) | (group == 5), f[0], 0.0)
+        out = jnp.where((group == 3) | (group == 6), pltpu.roll(f[1], 16, 1), out)
+        out = jnp.where((group == 4) | (group == 7), pltpu.roll(f[2], 32, 1), out)
+        out = jnp.where(group == 0, pltpu.roll(f[3], 96, 1), out)
+        return [jnp.where(group == 1, pltpu.roll(f[3], 64, 1), out)]
+    return f
+
+
+def unpack_vel(a, delta):
+    dz, dy, _ = delta
     if dz:
-        row = iota(b.shape, 0)
-        b = jnp.concatenate([jnp.where(row < 3, b, 0.0), jnp.where(row >= 5, b, 0.0)], axis=0)
-    return b
+        row = iota(a[0].shape, 0)
+        return [jnp.where(row == 2, jnp.broadcast_to(a[0][2 * k:2 * k + 1], a[0].shape), jnp.where(row == 5, jnp.broadcast_to(a[0][2 * k + 1:2 * k + 2], a[0].shape), 0.0)) for k in range(4)]
+    if dy:
+        group = iota(a[0].shape, 1) >> 4
+        low, high = group == 2, group == 5
+        both = low | high
+        last = jnp.where(low, pltpu.roll(a[0], 32, 1), jnp.where(high, pltpu.roll(a[0], 64, 1), 0.0))
+        return [jnp.where(both, a[0], 0.0), jnp.where(both, pltpu.roll(a[0], 112, 1), 0.0), jnp.where(both, pltpu.roll(a[0], 96, 1), 0.0), last]
+    return a
+
+
+def merge(own, parts):
+    flat = own + parts[(0, 0, 1)] + wide(parts[(0, 1, 0)] + parts[(0, 1, 1)])
+    return flat + tall(parts[(1, 0, 0)] + parts[(1, 0, 1)] + wide(parts[(1, 1, 0)] + parts[(1, 1, 1)]))
 
 
 def kernel(pos_ref, vel_ref, frc_ref, id_ref, val_ref, opos_ref, ovel_ref, ofrc_ref, oid_ref, oval_ref, oen_ref, *scratch):
-    sbufs = scratch[0:7]
-    rbufs = scratch[7:14]
-    atom_ref, g_ref, t_ref, q_ref, ebuf, send_sem, recv_sem, esend_sem, erecv_sem = scratch[14:]
+    psend, precv, vsend, vrecv = (scratch[7 * i:7 * i + 7] for i in range(4))
+    atom_ref, g_ref, t_ref, q_ref, ebuf, psend_sem, precv_sem, vsend_sem, vrecv_sem, esend_sem, erecv_sem = scratch[28:]
     bz, by, bx = lax.axis_index("bz"), lax.axis_index("by"), lax.axis_index("bx")
 
     def partner(delta):
@@ -98,8 +158,8 @@
     rel = moved - brick_lo
     rel = jnp.where(rel < -0.5 * BRICK, rel + BOX, jnp.where(rel >= 1.5 * BRICK, rel - BOX, rel))
     cell = jnp.floor(rel * (1.0 / SPACING)).astype(jnp.int32) + 2
-    live = val_ref[...] == 1
-    ids = id_ref[...]
+    live = val_ref[...].reshape(1, CAP) == 1
+    ids = id_ref[...].reshape(1, CAP)
     atom_ref[:, pl.ds(KPAD - 128, 128)] = jnp.zeros((atom_ref.shape[0], 128), F32)
     zi = jnp.where(live, cell[2:3, :], 0)
     lo = jnp.where(live, cell[1:2, :] * 16 + cell[0:1, :], 0)
@@ -119,32 +179,48 @@
     def spread(row_idx):
         return jnp.where(zmask, jnp.broadcast_to(atom_ref[row_idx:row_idx + 1, :], (16, KPAD)), 0.0).astype(BF16)
 
-    order = [8 * k + c for k in range(6) for c in range(3)] + [48, 49]
-    lhs = jnp.concatenate([spread(i) for i in order], axis=0)
+    def exchange(src, dst, ssem, rsem):
+        copies = {}
+        for delta in SEND_ORDER:
+            k = DELTAS.index(delta)
+            copies[delta] = pltpu.make_async_remote_copy(src_ref=src[k], dst_ref=dst[k], send_sem=ssem.at[k], recv_sem=rsem.at[k], device_id=partner(delta), device_id_type=MESH_ID)
+            copies[delta].start()
+        return copies
+
+    def fill(bufs, fields, pack):
+        for k, delta in enumerate(DELTAS):
+            rz = tile_of(delta)[0]
+            for i, arr in enumerate(pack([to_delta(f, delta) for f in fields], delta)):
+                bufs[k][i * rz:(i + 1) * rz, :] = arr
+
+    def gather(own, bufs, count, unpack):
+        parts = {}
+        for k, delta in enumerate(DELTAS):
+            rz = tile_of(delta)[0]
+            parts[delta] = unpack([bufs[k][i * rz:(i + 1) * rz, :] for i in range(count(delta))], delta)
+        return [merge(own[f], {d: parts[d][f] for d in DELTAS}) for f in range(len(own))]
+
+    lhs = jnp.concatenate([spread(8 * k + c) for k in range(3) for c in range(3)], axis=0)
     binned = dot_nt(lhs, onehot)
-    g_ref[0:48, :] = binned[0:48] + binned[48:96] + binned[96:144]
-    g_ref[48:96, :] = binned[144:192] + binned[192:240] + binned[240:288]
-    g_ref[96:112, :] = binned[288:304] * 128.0 + binned[304:320]
-
-    for k, delta in enumerate(DELTAS):
-        rz = 8 if delta[0] else 16
-        for f in range(NF):
-            sbufs[k][f * rz:(f + 1) * rz, :] = to_delta(g_ref[16 * f:16 * f + 16, :], delta)
+    pos_own = [binned[16 * c:16 * c + 16] + binned[48 + 16 * c:64 + 16 * c] + binned[96 + 16 * c:112 + 16 * c] for c in range(3)]
+    fill(psend, pos_own, pack_pos)
+    for c in range(3):
+        g_ref[16 * c:16 * c + 16, :] = pos_own[c]
     pl.semaphore_wait(barrier, 7)
-    copies = []
-    for k, delta in enumerate(DELTAS):
-        copy = pltpu.make_async_remote_copy(src_ref=sbufs[k], dst_ref=rbufs[k], send_sem=send_sem.at[k], recv_sem=recv_sem.at[k], device_id=partner(delta), device_id_type=MESH_ID)
-        copy.start()
-        copies.append(copy)
-    for copy in copies:
-        copy.wait_recv()
-    fields = []
-    for f in range(NF):
-        acc = g_ref[16 * f:16 * f + 16, :]
-        for k, delta in enumerate(DELTAS):
-            rz = 8 if delta[0] else 16
-            acc = acc + from_delta(rbufs[k][f * rz:(f + 1) * rz, :], delta)
-        fields.append(acc)
+    copies = exchange(psend, precv, psend_sem, precv_sem)
+
+    lhs = jnp.concatenate([spread(8 * k + c) for k in range(3, 6) for c in range(3)] + [spread(48), spread(49)], axis=0)
+    binned = dot_nt(lhs, onehot)
+    vel_own = [binned[16 * c:16 * c + 16] + binned[48 + 16 * c:64 + 16 * c] + binned[96 + 16 * c:112 + 16 * c] for c in range(3)]
+    vel_own.append(binned[144:160] * 128.0 + binned[160:176])
+    fill(vsend, vel_own, pack_vel)
+    for c in range(4):
+        g_ref[48 + 16 * c:64 + 16 * c, :] = vel_own[c]
+    vcopies = exchange(vsend, vrecv, vsend_sem, vrecv_sem)
+
+    for delta in DELTAS:
+        copies[delta].wait_recv()
+    fields = gather([g_ref[16 * c:16 * c + 16, :] for c in range(3)], precv, pos_arrays, unpack_pos)
 
     present = fields[0] != 0.0
     lane = iota((16, 256), 1)
@@ -162,11 +238,14 @@
             for c in range(3):
                 rolled = pltpu.roll(local[c], (256 - left) % 256, 1)
                 t_ref[3 * s + c, pl.ds(h, 16, stride=2), :] = rolled[:, 0:128]
-    for h in range(2):
-        left = 32 + 96 * h
-        for f in range(NF):
-            rolled = pltpu.roll(fields[f], (256 - left) % 256, 1)
+
+    def keep(f, x):
+        for h in range(2):
+            rolled = pltpu.roll(x, (256 - 32 - 96 * h) % 256, 1)
             q_ref[f, pl.ds(h, 16, stride=2), :] = rolled[:, 0:128]
+
+    for c in range(3):
+        keep(c, fields[c])
 
     base = SHIFTS.index((0, 0))
     mine = [t_ref[3 * base + c, 4:28, :] for c in range(3)]
@@ -223,6 +302,11 @@
         copy.start()
         ecopies.append(copy)
 
+    for delta in DELTAS:
+        vcopies[delta].wait_recv()
+    for f, x in enumerate(gather([g_ref[48 + 16 * c:64 + 16 * c, :] for c in range(4)], vrecv, vel_arrays, unpack_vel)):
+        keep(3 + f, x)
+
     idv = jnp.where(own, q_ref[6, 4:28, :], -1.0)
     id_int = idv.astype(jnp.int32)
     id_hi = jnp.where(own, id_int >> 7, -1).astype(F32)
@@ -283,8 +367,17 @@
     for k in range(1, 8):
         acc = acc + ebuf[k]
     oen_ref[...] = jnp.sum(jnp.sum(acc, axis=0, keepdims=True), axis=1, keepdims=True)
-    for copy in copies + ecopies:
+    for copy in list(copies.values()) + list(vcopies.values()) + ecopies:
         copy.wait_send()
+
+
+def finish(pos_ref, vel_ref, frc_ref, id_ref, val_ref, en_ref, opos_ref, ovel_ref, ofrc_ref, oid_ref, oval_ref, oen_ref):
+    opos_ref[...] = pos_ref[...]
+    ovel_ref[...] = vel_ref[...]
+    ofrc_ref[...] = frc_ref[...]
+    oid_ref[...] = id_ref[...].reshape(CAP)
+    oval_ref[...] = val_ref[...].reshape(CAP)
+    oen_ref[...] = en_ref[...]
 
 
 def solution(mesh):
@@ -294,13 +387,13 @@
 
     def local_step(pos, vel, frc, ids, valid):
         f3 = jax.ShapeDtypeStruct((3, CAP), F32)
-        i1 = jax.ShapeDtypeStruct((1, CAP), jnp.int32)
+        i1 = jax.ShapeDtypeStruct((CAP,), jnp.int32)
         outs = pl.pallas_call(
             kernel,
-            out_shape=(f3, f3, f3, i1, i1, jax.ShapeDtypeStruct((1, 1), F32)),
+            out_shape=(pltpu.VMEM((3, CAP), F32),) * 3 + (pltpu.VMEM((1, CAP), jnp.int32),) * 2 + (pltpu.VMEM((1, 1), F32),),
             in_specs=[vmem] * 5,
             out_specs=(vmem,) * 6,
-            scratch_shapes=[pltpu.VMEM(buf_shape(d), F32) for d in DELTAS] * 2 + [
+            scratch_shapes=[pltpu.VMEM((pos_arrays(d) * tile_of(d)[0], tile_of(d)[1]), F32) for d in DELTAS] * 2 + [pltpu.VMEM((vel_arrays(d) * tile_of(d)[0], tile_of(d)[1]), F32) for d in DELTAS] * 2 + [
                 pltpu.VMEM((56, KPAD), F32),
                 pltpu.VMEM((112, 256), F32),
                 pltpu.VMEM((75, 32, 128), F32),
@@ -310,9 +403,18 @@
                 pltpu.SemaphoreType.DMA((7,)),
                 pltpu.SemaphoreType.DMA((7,)),
                 pltpu.SemaphoreType.DMA((7,)),
+                pltpu.SemaphoreType.DMA((7,)),
+                pltpu.SemaphoreType.DMA((7,)),
             ],
             compiler_params=pltpu.CompilerParams(collective_id=0, has_side_effects=True),
-        )(pos.T, vel.T, frc.T, ids[None, :], valid[None, :])
-        return outs[0].T, outs[1].T, outs[2].T, outs[3][0], outs[4][0], outs[5][0, 0]
+        )(pos.T, vel.T, frc.T, ids, valid)
+        outs = pl.pallas_call(
+            finish,
+            out_shape=(f3, f3, f3, i1, i1, jax.ShapeDtypeStruct((1, 1), F32)),
+            in_specs=[vmem] * 6,
+            out_specs=(vmem,) * 6,
+            compiler_params=pltpu.CompilerParams(vmem_limit_bytes=4 << 20),
+        )(*outs)
+        return outs[0].T, outs[1].T, outs[2].T, outs[3], outs[4], outs[5][0, 0]
 
     return jax.shard_map(local_step, mesh=mesh, in_specs=(row_spec, row_spec, row_spec, flat_spec, flat_spec), out_specs=(row_spec, row_spec, row_spec, flat_spec, flat_spec, P()), check_vma=False)

time: 26 us -> 16.2 us (0.62); the launches traced: 25.5 us -> 16 us
  local copies, waits for them, and re-layouts: 4.03 us -> 0 us
  other arithmetic: 2.63 us -> 0 us
  between operations: 2.35 us -> 0.64 us
  Pallas kernels: 16.5 us -> 15.4 us
    pallas_call x2 -> x0, other arithmetic: 2.63 us -> none  [local_step(): pl.pallas_call(kernel, out_shape=(f3, f3, f3, i1, i1, jax.ShapeDtypeStruc...]
    unnamed x11 -> x0, local copies, waits for them, and re-layouts: 2.13 us -> none
    broadcast_in_dim x2 -> x0, local copies, waits for them, and re-layouts: 1.9 us -> none  [the longest x1 1.3 us: local_step(): ids[None, :]]
    pallas_call x1 -> x2, Pallas kernels: 16.5 us -> 15.4 us  [the longest x1 14.1 us: local_step(): pl.pallas_call(kernel, out_shape=(pltpu.VMEM((3, CAP), F32),) * 3 + (pltp...]
where the time goes in v2:
time: 16.2 us; the launch traced here: 16 us
  Pallas kernels  15.4 us (95%)
  between operations  0.64 us (4%)
    pallas_call x1, Pallas kernels, local_step(): pl.pallas_call(kernel, out_shape=(pltpu.VMEM((3, CAP), F32),) * 3 + (pltp...  14.1 us
    pallas_call x1, Pallas kernels, local_step(): pl.pallas_call(finish, out_shape=(f3, f3, f3, i1, i1, jax.ShapeDtypeStruc...  1.28 us

profile of v2, /device:TPU:0, one launch (start us, length us, event | category | flops | bytes accessed | tf_op | source)
XLA Modules:
  0.0 16.0 jit_solution(11953383683008148113)
XLA Ops:
  0.6 14.1 %shard_map.100 = (f32[3,1728]{1,0:T(4,128)S(1)}, f32[3,1728]{1,0:T(4,128)S(1)}, f32[3,1728]{1,0:T(4,128)S(1)}, s32[1,1728]{1,0:T(1,128)S(1)}, s32[1,1728]{1,0:T(1,128)S(1)}, /*index=5*/f32[1,1]{1,0:T(1,128)}) custom-call(f32[3,1728]{1,0:T(4,128)} %bitcast.7, f32[3,1728]{1,0:T(4,128)} %bitcast.8, f32[3,1728]{1,0:T(4,128)} %bitcast.9, s32[1728]{0:T(1024)} %id_ref.1, ...), custom_call_target="tpu_custom_call" | custom-call | tf_op jit(solution)/shard_map/pallas_call | solution.py:391
  14.8 1.3 %shard_map.101 = (f32[3,1728]{1,0:T(4,128)}, f32[3,1728]{1,0:T(4,128)}, f32[3,1728]{1,0:T(4,128)}, s32[1728]{0:T(1024)}, s32[1728]{0:T(1024)}, /*index=5*/f32[1,1]{1,0:T(1,128)}) custom-call(f32[3,1728]{1,0:T(4,128)S(1)} %get-tuple-element.18.pos_ref, f32[3,1728]{1,0:T(4,128)S(1)} %get-tuple-element.19.vel_ref, f32[3,1728]{1,0:T(4,128)S(1)} %get-tuple-element.20.frc_ref, ...), custom_call_target="tpu_custom_call" | custom-call | tf_op jit(solution)/shard_map/pallas_call | solution.py:411

commit v3 on v2

--- a/solution.py
+++ b/solution.py
@@ -139,7 +139,7 @@
 
 def kernel(pos_ref, vel_ref, frc_ref, id_ref, val_ref, opos_ref, ovel_ref, ofrc_ref, oid_ref, oval_ref, oen_ref, *scratch):
     psend, precv, vsend, vrecv = (scratch[7 * i:7 * i + 7] for i in range(4))
-    atom_ref, g_ref, t_ref, q_ref, ebuf, psend_sem, precv_sem, vsend_sem, vrecv_sem, esend_sem, erecv_sem = scratch[28:]
+    atom_ref, g_ref, t_ref, q_ref, p_ref, ebuf, psend_sem, precv_sem, vsend_sem, vrecv_sem, esend_sem, erecv_sem = scratch[28:]
     bz, by, bx = lax.axis_index("bz"), lax.axis_index("by"), lax.axis_index("bx")
 
     def partner(delta):
@@ -232,7 +232,8 @@
         u = jnp.where(u < -0.5 * BRICK, u + BOX, jnp.where(u >= 1.5 * BRICK, u - BOX, u))
         local.append(jnp.where(present, u, 1000.0 + 10.0 * frame[c].astype(F32)))
 
-    for s, (dx, dy) in enumerate(SHIFTS):
+    def shift_in(s):
+        dx, dy = SHIFTS[s]
         for h in range(2):
             left = 32 + 96 * h + 16 * dy + dx
             for c in range(3):
@@ -244,60 +245,67 @@
             rolled = pltpu.roll(x, (256 - 32 - 96 * h) % 256, 1)
             q_ref[f, pl.ds(h, 16, stride=2), :] = rolled[:, 0:128]
 
-    for c in range(3):
-        keep(c, fields[c])
-
-    base = SHIFTS.index((0, 0))
-    mine = [t_ref[3 * base + c, 4:28, :] for c in range(3)]
-
-    def pair(carry, nbr):
-        fx, fy, fz, sw, s6, sr, sn = carry
-        ex, ey, ez = mine[0] - nbr[0], mine[1] - nbr[1], mine[2] - nbr[2]
-        r2 = ex * ex + ey * ey + ez * ez
-        near = r2 < RCUT * RCUT
-        inv = jnp.where(near, lax.rsqrt(r2), 0.0)
-        i2 = inv * inv
-        i6 = i2 * i2 * i2
-        w = i6 * (i6 - 0.5)
-        fr = w * i2 + (DU_CUT / 48.0) * inv
-        return (fx + fr * ex, fy + fr * ey, fz + fr * ez, sw + w, s6 + i6, sr + r2 * inv, sn + jnp.where(near, 1.0, 0.0))
-
-    def load(s, dz):
+    def load(dx, dy, dz):
+        s = SHIFTS.index((dx, dy))
         return [t_ref[3 * s + c, 4 + 2 * dz:28 + 2 * dz, :] for c in range(3)]
 
-    carry = tuple(jnp.zeros((24, 128), F32) for _ in range(7))
-    for s, (dx, dy) in enumerate(SHIFTS):
-        twos = (abs(dx) == 2) + (abs(dy) == 2)
-        if twos == 2:
-            continue
-        for dz in (range(-2, 3) if twos == 0 else range(-1, 2)):
-            if (dx, dy, dz) != (0, 0, 0):
-                carry = pair(carry, load(s, dz))
     low_x = (iota((24, 128), 1) & 15) < 8
     row24 = iota((24, 128), 0)
     low_y = (row24 & 1) == 0
     low_z = row24 < 12
-    idx = SHIFTS.index
+
+    def pick(mask, p, q):
+        return [jnp.where(mask, p[c], q[c]) for c in range(3)]
+
+    def half(dx, dy, dz):
+        return dy > 0 or (dy == 0 and (dx > 0 or (dx == 0 and dz > 0)))
+
+    offsets = [(dx, dy, dz) for dx, dy in SHIFTS for dz in range(-2, 3) if (dx, dy, dz) != (0, 0, 0) and (abs(dx) == 2) + (abs(dy) == 2) + (abs(dz) == 2) <= 1]
+    first = [functools.partial(load, *d) for d in offsets if half(*d)]
+    second = [functools.partial(load, *d) for d in offsets if not half(*d)]
     for dz in range(-1, 2):
-        a, b, c2, d = load(idx((-2, -2)), dz), load(idx((2, -2)), dz), load(idx((-2, 2)), dz), load(idx((2, 2)), dz)
-        carry = pair(carry, [jnp.where(low_y, jnp.where(low_x, a[c], b[c]), jnp.where(low_x, c2[c], d[c])) for c in range(3)])
-    for dy in range(-1, 2):
-        a, b, c2, d = load(idx((-2, dy)), -2), load(idx((2, dy)), -2), load(idx((-2, dy)), 2), load(idx((2, dy)), 2)
-        carry = pair(carry, [jnp.where(low_z, jnp.where(low_x, a[c], b[c]), jnp.where(low_x, c2[c], d[c])) for c in range(3)])
+        first.append(lambda dz=dz: pick(low_x, load(-2, 2, dz), load(2, 2, dz)))
+        second.append(lambda dz=dz: pick(low_x, load(-2, -2, dz), load(2, -2, dz)))
     for dx in range(-1, 2):
-        a, b, c2, d = load(idx((dx, -2)), -2), load(idx((dx, 2)), -2), load(idx((dx, -2)), 2), load(idx((dx, 2)), 2)
-        carry = pair(carry, [jnp.where(low_z, jnp.where(low_y, a[c], b[c]), jnp.where(low_y, c2[c], d[c])) for c in range(3)])
-    force = [48.0 * carry[c] for c in range(3)]
-
+        first.append(lambda dx=dx: pick(low_z, load(dx, 2, -2), load(dx, 2, 2)))
+        second.append(lambda dx=dx: pick(low_z, load(dx, -2, -2), load(dx, -2, 2)))
+    for dy in (1, -1):
+        (first if dy == 1 else second).append(lambda dy=dy: pick(low_z, pick(low_x, load(-2, dy, -2), load(2, dy, -2)), pick(low_x, load(-2, dy, 2), load(2, dy, 2))))
+    first.append(lambda: pick(low_z, load(2, 0, -2), load(2, 0, 2)))
+    second.append(lambda: pick(low_z, load(-2, 0, -2), load(-2, 0, 2)))
+
+    for s, (dx, dy) in enumerate(SHIFTS):
+        if dy > 0 or (dy == 0 and dx >= 0):
+            shift_in(s)
+    mine = load(0, 0, 0)
+
+    def apart(nbr):
+        ex, ey, ez = mine[0] - nbr[0], mine[1] - nbr[1], mine[2] - nbr[2]
+        r2 = ex * ex + ey * ey + ez * ez
+        near = r2 < RCUT * RCUT
+        return ex, ey, ez, r2, near, jnp.where(near, lax.rsqrt(r2), 0.0)
+
+    sw, sr, sn = (jnp.zeros((24, 128), F32) for _ in range(3))
+    for i, nbr in enumerate(first):
+        ex, ey, ez, r2, near, inv = apart(nbr())
+        i2 = inv * inv
+        i6 = i2 * i2 * i2
+        sw = sw + i6 * (i6 - 1.0)
+        sr = sr + r2 * inv
+        sn = sn + jnp.where(near, 1.0, 0.0)
+        for k, x in enumerate((ex, ey, ez, inv)):
+            p_ref[4 * i + k] = x
+    keep(0, fields[0])
     lane24 = iota((24, 128), 1)
     x24 = lane24 & 15
     own = (lane24 < 96) & (x24 >= 2) & (x24 < 14) & (q_ref[0, 4:28, :] != 0.0)
-    energy = 4.0 * (carry[3] - 0.5 * carry[4]) - DU_CUT * carry[5] + (RCUT * DU_CUT - U_CUT) * carry[6]
-    energy = jnp.where(own, 0.5 * energy, 0.0)
+    energy = 4.0 * sw - DU_CUT * sr + (RCUT * DU_CUT - U_CUT) * sn
+    energy = jnp.where(own, energy, 0.0)
     me = bz * 4 + by * 2 + bx
     ebuf[me, :, :] = energy[0:8] + energy[8:16] + energy[16:24]
     ecopies = []
-    for k, delta in enumerate(DELTAS):
+    for delta in SEND_ORDER:
+        k = DELTAS.index(delta)
         copy = pltpu.make_async_remote_copy(src_ref=ebuf.at[me], dst_ref=ebuf.at[me], send_sem=esend_sem.at[k], recv_sem=erecv_sem.at[k], device_id=partner(delta), device_id_type=MESH_ID)
         copy.start()
         ecopies.append(copy)
@@ -306,6 +314,26 @@
         vcopies[delta].wait_recv()
     for f, x in enumerate(gather([g_ref[48 + 16 * c:64 + 16 * c, :] for c in range(4)], vrecv, vel_arrays, unpack_vel)):
         keep(3 + f, x)
+    for c in range(1, 3):
+        keep(c, fields[c])
+
+    for s, (dx, dy) in enumerate(SHIFTS):
+        if not (dy > 0 or (dy == 0 and dx >= 0)):
+            shift_in(s)
+
+    def push(acc, ex, ey, ez, inv):
+        i2 = inv * inv
+        i6 = i2 * i2 * i2
+        fr = (i6 * (i6 - 0.5)) * i2 + (DU_CUT / 48.0) * inv
+        return (acc[0] + fr * ex, acc[1] + fr * ey, acc[2] + fr * ez)
+
+    acc = tuple(jnp.zeros((24, 128), F32) for _ in range(3))
+    for i in range(len(first)):
+        acc = push(acc, *(p_ref[4 * i + k] for k in range(4)))
+    for nbr in second:
+        ex, ey, ez, r2, near, inv = apart(nbr())
+        acc = push(acc, ex, ey, ez, inv)
+    force = [48.0 * acc[c] for c in range(3)]
 
     idv = jnp.where(own, q_ref[6, 4:28, :], -1.0)
     id_int = idv.astype(jnp.int32)
@@ -398,6 +426,7 @@
                 pltpu.VMEM((112, 256), F32),
                 pltpu.VMEM((75, 32, 128), F32),
                 pltpu.VMEM((NF, 32, 128), F32),
+                pltpu.VMEM((192, 24, 128), F32),
                 pltpu.VMEM((8, 8, 128), F32),
                 pltpu.SemaphoreType.DMA((7,)),
                 pltpu.SemaphoreType.DMA((7,)),

time: 16.2 us -> 15.1 us (0.932)
  Pallas kernels: 15.4 us -> 14.3 us
    pallas_call x1, Pallas kernels: 14.1 us -> 13 us  [local_step(): pl.pallas_call(kernel, out_shape=(pltpu.VMEM((3, CAP), F32),) * 3 + (pltp...]
where the time goes in v3:
time: 15.1 us; the launch traced here: 15 us
  Pallas kernels  14.3 us (95%)
  between operations  0.64 us (4%)
    pallas_call x1, Pallas kernels, local_step(): pl.pallas_call(kernel, out_shape=(pltpu.VMEM((3, CAP), F32),) * 3 + (pltp...  13 us
    pallas_call x1, Pallas kernels, local_step(): pl.pallas_call(finish, out_shape=(f3, f3, f3, i1, i1, jax.ShapeDtypeStruc...  1.28 us

profile of v3, /device:TPU:0, one launch (start us, length us, event | category | flops | bytes accessed | tf_op | source)
XLA Modules:
  0.0 15.0 jit_solution(18309381191999070177)
XLA Ops:
  0.6 13.0 %shard_map.100 = (f32[3,1728]{1,0:T(4,128)S(1)}, f32[3,1728]{1,0:T(4,128)S(1)}, f32[3,1728]{1,0:T(4,128)S(1)}, s32[1,1728]{1,0:T(1,128)S(1)}, s32[1,1728]{1,0:T(1,128)S(1)}, /*index=5*/f32[1,1]{1,0:T(1,128)}) custom-call(f32[3,1728]{1,0:T(4,128)} %bitcast.7, f32[3,1728]{1,0:T(4,128)} %bitcast.8, f32[3,1728]{1,0:T(4,128)} %bitcast.9, s32[1728]{0:T(1024)} %id_ref.1, ...), custom_call_target="tpu_custom_call" | custom-call | tf_op jit(solution)/shard_map/pallas_call | solution.py:419
  13.7 1.3 %shard_map.101 = (f32[3,1728]{1,0:T(4,128)}, f32[3,1728]{1,0:T(4,128)}, f32[3,1728]{1,0:T(4,128)}, s32[1728]{0:T(1024)}, s32[1728]{0:T(1024)}, /*index=5*/f32[1,1]{1,0:T(1,128)}) custom-call(f32[3,1728]{1,0:T(4,128)S(1)} %get-tuple-element.18.pos_ref, f32[3,1728]{1,0:T(4,128)S(1)} %get-tuple-element.19.vel_ref, f32[3,1728]{1,0:T(4,128)S(1)} %get-tuple-element.20.frc_ref, ...), custom_call_target="tpu_custom_call" | custom-call | tf_op jit(solution)/shard_map/pallas_call | solution.py:440

commit v4 on v3

--- a/solution.py
+++ b/solution.py
@@ -44,6 +44,11 @@
     return lax.dot_general(a, b, (((1,), (1,)), ((), ())), preferred_element_type=F32)
 
 
+def dot_split(a, b, true):
+    cut = a.shape[1] // 512 * 256
+    return dot_nt(a[:, :cut], b[:, :cut]) + jnp.where(true, dot_nt(a[:, cut:], b[:, cut:]), 0.0)
+
+
 def dot_nn(a, b):
     return lax.dot_general(a, b, (((1,), (0,)), ((), ())), preferred_element_type=F32)
 
@@ -58,6 +63,15 @@
 
 def vel_arrays(delta):
     return 1 if delta[0] or delta[1] else 4
+
+
+def offsets_of(arrays):
+    starts, row = {}, 0
+    for delta in DELTAS:
+        starts[delta] = row
+        rz, lanes = tile_of(delta)
+        row += arrays(delta) * rz * lanes // 128
+    return starts, row
 
 
 def to_delta(g, delta):
@@ -137,10 +151,14 @@
     return flat + tall(parts[(1, 0, 0)] + parts[(1, 0, 1)] + wide(parts[(1, 1, 0)] + parts[(1, 1, 1)]))
 
 
-def kernel(pos_ref, vel_ref, frc_ref, id_ref, val_ref, opos_ref, ovel_ref, ofrc_ref, oid_ref, oval_ref, oen_ref, *scratch):
-    psend, precv, vsend, vrecv = (scratch[7 * i:7 * i + 7] for i in range(4))
-    atom_ref, g_ref, t_ref, q_ref, p_ref, ebuf, psend_sem, precv_sem, vsend_sem, vrecv_sem, esend_sem, erecv_sem = scratch[28:]
+def kernel(pos_hbm, vel_hbm, frc_hbm, id_hbm, val_hbm, opos_ref, ovel_ref, ofrc_ref, oid_ref, oval_ref, oen_ref, *scratch):
+    psend, precv, vsend, vrecv, pos_ref, vel_ref, frc_ref, id_ref, val_ref, in_sem, atom_ref, g_ref, t_ref, q_ref, p_ref, ebuf, psend_sem, precv_sem, vsend_sem, vrecv_sem, esend_sem, erecv_sem = scratch
+    loads = [pltpu.make_async_copy(src, dst, in_sem.at[i]) for i, (src, dst) in enumerate(((vel_hbm, vel_ref), (frc_hbm, frc_ref), (pos_hbm, pos_ref), (val_hbm, val_ref), (id_hbm, id_ref)))]
+    for copy in loads:
+        copy.start()
     bz, by, bx = lax.axis_index("bz"), lax.axis_index("by"), lax.axis_index("bx")
+
+    true = bz >= 0
 
     def partner(delta):
         return (lax.rem(bz + delta[0], 2), lax.rem(by + delta[1], 2), lax.rem(bx + delta[2], 2))
@@ -149,6 +167,8 @@
     for delta in DELTAS:
         pl.semaphore_signal(barrier, inc=1, device_id=partner(delta), device_id_type=MESH_ID)
 
+    for copy in loads:
+        copy.wait()
     v_half = vel_ref[...] + (0.5 * TIME_STEP) * frc_ref[...]
     moved = pos_ref[...] + TIME_STEP * v_half
     moved = moved - BOX * jnp.floor(moved * (1.0 / BOX))
@@ -179,47 +199,57 @@
     def spread(row_idx):
         return jnp.where(zmask, jnp.broadcast_to(atom_ref[row_idx:row_idx + 1, :], (16, KPAD)), 0.0).astype(BF16)
 
-    def exchange(src, dst, ssem, rsem):
-        copies = {}
+    def exchange(src, dst, ssem, rsem, arrays):
+        starts, total = offsets_of(arrays)
         for delta in SEND_ORDER:
-            k = DELTAS.index(delta)
-            copies[delta] = pltpu.make_async_remote_copy(src_ref=src[k], dst_ref=dst[k], send_sem=ssem.at[k], recv_sem=rsem.at[k], device_id=partner(delta), device_id_type=MESH_ID)
-            copies[delta].start()
-        return copies
-
-    def fill(bufs, fields, pack):
-        for k, delta in enumerate(DELTAS):
-            rz = tile_of(delta)[0]
-            for i, arr in enumerate(pack([to_delta(f, delta) for f in fields], delta)):
-                bufs[k][i * rz:(i + 1) * rz, :] = arr
-
-    def gather(own, bufs, count, unpack):
+            rz, lanes = tile_of(delta)
+            part = pl.ds(starts[delta], arrays(delta) * rz * lanes // 128)
+            pltpu.make_async_remote_copy(src_ref=src.at[part], dst_ref=dst.at[part], send_sem=ssem, recv_sem=rsem, device_id=partner(delta), device_id_type=MESH_ID).start()
+        return pltpu.make_async_remote_copy(src_ref=src, dst_ref=dst, send_sem=ssem, recv_sem=rsem, device_id=partner(DELTAS[0]), device_id_type=MESH_ID)
+
+    def fill(buf, fields, pack, arrays):
+        starts, _ = offsets_of(arrays)
+        for delta in DELTAS:
+            rz, lanes = tile_of(delta)
+            row = starts[delta]
+            for arr in pack([to_delta(f, delta) for f in fields], delta):
+                for j in range(lanes // 128):
+                    buf[row:row + rz, :] = arr[:, 128 * j:128 * j + 128]
+                    row += rz
+
+    def gather(own, buf, arrays, unpack):
+        starts, _ = offsets_of(arrays)
         parts = {}
-        for k, delta in enumerate(DELTAS):
-            rz = tile_of(delta)[0]
-            parts[delta] = unpack([bufs[k][i * rz:(i + 1) * rz, :] for i in range(count(delta))], delta)
+        for delta in DELTAS:
+            rz, lanes = tile_of(delta)
+            row = starts[delta]
+            arrs = []
+            for i in range(arrays(delta)):
+                pieces = [buf[row + rz * j:row + rz * j + rz, :] for j in range(lanes // 128)]
+                row += rz * len(pieces)
+                arrs.append(pieces[0] if len(pieces) == 1 else jnp.concatenate(pieces, axis=1))
+            parts[delta] = unpack(arrs, delta)
         return [merge(own[f], {d: parts[d][f] for d in DELTAS}) for f in range(len(own))]
 
     lhs = jnp.concatenate([spread(8 * k + c) for k in range(3) for c in range(3)], axis=0)
-    binned = dot_nt(lhs, onehot)
+    binned = dot_split(lhs, onehot, true)
     pos_own = [binned[16 * c:16 * c + 16] + binned[48 + 16 * c:64 + 16 * c] + binned[96 + 16 * c:112 + 16 * c] for c in range(3)]
-    fill(psend, pos_own, pack_pos)
+    fill(psend, pos_own, pack_pos, pos_arrays)
     for c in range(3):
         g_ref[16 * c:16 * c + 16, :] = pos_own[c]
     pl.semaphore_wait(barrier, 7)
-    copies = exchange(psend, precv, psend_sem, precv_sem)
+    pos_all = exchange(psend, precv, psend_sem, precv_sem, pos_arrays)
 
     lhs = jnp.concatenate([spread(8 * k + c) for k in range(3, 6) for c in range(3)] + [spread(48), spread(49)], axis=0)
-    binned = dot_nt(lhs, onehot)
+    binned = dot_split(lhs, onehot, true)
     vel_own = [binned[16 * c:16 * c + 16] + binned[48 + 16 * c:64 + 16 * c] + binned[96 + 16 * c:112 + 16 * c] for c in range(3)]
     vel_own.append(binned[144:160] * 128.0 + binned[160:176])
-    fill(vsend, vel_own, pack_vel)
+    fill(vsend, vel_own, pack_vel, vel_arrays)
     for c in range(4):
         g_ref[48 + 16 * c:64 + 16 * c, :] = vel_own[c]
-    vcopies = exchange(vsend, vrecv, vsend_sem, vrecv_sem)
-
-    for delta in DELTAS:
-        copies[delta].wait_recv()
+    vel_all = exchange(vsend, vrecv, vsend_sem, vrecv_sem, vel_arrays)
+
+    pos_all.wait_recv()
     fields = gather([g_ref[16 * c:16 * c + 16, :] for c in range(3)], precv, pos_arrays, unpack_pos)
 
     present = fields[0] != 0.0
@@ -230,7 +260,7 @@
     for c in range(3):
         u = fields[c] - los[c].astype(F32) * BRICK
         u = jnp.where(u < -0.5 * BRICK, u + BOX, jnp.where(u >= 1.5 * BRICK, u - BOX, u))
-        local.append(jnp.where(present, u, 1000.0 + 10.0 * frame[c].astype(F32)))
+        local.append(jnp.where(present, u, 64.0 + 4.0 * frame[c].astype(F32)))
 
     def shift_in(s):
         dx, dy = SHIFTS[s]
@@ -282,36 +312,31 @@
     def apart(nbr):
         ex, ey, ez = mine[0] - nbr[0], mine[1] - nbr[1], mine[2] - nbr[2]
         r2 = ex * ex + ey * ey + ez * ez
-        near = r2 < RCUT * RCUT
-        return ex, ey, ez, r2, near, jnp.where(near, lax.rsqrt(r2), 0.0)
-
-    sw, sr, sn = (jnp.zeros((24, 128), F32) for _ in range(3))
+        r2 = jnp.minimum(r2, RCUT * RCUT)
+        return ex, ey, ez, r2, lax.rsqrt(r2)
+
+    sw, sr = jnp.zeros((24, 128), F32), jnp.zeros((24, 128), F32)
     for i, nbr in enumerate(first):
-        ex, ey, ez, r2, near, inv = apart(nbr())
+        ex, ey, ez, r2, inv = apart(nbr())
         i2 = inv * inv
         i6 = i2 * i2 * i2
         sw = sw + i6 * (i6 - 1.0)
         sr = sr + r2 * inv
-        sn = sn + jnp.where(near, 1.0, 0.0)
         for k, x in enumerate((ex, ey, ez, inv)):
             p_ref[4 * i + k] = x
     keep(0, fields[0])
     lane24 = iota((24, 128), 1)
     x24 = lane24 & 15
     own = (lane24 < 96) & (x24 >= 2) & (x24 < 14) & (q_ref[0, 4:28, :] != 0.0)
-    energy = 4.0 * sw - DU_CUT * sr + (RCUT * DU_CUT - U_CUT) * sn
+    energy = 4.0 * sw - DU_CUT * sr + (RCUT * DU_CUT - U_CUT) * len(first)
     energy = jnp.where(own, energy, 0.0)
     me = bz * 4 + by * 2 + bx
     ebuf[me, :, :] = energy[0:8] + energy[8:16] + energy[16:24]
-    ecopies = []
     for delta in SEND_ORDER:
-        k = DELTAS.index(delta)
-        copy = pltpu.make_async_remote_copy(src_ref=ebuf.at[me], dst_ref=ebuf.at[me], send_sem=esend_sem.at[k], recv_sem=erecv_sem.at[k], device_id=partner(delta), device_id_type=MESH_ID)
-        copy.start()
-        ecopies.append(copy)
-
-    for delta in DELTAS:
-        vcopies[delta].wait_recv()
+        pltpu.make_async_remote_copy(src_ref=ebuf.at[me], dst_ref=ebuf.at[me], send_sem=esend_sem, recv_sem=erecv_sem, device_id=partner(delta), device_id_type=MESH_ID).start()
+    energy_all = pltpu.make_async_remote_copy(src_ref=ebuf.at[pl.ds(0, 7)], dst_ref=ebuf.at[pl.ds(0, 7)], send_sem=esend_sem, recv_sem=erecv_sem, device_id=partner(DELTAS[0]), device_id_type=MESH_ID)
+
+    vel_all.wait_recv()
     for f, x in enumerate(gather([g_ref[48 + 16 * c:64 + 16 * c, :] for c in range(4)], vrecv, vel_arrays, unpack_vel)):
         keep(3 + f, x)
     for c in range(1, 3):
@@ -331,7 +356,7 @@
     for i in range(len(first)):
         acc = push(acc, *(p_ref[4 * i + k] for k in range(4)))
     for nbr in second:
-        ex, ey, ez, r2, near, inv = apart(nbr())
+        ex, ey, ez, r2, inv = apart(nbr())
         acc = push(acc, ex, ey, ez, inv)
     force = [48.0 * acc[c] for c in range(3)]
 
@@ -346,7 +371,7 @@
     hot_hi = jnp.where(flat(id_hi, 128) == iota((128, 3072), 0).astype(F32), 1.0, 0.0).astype(BF16)
     lo_eq = flat(id_lo, 128) == iota((128, 3072), 0).astype(F32)
     hot_lo = jnp.where(lo_eq, 1.0, 0.0).astype(BF16)
-    table = dot_nt(hot_lo, hot_hi).astype(BF16)
+    table = dot_split(hot_lo, hot_hi, true).astype(BF16)
     r128, c128 = iota((128, 128), 0), iota((128, 128), 1)
     below = dot_nn(jnp.where(c128 < r128, 1.0, 0.0).astype(BF16), table)
     total = dot_nn(jnp.ones((128, 128), BF16), table).astype(BF16)
@@ -354,7 +379,9 @@
     rank_tab = below + before
     tab_hi = jnp.floor(rank_tab * (1.0 / 256.0)) * 256.0
     tab_lo = rank_tab - tab_hi
-    looked = dot_nn(tab_hi.astype(BF16), hot_hi) + dot_nn(tab_lo.astype(BF16), hot_hi)
+    tabs = jnp.concatenate([tab_hi, tab_lo], axis=1).astype(BF16)
+    hot2 = jnp.concatenate([hot_hi, hot_hi], axis=0)
+    looked = jnp.concatenate([dot_nn(tabs, hot2[:, :1536]), dot_nn(tabs, hot2[:, 1536:])], axis=1)
     rank = jnp.sum(jnp.where(lo_eq, looked, 0.0), axis=0, keepdims=True)
     any_own = flat(jnp.where(own, 1.0, 0.0), 1) > 0.5
     rank_hi = jnp.floor(rank * (1.0 / 256.0))
@@ -372,7 +399,7 @@
         outs += list(split3(force[c]))
     outs += [id_hi, id_lo, jnp.where(own, 1.0, 0.0)]
     lhs = jnp.concatenate([jnp.where(hi_mask, flat(x, 8), 0.0) for x in outs], axis=0).astype(BF16)
-    slots = dot_nt(lhs, hot_slot)
+    slots = dot_split(lhs, hot_slot, true)
 
     def field(i):
         return slots[8 * i:8 * i + 8, :]
@@ -389,14 +416,13 @@
     put(oid_ref, 0, field(27) * 128.0 + field(28))
     put(oval_ref, 0, field(29))
 
-    for copy in ecopies:
-        copy.wait_recv()
+    for copy in (pos_all, vel_all, energy_all):
+        copy.wait_send()
+    energy_all.wait_recv()
     acc = ebuf[0]
     for k in range(1, 8):
         acc = acc + ebuf[k]
     oen_ref[...] = jnp.sum(jnp.sum(acc, axis=0, keepdims=True), axis=1, keepdims=True)
-    for copy in list(copies.values()) + list(vcopies.values()) + ecopies:
-        copy.wait_send()
 
 
 def finish(pos_ref, vel_ref, frc_ref, id_ref, val_ref, en_ref, opos_ref, ovel_ref, ofrc_ref, oid_ref, oval_ref, oen_ref):
@@ -419,21 +445,27 @@
         outs = pl.pallas_call(
             kernel,
             out_shape=(pltpu.VMEM((3, CAP), F32),) * 3 + (pltpu.VMEM((1, CAP), jnp.int32),) * 2 + (pltpu.VMEM((1, 1), F32),),
-            in_specs=[vmem] * 5,
+            in_specs=[pl.BlockSpec(memory_space=pltpu.HBM)] * 5,
             out_specs=(vmem,) * 6,
-            scratch_shapes=[pltpu.VMEM((pos_arrays(d) * tile_of(d)[0], tile_of(d)[1]), F32) for d in DELTAS] * 2 + [pltpu.VMEM((vel_arrays(d) * tile_of(d)[0], tile_of(d)[1]), F32) for d in DELTAS] * 2 + [
+            scratch_shapes=[pltpu.VMEM((offsets_of(pos_arrays)[1], 128), F32)] * 2 + [pltpu.VMEM((offsets_of(vel_arrays)[1], 128), F32)] * 2 + [
+                pltpu.VMEM((3, CAP), F32),
+                pltpu.VMEM((3, CAP), F32),
+                pltpu.VMEM((3, CAP), F32),
+                pltpu.VMEM((CAP,), jnp.int32),
+                pltpu.VMEM((CAP,), jnp.int32),
+                pltpu.SemaphoreType.DMA((5,)),
                 pltpu.VMEM((56, KPAD), F32),
                 pltpu.VMEM((112, 256), F32),
                 pltpu.VMEM((75, 32, 128), F32),
                 pltpu.VMEM((NF, 32, 128), F32),
                 pltpu.VMEM((192, 24, 128), F32),
                 pltpu.VMEM((8, 8, 128), F32),
-                pltpu.SemaphoreType.DMA((7,)),
-                pltpu.SemaphoreType.DMA((7,)),
-                pltpu.SemaphoreType.DMA((7,)),
-                pltpu.SemaphoreType.DMA((7,)),
-                pltpu.SemaphoreType.DMA((7,)),
-                pltpu.SemaphoreType.DMA((7,)),
+                pltpu.SemaphoreType.DMA,
+                pltpu.SemaphoreType.DMA,
+                pltpu.SemaphoreType.DMA,
+                pltpu.SemaphoreType.DMA,
+                pltpu.SemaphoreType.DMA,
+                pltpu.SemaphoreType.DMA,
             ],
             compiler_params=pltpu.CompilerParams(collective_id=0, has_side_effects=True),
         )(pos.T, vel.T, frc.T, ids, valid)

time: 15.1 us -> 14.1 us (0.934)
  Pallas kernels: 14.3 us -> 13.3 us
    pallas_call x1, Pallas kernels: 13 us -> 12 us  [local_step(): pl.pallas_call(kernel, out_shape=(pltpu.VMEM((3, CAP), F32),) * 3 + (pltp...]
where the time goes in v4:
time: 14.1 us; the launch traced here: 13.9 us
  Pallas kernels  13.3 us (94%)
  between operations  0.64 us (5%)
    pallas_call x1, Pallas kernels, local_step(): pl.pallas_call(kernel, out_shape=(pltpu.VMEM((3, CAP), F32),) * 3 + (pltp...  12 us
    pallas_call x1, Pallas kernels, local_step(): pl.pallas_call(finish, out_shape=(f3, f3, f3, i1, i1, jax.ShapeDtypeStruc...  1.28 us

profile of v4, /device:TPU:0, one launch (start us, length us, event | category | flops | bytes accessed | tf_op | source)
XLA Modules:
  0.0 13.9 jit_solution(15020286646575130686)
XLA Ops:
  0.6 12.0 %shard_map.100 = (f32[3,1728]{1,0:T(4,128)S(1)}, f32[3,1728]{1,0:T(4,128)S(1)}, f32[3,1728]{1,0:T(4,128)S(1)}, s32[1,1728]{1,0:T(1,128)S(1)}, s32[1,1728]{1,0:T(1,128)S(1)}, /*index=5*/f32[1,1]{1,0:T(1,128)}) custom-call(f32[3,1728]{1,0:T(4,128)} %bitcast.7, f32[3,1728]{1,0:T(4,128)} %bitcast.8, f32[3,1728]{1,0:T(4,128)} %bitcast.9, s32[1728]{0:T(1024)} %id_hbm.1, ...), custom_call_target="tpu_custom_call" | custom-call | tf_op jit(solution)/shard_map/pallas_call | solution.py:445
  12.6 1.3 %shard_map.101 = (f32[3,1728]{1,0:T(4,128)}, f32[3,1728]{1,0:T(4,128)}, f32[3,1728]{1,0:T(4,128)}, s32[1728]{0:T(1024)}, s32[1728]{0:T(1024)}, /*index=5*/f32[1,1]{1,0:T(1,128)}) custom-call(f32[3,1728]{1,0:T(4,128)S(1)} %get-tuple-element.18.pos_ref, f32[3,1728]{1,0:T(4,128)S(1)} %get-tuple-element.19.vel_ref, f32[3,1728]{1,0:T(4,128)S(1)} %get-tuple-element.20.frc_ref, ...), custom_call_target="tpu_custom_call" | custom-call | tf_op jit(solution)/shard_map/pallas_call | solution.py:472

commit v5 on v4

--- a/solution.py
+++ b/solution.py
@@ -58,7 +58,7 @@
 
 
 def pos_arrays(delta):
-    return 2 if delta[2] and (delta[0] or delta[1]) else 3
+    return 3
 
 
 def vel_arrays(delta):
@@ -69,28 +69,43 @@
     starts, row = {}, 0
     for delta in DELTAS:
         starts[delta] = row
-        rz, lanes = tile_of(delta)
-        row += arrays(delta) * rz * lanes // 128
+        row += part_rows(arrays, delta)
     return starts, row
 
 
-def to_delta(g, delta):
+def part_rows(arrays, delta):
+    rz, lanes = tile_of(delta)
+    if arrays is pos_arrays:
+        rz = 6 if delta[0] else 14
+    return arrays(delta) * rz * lanes // 128
+
+
+def to_delta(g_ref, f, delta):
     dz, dy, dx = delta
-    if dx:
-        xf = iota(g.shape, 1) & 15
-        g = jnp.where(xf < 3, pltpu.roll(g, 244, 1), jnp.where(xf >= 13, pltpu.roll(g, 12, 1), 0.0))
-    if dz:
-        row = iota((8, 256), 0)
-        g = jnp.where(row < 3, pltpu.roll(g[8:16], 4, 0), jnp.where(row >= 5, pltpu.roll(g[0:8], 4, 0), 0.0))
+    first = 24 * f + 4
+    halves = []
+    for h in range(2):
+        if dz:
+            row = iota((8, 128), 0)
+            halves.append(jnp.where(row < 3, g_ref[h, first + 12:first + 20, :], jnp.where(row >= 5, g_ref[h, first - 4:first + 4, :], 0.0)))
+        else:
+            halves.append(g_ref[h, first:first + 16, :])
+    lane = iota(halves[0].shape, 1)
+    xf = lane & 15
+
+    def along_x(x, turn):
+        if not dx:
+            return pltpu.roll(x, turn, 1) if turn else x
+        return jnp.where(xf < 3, pltpu.roll(x, (turn + 116) % 128, 1), jnp.where(xf >= 13, pltpu.roll(x, turn + 12, 1), 0.0))
+
     if dy:
-        lane = iota((g.shape[0], 128), 1)
-        g = jnp.where(lane < 48, pltpu.roll(g[:, 128:], 64, 1), jnp.where(lane >= 80, pltpu.roll(g[:, :128], 64, 1), 0.0))
-    return g
+        return [jnp.where(lane < 48, along_x(halves[1], 64), jnp.where(lane >= 80, along_x(halves[0], 64), 0.0))]
+    return [along_x(x, 0) for x in halves]
 
 
 def wide(b):
     lane = iota(b.shape, 1)
-    return jnp.concatenate([jnp.where(lane < 48, b, 0.0), jnp.where(lane >= 80, b, 0.0)], axis=1)
+    return [jnp.where(lane < 48, b, 0.0), jnp.where(lane >= 80, b, 0.0)]
 
 
 def tall(b):
@@ -98,57 +113,52 @@
     return jnp.concatenate([jnp.where(row < 3, b, 0.0), jnp.where(row >= 5, b, 0.0)], axis=0)
 
 
-def pack_pos(f, delta):
-    if pos_arrays(delta) == 3:
-        return f
-    return [f[0] + pltpu.roll(f[1], 6, 1), f[2]]
-
-
-def unpack_pos(a, delta):
-    if pos_arrays(delta) == 3:
-        return a
-    n = a[0].shape[1]
-    xf = iota(a[0].shape, 1) & 15
-    edge = (xf < 3) | (xf >= 13)
-    return [jnp.where(edge, a[0], 0.0), jnp.where(edge, pltpu.roll(a[0], n - 6, 1), 0.0), a[1]]
+def same(f, delta):
+    return f
 
 
 def pack_vel(f, delta):
     dz, dy, _ = delta
     if dz:
-        row = iota(f[0].shape, 0)
-        out = jnp.zeros_like(f[0])
-        for k in range(4):
-            out = jnp.where(row == 2 * k, jnp.broadcast_to(f[k][2:3], out.shape), out)
-            out = jnp.where(row == 2 * k + 1, jnp.broadcast_to(f[k][5:6], out.shape), out)
-        return [out]
+        row = iota(f[0][0].shape, 0)
+        outs = []
+        for j in range(len(f[0])):
+            out = jnp.zeros_like(f[0][j])
+            for k in range(4):
+                out = jnp.where(row == 2 * k, jnp.broadcast_to(f[k][j][2:3], out.shape), out)
+                out = jnp.where(row == 2 * k + 1, jnp.broadcast_to(f[k][j][5:6], out.shape), out)
+            outs.append(out)
+        return [outs]
     if dy:
+        f = [x[0] for x in f]
         group = iota(f[0].shape, 1) >> 4
         out = jnp.where((group == 2) | (group == 5), f[0], 0.0)
         out = jnp.where((group == 3) | (group == 6), pltpu.roll(f[1], 16, 1), out)
         out = jnp.where((group == 4) | (group == 7), pltpu.roll(f[2], 32, 1), out)
         out = jnp.where(group == 0, pltpu.roll(f[3], 96, 1), out)
-        return [jnp.where(group == 1, pltpu.roll(f[3], 64, 1), out)]
+        return [[jnp.where(group == 1, pltpu.roll(f[3], 64, 1), out)]]
     return f
 
 
 def unpack_vel(a, delta):
     dz, dy, _ = delta
     if dz:
-        row = iota(a[0].shape, 0)
-        return [jnp.where(row == 2, jnp.broadcast_to(a[0][2 * k:2 * k + 1], a[0].shape), jnp.where(row == 5, jnp.broadcast_to(a[0][2 * k + 1:2 * k + 2], a[0].shape), 0.0)) for k in range(4)]
+        row = iota(a[0][0].shape, 0)
+        return [[jnp.where(row == 2, jnp.broadcast_to(x[2 * k:2 * k + 1], x.shape), jnp.where(row == 5, jnp.broadcast_to(x[2 * k + 1:2 * k + 2], x.shape), 0.0)) for x in a[0]] for k in range(4)]
     if dy:
-        group = iota(a[0].shape, 1) >> 4
+        x = a[0][0]
+        group = iota(x.shape, 1) >> 4
         low, high = group == 2, group == 5
         both = low | high
-        last = jnp.where(low, pltpu.roll(a[0], 32, 1), jnp.where(high, pltpu.roll(a[0], 64, 1), 0.0))
-        return [jnp.where(both, a[0], 0.0), jnp.where(both, pltpu.roll(a[0], 112, 1), 0.0), jnp.where(both, pltpu.roll(a[0], 96, 1), 0.0), last]
+        last = jnp.where(low, pltpu.roll(x, 32, 1), jnp.where(high, pltpu.roll(x, 64, 1), 0.0))
+        return [[jnp.where(both, x, 0.0)], [jnp.where(both, pltpu.roll(x, 112, 1), 0.0)], [jnp.where(both, pltpu.roll(x, 96, 1), 0.0)], [last]]
     return a
 
 
 def merge(own, parts):
-    flat = own + parts[(0, 0, 1)] + wide(parts[(0, 1, 0)] + parts[(0, 1, 1)])
-    return flat + tall(parts[(1, 0, 0)] + parts[(1, 0, 1)] + wide(parts[(1, 1, 0)] + parts[(1, 1, 1)]))
+    near = wide(parts[(0, 1, 0)][0] + parts[(0, 1, 1)][0])
+    far = wide(parts[(1, 1, 0)][0] + parts[(1, 1, 1)][0])
+    return jnp.concatenate([(own[h] + parts[(0, 0, 1)][h] + near[h]) + tall(parts[(1, 0, 0)][h] + parts[(1, 0, 1)][h] + far[h]) for h in range(2)], axis=1)
 
 
 def kernel(pos_hbm, vel_hbm, frc_hbm, id_hbm, val_hbm, opos_ref, ovel_ref, ofrc_ref, oid_ref, oval_ref, oen_ref, *scratch):
@@ -166,6 +176,11 @@
     barrier = pltpu.get_barrier_semaphore()
     for delta in DELTAS:
         pl.semaphore_signal(barrier, inc=1, device_id=partner(delta), device_id_type=MESH_ID)
+
+    for f in range(NF):
+        for h in range(2):
+            g_ref[h, 24 * f:24 * f + 4, :] = jnp.zeros((4, 128), F32)
+            g_ref[h, 24 * f + 20:24 * f + 24, :] = jnp.zeros((4, 128), F32)
 
     for copy in loads:
         copy.wait()
@@ -201,42 +216,68 @@
 
     def exchange(src, dst, ssem, rsem, arrays):
         starts, total = offsets_of(arrays)
+        shift = 8 if arrays is pos_arrays else 0
         for delta in SEND_ORDER:
             rz, lanes = tile_of(delta)
-            part = pl.ds(starts[delta], arrays(delta) * rz * lanes // 128)
-            pltpu.make_async_remote_copy(src_ref=src.at[part], dst_ref=dst.at[part], send_sem=ssem, recv_sem=rsem, device_id=partner(delta), device_id_type=MESH_ID).start()
-        return pltpu.make_async_remote_copy(src_ref=src, dst_ref=dst, send_sem=ssem, recv_sem=rsem, device_id=partner(DELTAS[0]), device_id_type=MESH_ID)
+            part = pl.ds(starts[delta], part_rows(arrays, delta))
+            pltpu.make_async_remote_copy(src_ref=src.at[part], dst_ref=dst.at[pl.ds(starts[delta] + shift, part_rows(arrays, delta))], send_sem=ssem, recv_sem=rsem, device_id=partner(delta), device_id_type=MESH_ID).start()
+        return pltpu.make_async_remote_copy(src_ref=src, dst_ref=dst.at[pl.ds(shift, total)], send_sem=ssem, recv_sem=rsem, device_id=partner(DELTAS[0]), device_id_type=MESH_ID)
+
+    def keep_own(f, x):
+        for h in range(2):
+            g_ref[h, 24 * f + 4:24 * f + 20, :] = x[:, 128 * h:128 * h + 128]
 
     def fill(buf, fields, pack, arrays):
         starts, _ = offsets_of(arrays)
         for delta in DELTAS:
             rz, lanes = tile_of(delta)
             row = starts[delta]
-            for arr in pack([to_delta(f, delta) for f in fields], delta):
-                for j in range(lanes // 128):
-                    buf[row:row + rz, :] = arr[:, 128 * j:128 * j + 128]
-                    row += rz
-
-    def gather(own, buf, arrays, unpack):
+            for arr in pack([to_delta(g_ref, f, delta) for f in fields], delta):
+                for piece in arr:
+                    if arrays is not pos_arrays:
+                        buf[row:row + rz, :] = piece
+                        row += rz
+                    elif delta[0]:
+                        buf[row:row + 3, :] = piece[0:3]
+                        buf[row + 3:row + 6, :] = piece[5:8]
+                        row += 6
+                    else:
+                        buf[row:row + 14, :] = piece[1:15]
+                        row += 14
+
+    def gather(fields, buf, arrays, unpack):
         starts, _ = offsets_of(arrays)
         parts = {}
         for delta in DELTAS:
             rz, lanes = tile_of(delta)
             row = starts[delta]
             arrs = []
+            if arrays is pos_arrays:
+                for i in range(3):
+                    arrs.append([])
+                    for j in range(lanes // 128):
+                        if delta[0]:
+                            row8 = iota((8, 128), 0)
+                            arrs[i].append(jnp.where(row8 < 3, buf[row + 8:row + 16, :], jnp.where(row8 >= 5, buf[row + 6:row + 14, :], 0.0)))
+                            row += 6
+                        else:
+                            row16 = iota((16, 128), 0)
+                            arrs[i].append(jnp.where((row16 >= 1) & (row16 < 15), buf[row + 7:row + 23, :], 0.0))
+                            row += 14
+                parts[delta] = arrs
+                continue
             for i in range(arrays(delta)):
-                pieces = [buf[row + rz * j:row + rz * j + rz, :] for j in range(lanes // 128)]
-                row += rz * len(pieces)
-                arrs.append(pieces[0] if len(pieces) == 1 else jnp.concatenate(pieces, axis=1))
+                arrs.append([buf[row + rz * j:row + rz * j + rz, :] for j in range(lanes // 128)])
+                row += rz * lanes // 128
             parts[delta] = unpack(arrs, delta)
-        return [merge(own[f], {d: parts[d][f] for d in DELTAS}) for f in range(len(own))]
+        return [merge([g_ref[h, 24 * f + 4:24 * f + 20, :] for h in range(2)], {d: parts[d][i] for d in DELTAS}) for i, f in enumerate(fields)]
 
     lhs = jnp.concatenate([spread(8 * k + c) for k in range(3) for c in range(3)], axis=0)
     binned = dot_split(lhs, onehot, true)
     pos_own = [binned[16 * c:16 * c + 16] + binned[48 + 16 * c:64 + 16 * c] + binned[96 + 16 * c:112 + 16 * c] for c in range(3)]
-    fill(psend, pos_own, pack_pos, pos_arrays)
     for c in range(3):
-        g_ref[16 * c:16 * c + 16, :] = pos_own[c]
+        keep_own(c, pos_own[c])
+    fill(psend, range(3), same, pos_arrays)
     pl.semaphore_wait(barrier, 7)
     pos_all = exchange(psend, precv, psend_sem, precv_sem, pos_arrays)
 
@@ -244,13 +285,13 @@
     binned = dot_split(lhs, onehot, true)
     vel_own = [binned[16 * c:16 * c + 16] + binned[48 + 16 * c:64 + 16 * c] + binned[96 + 16 * c:112 + 16 * c] for c in range(3)]
     vel_own.append(binned[144:160] * 128.0 + binned[160:176])
-    fill(vsend, vel_own, pack_vel, vel_arrays)
     for c in range(4):
-        g_ref[48 + 16 * c:64 + 16 * c, :] = vel_own[c]
+        keep_own(3 + c, vel_own[c])
+    fill(vsend, range(3, 7), pack_vel, vel_arrays)
     vel_all = exchange(vsend, vrecv, vsend_sem, vrecv_sem, vel_arrays)
 
     pos_all.wait_recv()
-    fields = gather([g_ref[16 * c:16 * c + 16, :] for c in range(3)], precv, pos_arrays, unpack_pos)
+    fields = gather(range(3), precv, pos_arrays, same)
 
     present = fields[0] != 0.0
     lane = iota((16, 256), 1)
@@ -337,7 +378,7 @@
     energy_all = pltpu.make_async_remote_copy(src_ref=ebuf.at[pl.ds(0, 7)], dst_ref=ebuf.at[pl.ds(0, 7)], send_sem=esend_sem, recv_sem=erecv_sem, device_id=partner(DELTAS[0]), device_id_type=MESH_ID)
 
     vel_all.wait_recv()
-    for f, x in enumerate(gather([g_ref[48 + 16 * c:64 + 16 * c, :] for c in range(4)], vrecv, vel_arrays, unpack_vel)):
+    for f, x in enumerate(gather(range(3, 7), vrecv, vel_arrays, unpack_vel)):
         keep(3 + f, x)
     for c in range(1, 3):
         keep(c, fields[c])
@@ -447,7 +488,7 @@
             out_shape=(pltpu.VMEM((3, CAP), F32),) * 3 + (pltpu.VMEM((1, CAP), jnp.int32),) * 2 + (pltpu.VMEM((1, 1), F32),),
             in_specs=[pl.BlockSpec(memory_space=pltpu.HBM)] * 5,
             out_specs=(vmem,) * 6,
-            scratch_shapes=[pltpu.VMEM((offsets_of(pos_arrays)[1], 128), F32)] * 2 + [pltpu.VMEM((offsets_of(vel_arrays)[1], 128), F32)] * 2 + [
+            scratch_shapes=[pltpu.VMEM((offsets_of(pos_arrays)[1], 128), F32), pltpu.VMEM((offsets_of(pos_arrays)[1] + 16, 128), F32)] + [pltpu.VMEM((offsets_of(vel_arrays)[1], 128), F32)] * 2 + [
                 pltpu.VMEM((3, CAP), F32),
                 pltpu.VMEM((3, CAP), F32),
                 pltpu.VMEM((3, CAP), F32),
@@ -455,7 +496,7 @@
                 pltpu.VMEM((CAP,), jnp.int32),
                 pltpu.SemaphoreType.DMA((5,)),
                 pltpu.VMEM((56, KPAD), F32),
-                pltpu.VMEM((112, 256), F32),
+                pltpu.VMEM((2, 168, 128), F32),
                 pltpu.VMEM((75, 32, 128), F32),
                 pltpu.VMEM((NF, 32, 128), F32),
                 pltpu.VMEM((192, 24, 128), F32),

time: 14.1 us -> 14 us (level)
  no operation moved by 1% of the time
where the time goes in v5:
time: 14 us; the launch traced here: 13.8 us
  Pallas kernels  13.2 us (94%)
  between operations  0.64 us (5%)
    pallas_call x1, Pallas kernels, local_step(): pl.pallas_call(kernel, out_shape=(pltpu.VMEM((3, CAP), F32),) * 3 + (pltp...  11.9 us
    pallas_call x1, Pallas kernels, local_step(): pl.pallas_call(finish, out_shape=(f3, f3, f3, i1, i1, jax.ShapeDtypeStruc...  1.28 us

profile of v5, /device:TPU:0, one launch (start us, length us, event | category | flops | bytes accessed | tf_op | source)
XLA Modules:
  0.0 13.8 jit_solution(2086784503734330103)
XLA Ops:
  0.6 11.9 %shard_map.100 = (f32[3,1728]{1,0:T(4,128)S(1)}, f32[3,1728]{1,0:T(4,128)S(1)}, f32[3,1728]{1,0:T(4,128)S(1)}, s32[1,1728]{1,0:T(1,128)S(1)}, s32[1,1728]{1,0:T(1,128)S(1)}, /*index=5*/f32[1,1]{1,0:T(1,128)}) custom-call(f32[3,1728]{1,0:T(4,128)} %bitcast.7, f32[3,1728]{1,0:T(4,128)} %bitcast.8, f32[3,1728]{1,0:T(4,128)} %bitcast.9, s32[1728]{0:T(1024)} %id_hbm.1, ...), custom_call_target="tpu_custom_call" | custom-call | tf_op jit(solution)/shard_map/pallas_call | solution.py:486
  12.5 1.3 %shard_map.101 = (f32[3,1728]{1,0:T(4,128)}, f32[3,1728]{1,0:T(4,128)}, f32[3,1728]{1,0:T(4,128)}, s32[1728]{0:T(1024)}, s32[1728]{0:T(1024)}, /*index=5*/f32[1,1]{1,0:T(1,128)}) custom-call(f32[3,1728]{1,0:T(4,128)S(1)} %get-tuple-element.18.pos_ref, f32[3,1728]{1,0:T(4,128)S(1)} %get-tuple-element.19.vel_ref, f32[3,1728]{1,0:T(4,128)S(1)} %get-tuple-element.20.frc_ref, ...), custom_call_target="tpu_custom_call" | custom-call | tf_op jit(solution)/shard_map/pallas_call | solution.py:513

commit v6 on v5

--- a/solution.py
+++ b/solution.py
@@ -86,8 +86,7 @@
     halves = []
     for h in range(2):
         if dz:
-            row = iota((8, 128), 0)
-            halves.append(jnp.where(row < 3, g_ref[h, first + 12:first + 20, :], jnp.where(row >= 5, g_ref[h, first - 4:first + 4, :], 0.0)))
+            halves.append(jnp.where(iota((8, 128), 0) < 4, g_ref[h, first + 12:first + 20, :], g_ref[h, first + 4:first + 12, :]))
         else:
             halves.append(g_ref[h, first:first + 16, :])
     lane = iota(halves[0].shape, 1)
@@ -99,18 +98,14 @@
         return jnp.where(xf < 3, pltpu.roll(x, (turn + 116) % 128, 1), jnp.where(xf >= 13, pltpu.roll(x, turn + 12, 1), 0.0))
 
     if dy:
-        return [jnp.where(lane < 48, along_x(halves[1], 64), jnp.where(lane >= 80, along_x(halves[0], 64), 0.0))]
+        group = lane >> 4
+        return [jnp.where((group == 4) | (group == 5), along_x(halves[0], 64), jnp.where((group == 1) | (group == 2), 0.0, along_x(halves[1], 64)))]
     return [along_x(x, 0) for x in halves]
 
 
 def wide(b):
     lane = iota(b.shape, 1)
-    return [jnp.where(lane < 48, b, 0.0), jnp.where(lane >= 80, b, 0.0)]
-
-
-def tall(b):
-    row = iota(b.shape, 0)
-    return jnp.concatenate([jnp.where(row < 3, b, 0.0), jnp.where(row >= 5, b, 0.0)], axis=0)
+    return [jnp.where(lane < 16, b, 0.0), jnp.where(lane >= 48, b, 0.0)]
 
 
 def same(f, delta):
@@ -125,18 +120,18 @@
         for j in range(len(f[0])):
             out = jnp.zeros_like(f[0][j])
             for k in range(4):
-                out = jnp.where(row == 2 * k, jnp.broadcast_to(f[k][j][2:3], out.shape), out)
-                out = jnp.where(row == 2 * k + 1, jnp.broadcast_to(f[k][j][5:6], out.shape), out)
+                out = jnp.where(row == 2 * k, jnp.broadcast_to(f[k][j][6:7], out.shape), out)
+                out = jnp.where(row == 2 * k + 1, jnp.broadcast_to(f[k][j][1:2], out.shape), out)
             outs.append(out)
         return [outs]
     if dy:
         f = [x[0] for x in f]
         group = iota(f[0].shape, 1) >> 4
-        out = jnp.where((group == 2) | (group == 5), f[0], 0.0)
-        out = jnp.where((group == 3) | (group == 6), pltpu.roll(f[1], 16, 1), out)
-        out = jnp.where((group == 4) | (group == 7), pltpu.roll(f[2], 32, 1), out)
-        out = jnp.where(group == 0, pltpu.roll(f[3], 96, 1), out)
-        return [[jnp.where(group == 1, pltpu.roll(f[3], 64, 1), out)]]
+        out = jnp.where((group == 0) | (group == 3), f[0], 0.0)
+        out = jnp.where((group == 1) | (group == 4), pltpu.roll(f[1], 16, 1), out)
+        out = jnp.where((group == 2) | (group == 5), pltpu.roll(f[2], 32, 1), out)
+        out = jnp.where(group == 6, pltpu.roll(f[3], 96, 1), out)
+        return [[jnp.where(group == 7, pltpu.roll(f[3], 64, 1), out)]]
     return f
 
 
@@ -144,25 +139,29 @@
     dz, dy, _ = delta
     if dz:
         row = iota(a[0][0].shape, 0)
-        return [[jnp.where(row == 2, jnp.broadcast_to(x[2 * k:2 * k + 1], x.shape), jnp.where(row == 5, jnp.broadcast_to(x[2 * k + 1:2 * k + 2], x.shape), 0.0)) for x in a[0]] for k in range(4)]
+        return [[jnp.where(row == 6, jnp.broadcast_to(x[2 * k:2 * k + 1], x.shape), jnp.where(row == 1, jnp.broadcast_to(x[2 * k + 1:2 * k + 2], x.shape), 0.0)) for x in a[0]] for k in range(4)]
     if dy:
         x = a[0][0]
         group = iota(x.shape, 1) >> 4
-        low, high = group == 2, group == 5
+        low, high = group == 0, group == 3
         both = low | high
         last = jnp.where(low, pltpu.roll(x, 32, 1), jnp.where(high, pltpu.roll(x, 64, 1), 0.0))
         return [[jnp.where(both, x, 0.0)], [jnp.where(both, pltpu.roll(x, 112, 1), 0.0)], [jnp.where(both, pltpu.roll(x, 96, 1), 0.0)], [last]]
     return a
 
 
-def merge(own, parts):
+def merge_level(own, parts):
     near = wide(parts[(0, 1, 0)][0] + parts[(0, 1, 1)][0])
+    return [own[h] + parts[(0, 0, 1)][h] + near[h] for h in range(2)]
+
+
+def merge_above(own, parts):
     far = wide(parts[(1, 1, 0)][0] + parts[(1, 1, 1)][0])
-    return jnp.concatenate([(own[h] + parts[(0, 0, 1)][h] + near[h]) + tall(parts[(1, 0, 0)][h] + parts[(1, 0, 1)][h] + far[h]) for h in range(2)], axis=1)
+    return [own[h] + parts[(1, 0, 0)][h] + parts[(1, 0, 1)][h] + far[h] for h in range(2)]
 
 
 def kernel(pos_hbm, vel_hbm, frc_hbm, id_hbm, val_hbm, opos_ref, ovel_ref, ofrc_ref, oid_ref, oval_ref, oen_ref, *scratch):
-    psend, precv, vsend, vrecv, pos_ref, vel_ref, frc_ref, id_ref, val_ref, in_sem, atom_ref, g_ref, t_ref, q_ref, p_ref, ebuf, psend_sem, precv_sem, vsend_sem, vrecv_sem, esend_sem, erecv_sem = scratch
+    psend, precv, vsend, vrecv, pos_ref, vel_ref, frc_ref, id_ref, val_ref, in_sem, atom_ref, g_ref, t_ref, q_ref, p_ref, ebuf, psend_sem, precv_sem, pabove_sem, vsend_sem, vrecv_sem, esend_sem, erecv_sem = scratch
     loads = [pltpu.make_async_copy(src, dst, in_sem.at[i]) for i, (src, dst) in enumerate(((vel_hbm, vel_ref), (frc_hbm, frc_ref), (pos_hbm, pos_ref), (val_hbm, val_ref), (id_hbm, id_ref)))]
     for copy in loads:
         copy.start()
@@ -196,8 +195,8 @@
     live = val_ref[...].reshape(1, CAP) == 1
     ids = id_ref[...].reshape(1, CAP)
     atom_ref[:, pl.ds(KPAD - 128, 128)] = jnp.zeros((atom_ref.shape[0], 128), F32)
-    zi = jnp.where(live, cell[2:3, :], 0)
-    lo = jnp.where(live, cell[1:2, :] * 16 + cell[0:1, :], 0)
+    zi = jnp.where(live, (cell[2:3, :] - 4) & 15, 0)
+    lo = jnp.where(live, ((cell[1:2, :] - 2) & 15) * 16 + cell[0:1, :], 0)
     rows = list(split3(moved)) + list(split3(v_half))
     for k in range(6):
         atom_ref[8 * k:8 * k + 3, 0:CAP] = rows[k]
@@ -217,11 +216,12 @@
     def exchange(src, dst, ssem, rsem, arrays):
         starts, total = offsets_of(arrays)
         shift = 8 if arrays is pos_arrays else 0
+        cut = starts[(1, 0, 0)]
         for delta in SEND_ORDER:
             rz, lanes = tile_of(delta)
             part = pl.ds(starts[delta], part_rows(arrays, delta))
-            pltpu.make_async_remote_copy(src_ref=src.at[part], dst_ref=dst.at[pl.ds(starts[delta] + shift, part_rows(arrays, delta))], send_sem=ssem, recv_sem=rsem, device_id=partner(delta), device_id_type=MESH_ID).start()
-        return pltpu.make_async_remote_copy(src_ref=src, dst_ref=dst.at[pl.ds(shift, total)], send_sem=ssem, recv_sem=rsem, device_id=partner(DELTAS[0]), device_id_type=MESH_ID)
+            pltpu.make_async_remote_copy(src_ref=src.at[part], dst_ref=dst.at[pl.ds(starts[delta] + shift, part_rows(arrays, delta))], send_sem=ssem, recv_sem=rsem[delta[0]], device_id=partner(delta), device_id_type=MESH_ID).start()
+        return [pltpu.make_async_remote_copy(src_ref=src.at[pl.ds(lo, hi - lo)], dst_ref=dst.at[pl.ds(shift + lo, hi - lo)], send_sem=ssem, recv_sem=sem, device_id=partner(DELTAS[0]), device_id_type=MESH_ID) for lo, hi, sem in ((0, cut, rsem[0]), (cut, total, rsem[1]), (0, total, rsem[0]))]
 
     def keep_own(f, x):
         for h in range(2):
@@ -238,39 +238,54 @@
                         buf[row:row + rz, :] = piece
                         row += rz
                     elif delta[0]:
-                        buf[row:row + 3, :] = piece[0:3]
-                        buf[row + 3:row + 6, :] = piece[5:8]
+                        buf[row:row + 6, :] = piece[1:7]
                         row += 6
                     else:
-                        buf[row:row + 14, :] = piece[1:15]
+                        buf[row:row + 11, :] = piece[0:11]
+                        buf[row + 11:row + 14, :] = piece[13:16]
                         row += 14
 
-    def gather(fields, buf, arrays, unpack):
-        starts, _ = offsets_of(arrays)
+    def own_rows(f, start, count):
+        return [g_ref[h, 24 * f + 4 + start:24 * f + 4 + start + count, :] for h in range(2)]
+
+    def pos_parts(inner, deltas):
+        starts, _ = offsets_of(pos_arrays)
+        row8 = iota((8, 128), 0)
+        parts = [{} for _ in range(3)]
+        for delta in deltas:
+            rows = 6 if delta[0] else 14
+            row = starts[delta] + 8
+            for c in range(3):
+                parts[c][delta] = []
+                for _ in range(tile_of(delta)[1] // 128):
+                    if delta[0]:
+                        x = jnp.where((row8 >= 1) & (row8 < 7), precv[row - 1:row + 7, :], 0.0)
+                    elif inner:
+                        x = precv[row:row + 8, :]
+                    else:
+                        x = jnp.where(row8 < 3, precv[row + 8:row + 16, :], jnp.where(row8 >= 5, precv[row + 6:row + 14, :], 0.0))
+                    parts[c][delta].append(x)
+                    row += rows
+        return parts
+
+    def vel_fields():
+        starts, _ = offsets_of(vel_arrays)
         parts = {}
         for delta in DELTAS:
             rz, lanes = tile_of(delta)
             row = starts[delta]
             arrs = []
-            if arrays is pos_arrays:
-                for i in range(3):
-                    arrs.append([])
-                    for j in range(lanes // 128):
-                        if delta[0]:
-                            row8 = iota((8, 128), 0)
-                            arrs[i].append(jnp.where(row8 < 3, buf[row + 8:row + 16, :], jnp.where(row8 >= 5, buf[row + 6:row + 14, :], 0.0)))
-                            row += 6
-                        else:
-                            row16 = iota((16, 128), 0)
-                            arrs[i].append(jnp.where((row16 >= 1) & (row16 < 15), buf[row + 7:row + 23, :], 0.0))
-                            row += 14
-                parts[delta] = arrs
-                continue
-            for i in range(arrays(delta)):
-                arrs.append([buf[row + rz * j:row + rz * j + rz, :] for j in range(lanes // 128)])
+            for i in range(vel_arrays(delta)):
+                arrs.append([vrecv[row + rz * j:row + rz * j + rz, :] for j in range(lanes // 128)])
                 row += rz * lanes // 128
-            parts[delta] = unpack(arrs, delta)
-        return [merge([g_ref[h, 24 * f + 4:24 * f + 20, :] for h in range(2)], {d: parts[d][i] for d in DELTAS}) for i, f in enumerate(fields)]
+            parts[delta] = unpack_vel(arrs, delta)
+        out = []
+        for i in range(4):
+            mine = {d: parts[d][i] for d in DELTAS}
+            level = merge_level(own_rows(3 + i, 0, 16), mine)
+            above = merge_above([x[8:16] for x in level], mine)
+            out.append([[x[0:8] for x in level], above])
+        return out
 
     lhs = jnp.concatenate([spread(8 * k + c) for k in range(3) for c in range(3)], axis=0)
     binned = dot_split(lhs, onehot, true)
@@ -279,7 +294,7 @@
         keep_own(c, pos_own[c])
     fill(psend, range(3), same, pos_arrays)
     pl.semaphore_wait(barrier, 7)
-    pos_all = exchange(psend, precv, psend_sem, precv_sem, pos_arrays)
+    pos_all = exchange(psend, precv, psend_sem, (precv_sem, pabove_sem), pos_arrays)
 
     lhs = jnp.concatenate([spread(8 * k + c) for k in range(3, 6) for c in range(3)] + [spread(48), spread(49)], axis=0)
     binned = dot_split(lhs, onehot, true)
@@ -288,45 +303,66 @@
     for c in range(4):
         keep_own(3 + c, vel_own[c])
     fill(vsend, range(3, 7), pack_vel, vel_arrays)
-    vel_all = exchange(vsend, vrecv, vsend_sem, vrecv_sem, vel_arrays)
-
-    pos_all.wait_recv()
-    fields = gather(range(3), precv, pos_arrays, same)
-
-    present = fields[0] != 0.0
-    lane = iota((16, 256), 1)
-    frame = [lane & 15, lane >> 4, iota((16, 256), 0)]
+    vel_all = exchange(vsend, vrecv, vsend_sem, (vrecv_sem, vrecv_sem), vel_arrays)
+
     los = [bx, by, bz]
-    local = []
-    for c in range(3):
-        u = fields[c] - los[c].astype(F32) * BRICK
-        u = jnp.where(u < -0.5 * BRICK, u + BOX, jnp.where(u >= 1.5 * BRICK, u - BOX, u))
-        local.append(jnp.where(present, u, 64.0 + 4.0 * frame[c].astype(F32)))
-
-    def shift_in(s):
+
+    def localise(fields, start):
+        out = [[], [], []]
+        for h in range(2):
+            present = fields[0][h] != 0.0
+            lane = iota((8, 128), 1) + 128 * h
+            frame = [lane & 15, lane >> 4, iota((8, 128), 0) + start]
+            for c in range(3):
+                u = fields[c][h] - los[c].astype(F32) * BRICK
+                u = jnp.where(u < -0.5 * BRICK, u + BOX, jnp.where(u >= 1.5 * BRICK, u - BOX, u))
+                out[c].append(jnp.where(present, u, 64.0 + 4.0 * frame[c].astype(F32)))
+        return out
+
+    lane8 = iota((8, 128), 1)
+
+    def put_rows(ref, k, h, x, inner):
+        if inner:
+            ref[k, pl.ds(8 + h, 8, stride=2), :] = x
+        else:
+            ref[k, pl.ds(24 + h, 4, stride=2), :] = x[0:4]
+            ref[k, pl.ds(h, 4, stride=2), :] = x[4:8]
+
+    def shift_in(s, local, inner):
         dx, dy = SHIFTS[s]
+        left = 16 * dy + dx
+        for c in range(3):
+            a, b = local[c]
+            if left:
+                a, b = pltpu.roll(a, (-left) % 128, 1), pltpu.roll(b, (-left) % 128, 1)
+                here = lane8 < 128 - left if left > 0 else lane8 >= -left
+                a, b = jnp.where(here, a, b), jnp.where(here, b, a)
+            put_rows(t_ref, 3 * s + c, 0, a, inner)
+            put_rows(t_ref, 3 * s + c, 1, b, inner)
+
+    def keep(f, inner_rows, outer_rows):
         for h in range(2):
-            left = 32 + 96 * h + 16 * dy + dx
-            for c in range(3):
-                rolled = pltpu.roll(local[c], (256 - left) % 256, 1)
-                t_ref[3 * s + c, pl.ds(h, 16, stride=2), :] = rolled[:, 0:128]
-
-    def keep(f, x):
-        for h in range(2):
-            rolled = pltpu.roll(x, (256 - 32 - 96 * h) % 256, 1)
-            q_ref[f, pl.ds(h, 16, stride=2), :] = rolled[:, 0:128]
+            put_rows(q_ref, f, h, inner_rows[h], True)
+            put_rows(q_ref, f, h, outer_rows[h], False)
+
+    span = [4, 24]
 
     def load(dx, dy, dz):
         s = SHIFTS.index((dx, dy))
-        return [t_ref[3 * s + c, 4 + 2 * dz:28 + 2 * dz, :] for c in range(3)]
-
-    low_x = (iota((24, 128), 1) & 15) < 8
-    row24 = iota((24, 128), 0)
-    low_y = (row24 & 1) == 0
-    low_z = row24 < 12
+        return [t_ref[3 * s + c, span[0] + 2 * dz:span[0] + 2 * dz + span[1], :] for c in range(3)]
+
+    def low_x():
+        return (iota((span[1], 128), 1) & 15) < 8
+
+    def low_y():
+        return ((iota((span[1], 128), 0) & 1) == 0) & (iota((span[1], 128), 1) < 96)
+
+    def low_z():
+        return iota((span[1], 128), 0) + span[0] < 16
 
     def pick(mask, p, q):
-        return [jnp.where(mask, p[c], q[c]) for c in range(3)]
+        m = mask()
+        return [jnp.where(m, p[c], q[c]) for c in range(3)]
 
     def half(dx, dy, dz):
         return dy > 0 or (dy == 0 and (dx > 0 or (dx == 0 and dz > 0)))
@@ -345,47 +381,63 @@
     first.append(lambda: pick(low_z, load(2, 0, -2), load(2, 0, 2)))
     second.append(lambda: pick(low_z, load(-2, 0, -2), load(-2, 0, 2)))
 
-    for s, (dx, dy) in enumerate(SHIFTS):
-        if dy > 0 or (dy == 0 and dx >= 0):
-            shift_in(s)
-    mine = load(0, 0, 0)
-
-    def apart(nbr):
+    def apart(mine, nbr):
         ex, ey, ez = mine[0] - nbr[0], mine[1] - nbr[1], mine[2] - nbr[2]
-        r2 = ex * ex + ey * ey + ez * ez
-        r2 = jnp.minimum(r2, RCUT * RCUT)
+        r2 = jnp.minimum(ex * ex + ey * ey + ez * ez, RCUT * RCUT)
         return ex, ey, ez, r2, lax.rsqrt(r2)
 
-    sw, sr = jnp.zeros((24, 128), F32), jnp.zeros((24, 128), F32)
-    for i, nbr in enumerate(first):
-        ex, ey, ez, r2, inv = apart(nbr())
-        i2 = inv * inv
-        i6 = i2 * i2 * i2
-        sw = sw + i6 * (i6 - 1.0)
-        sr = sr + r2 * inv
-        for k, x in enumerate((ex, ey, ez, inv)):
-            p_ref[4 * i + k] = x
-    keep(0, fields[0])
+    def pair_energy(row):
+        span[:] = [row, 8]
+        mine = load(0, 0, 0)
+        sw, sr = jnp.zeros((8, 128), F32), jnp.zeros((8, 128), F32)
+        for i, nbr in enumerate(first):
+            ex, ey, ez, r2, inv = apart(mine, nbr())
+            i2 = inv * inv
+            i6 = i2 * i2 * i2
+            sw = sw + i6 * (i6 - 1.0)
+            sr = sr + r2 * inv
+            for k, x in enumerate((ex, ey, ez, inv)):
+                p_ref[4 * i + k, row - 4:row + 4, :] = x
+        return 4.0 * sw - DU_CUT * sr + (RCUT * DU_CUT - U_CUT) * len(first)
+
+    early = [s for s, (dx, dy) in enumerate(SHIFTS) if dy > 0 or (dy == 0 and dx >= 0)]
+    late = [s for s in range(25) if s not in early]
+    pos_all[0].wait_recv()
+    parts = pos_parts(True, DELTAS[:3])
+    inner = [merge_level(own_rows(c, 0, 8), parts[c]) for c in range(3)]
+    inner_local = localise(inner, 0)
+    for s in early:
+        shift_in(s, inner_local, True)
+    e_mid = pair_energy(12)
+    pos_all[1].wait_recv()
+    parts = pos_parts(False, DELTAS)
+    outer = [merge_above(merge_level(own_rows(c, 8, 8), parts[c]), parts[c]) for c in range(3)]
+    outer_local = localise(outer, 8)
+    for s in early:
+        shift_in(s, outer_local, False)
+    e_low, e_high = pair_energy(4), pair_energy(20)
+    span[:] = [4, 24]
+    keep(0, inner[0], outer[0])
     lane24 = iota((24, 128), 1)
     x24 = lane24 & 15
-    own = (lane24 < 96) & (x24 >= 2) & (x24 < 14) & (q_ref[0, 4:28, :] != 0.0)
-    energy = 4.0 * sw - DU_CUT * sr + (RCUT * DU_CUT - U_CUT) * len(first)
-    energy = jnp.where(own, energy, 0.0)
+    own = (((iota((24, 128), 0) & 1) == 0) | (lane24 < 64)) & (x24 >= 2) & (x24 < 14) & (q_ref[0, 4:28, :] != 0.0)
+    energy = jnp.where(own, jnp.concatenate([e_low, e_mid, e_high], axis=0), 0.0)
     me = bz * 4 + by * 2 + bx
     ebuf[me, :, :] = energy[0:8] + energy[8:16] + energy[16:24]
     for delta in SEND_ORDER:
         pltpu.make_async_remote_copy(src_ref=ebuf.at[me], dst_ref=ebuf.at[me], send_sem=esend_sem, recv_sem=erecv_sem, device_id=partner(delta), device_id_type=MESH_ID).start()
     energy_all = pltpu.make_async_remote_copy(src_ref=ebuf.at[pl.ds(0, 7)], dst_ref=ebuf.at[pl.ds(0, 7)], send_sem=esend_sem, recv_sem=erecv_sem, device_id=partner(DELTAS[0]), device_id_type=MESH_ID)
 
-    vel_all.wait_recv()
-    for f, x in enumerate(gather(range(3, 7), vrecv, vel_arrays, unpack_vel)):
-        keep(3 + f, x)
+    vel_all[2].wait_recv()
+    for f, (a, b) in enumerate(vel_fields()):
+        keep(3 + f, a, b)
     for c in range(1, 3):
-        keep(c, fields[c])
-
-    for s, (dx, dy) in enumerate(SHIFTS):
-        if not (dy > 0 or (dy == 0 and dx >= 0)):
-            shift_in(s)
+        keep(c, inner[c], outer[c])
+
+    for s in late:
+        shift_in(s, inner_local, True)
+        shift_in(s, outer_local, False)
+    mine = load(0, 0, 0)
 
     def push(acc, ex, ey, ez, inv):
         i2 = inv * inv
@@ -397,7 +449,7 @@
     for i in range(len(first)):
         acc = push(acc, *(p_ref[4 * i + k] for k in range(4)))
     for nbr in second:
-        ex, ey, ez, r2, inv = apart(nbr())
+        ex, ey, ez, r2, inv = apart(mine, nbr())
         acc = push(acc, ex, ey, ez, inv)
     force = [48.0 * acc[c] for c in range(3)]
 
@@ -457,7 +509,7 @@
     put(oid_ref, 0, field(27) * 128.0 + field(28))
     put(oval_ref, 0, field(29))
 
-    for copy in (pos_all, vel_all, energy_all):
+    for copy in (pos_all[2], vel_all[2], energy_all):
         copy.wait_send()
     energy_all.wait_recv()
     acc = ebuf[0]
@@ -507,6 +559,7 @@
                 pltpu.SemaphoreType.DMA,
                 pltpu.SemaphoreType.DMA,
                 pltpu.SemaphoreType.DMA,
+                pltpu.SemaphoreType.DMA,
             ],
             compiler_params=pltpu.CompilerParams(collective_id=0, has_side_effects=True),
         )(pos.T, vel.T, frc.T, ids, valid)

time: 14 us -> 13.8 us (0.986)
  Pallas kernels: 13.2 us -> 13 us
    pallas_call x1, Pallas kernels: 11.9 us -> 11.7 us  [local_step(): pl.pallas_call(kernel, out_shape=(pltpu.VMEM((3, CAP), F32),) * 3 + (pltp...]
where the time goes in v6:
time: 13.8 us; the launch traced here: 13.7 us
  Pallas kernels  13 us (94%)
  between operations  0.64 us (5%)
    pallas_call x1, Pallas kernels, local_step(): pl.pallas_call(kernel, out_shape=(pltpu.VMEM((3, CAP), F32),) * 3 + (pltp...  11.7 us
    pallas_call x1, Pallas kernels, local_step(): pl.pallas_call(finish, out_shape=(f3, f3, f3, i1, i1, jax.ShapeDtypeStruc...  1.28 us

profile of v6, /device:TPU:0, one launch (start us, length us, event | category | flops | bytes accessed | tf_op | source)
XLA Modules:
  0.0 13.7 jit_solution(13269509581154175428)
XLA Ops:
  0.6 11.7 %shard_map.100 = (f32[3,1728]{1,0:T(4,128)S(1)}, f32[3,1728]{1,0:T(4,128)S(1)}, f32[3,1728]{1,0:T(4,128)S(1)}, s32[1,1728]{1,0:T(1,128)S(1)}, s32[1,1728]{1,0:T(1,128)S(1)}, /*index=5*/f32[1,1]{1,0:T(1,128)}) custom-call(f32[3,1728]{1,0:T(4,128)} %bitcast.7, f32[3,1728]{1,0:T(4,128)} %bitcast.8, f32[3,1728]{1,0:T(4,128)} %bitcast.9, s32[1728]{0:T(1024)} %id_hbm.1, ...), custom_call_target="tpu_custom_call" | custom-call | tf_op jit(solution)/shard_map/pallas_call | solution.py:538
  12.4 1.3 %shard_map.101 = (f32[3,1728]{1,0:T(4,128)}, f32[3,1728]{1,0:T(4,128)}, f32[3,1728]{1,0:T(4,128)}, s32[1728]{0:T(1024)}, s32[1728]{0:T(1024)}, /*index=5*/f32[1,1]{1,0:T(1,128)}) custom-call(f32[3,1728]{1,0:T(4,128)S(1)} %get-tuple-element.18.pos_ref, f32[3,1728]{1,0:T(4,128)S(1)} %get-tuple-element.19.vel_ref, f32[3,1728]{1,0:T(4,128)S(1)} %get-tuple-element.20.frc_ref, ...), custom_call_target="tpu_custom_call" | custom-call | tf_op jit(solution)/shard_map/pallas_call | solution.py:566

commit v7 on v6

--- a/solution.py
+++ b/solution.py
@@ -515,7 +515,7 @@
     acc = ebuf[0]
     for k in range(1, 8):
         acc = acc + ebuf[k]
-    oen_ref[...] = jnp.sum(jnp.sum(acc, axis=0, keepdims=True), axis=1, keepdims=True)
+    oen_ref[...] = acc
 
 
 def finish(pos_ref, vel_ref, frc_ref, id_ref, val_ref, en_ref, opos_ref, ovel_ref, ofrc_ref, oid_ref, oval_ref, oen_ref):
@@ -524,7 +524,7 @@
     ofrc_ref[...] = frc_ref[...]
     oid_ref[...] = id_ref[...].reshape(CAP)
     oval_ref[...] = val_ref[...].reshape(CAP)
-    oen_ref[...] = en_ref[...]
+    oen_ref[...] = jnp.sum(jnp.sum(en_ref[...], axis=0, keepdims=True), axis=1, keepdims=True)
 
 
 def solution(mesh):
@@ -537,7 +537,7 @@
         i1 = jax.ShapeDtypeStruct((CAP,), jnp.int32)
         outs = pl.pallas_call(
             kernel,
-            out_shape=(pltpu.VMEM((3, CAP), F32),) * 3 + (pltpu.VMEM((1, CAP), jnp.int32),) * 2 + (pltpu.VMEM((1, 1), F32),),
+            out_shape=(pltpu.VMEM((3, CAP), F32),) * 3 + (pltpu.VMEM((1, CAP), jnp.int32),) * 2 + (pltpu.VMEM((8, 128), F32),),
             in_specs=[pl.BlockSpec(memory_space=pltpu.HBM)] * 5,
             out_specs=(vmem,) * 6,
             scratch_shapes=[pltpu.VMEM((offsets_of(pos_arrays)[1], 128), F32), pltpu.VMEM((offsets_of(pos_arrays)[1] + 16, 128), F32)] + [pltpu.VMEM((offsets_of(vel_arrays)[1], 128), F32)] * 2 + [

time: 13.8 us -> 12.6 us (0.913)
  Pallas kernels: 13 us -> 11.8 us
    pallas_call x1, Pallas kernels: 1.28 us -> 0.64 us  [local_step(): pl.pallas_call(finish, out_shape=(f3, f3, f3, i1, i1, jax.ShapeDtypeStruc...]
    pallas_call x1, Pallas kernels: 11.7 us -> 11.1 us  [local_step(): pl.pallas_call(kernel, out_shape=(pltpu.VMEM((3, CAP), F32),) * 3 + (pltp...]
where the time goes in v7:
time: 12.6 us; the launch traced here: 12.4 us
  Pallas kernels  11.8 us (94%)
  between operations  0.64 us (5%)
    pallas_call x1, Pallas kernels, local_step(): pl.pallas_call(kernel, out_shape=(pltpu.VMEM((3, CAP), F32),) * 3 + (pltp...  11.1 us
    pallas_call x1, Pallas kernels, local_step(): pl.pallas_call(finish, out_shape=(f3, f3, f3, i1, i1, jax.ShapeDtypeStruc...  0.64 us

profile of v7, /device:TPU:0, one launch (start us, length us, event | category | flops | bytes accessed | tf_op | source)
XLA Modules:
  0.0 12.4 jit_solution(14565213976097391558)
XLA Ops:
  0.6 11.1 %shard_map.100 = (f32[3,1728]{1,0:T(4,128)S(1)}, f32[3,1728]{1,0:T(4,128)S(1)}, f32[3,1728]{1,0:T(4,128)S(1)}, s32[1,1728]{1,0:T(1,128)S(1)}, s32[1,1728]{1,0:T(1,128)S(1)}, /*index=5*/f32[8,128]{1,0:T(8,128)S(1)}) custom-call(f32[3,1728]{1,0:T(4,128)} %bitcast.7, f32[3,1728]{1,0:T(4,128)} %bitcast.8, f32[3,1728]{1,0:T(4,128)} %bitcast.9, s32[1728]{0:T(1024)} %id_hbm.1, ...), custom_call_target="tpu_custom_call" | custom-call | tf_op jit(solution)/shard_map/pallas_call | solution.py:538
  11.8 0.6 %shard_map.101 = (f32[3,1728]{1,0:T(4,128)}, f32[3,1728]{1,0:T(4,128)}, f32[3,1728]{1,0:T(4,128)}, s32[1728]{0:T(1024)}, s32[1728]{0:T(1024)}, /*index=5*/f32[1,1]{1,0:T(1,128)}) custom-call(f32[3,1728]{1,0:T(4,128)S(1)} %get-tuple-element.18.pos_ref, f32[3,1728]{1,0:T(4,128)S(1)} %get-tuple-element.19.vel_ref, f32[3,1728]{1,0:T(4,128)S(1)} %get-tuple-element.20.frc_ref, ...), custom_call_target="tpu_custom_call" | custom-call | tf_op jit(solution)/shard_map/pallas_call | solution.py:566

commit v8 on v7

--- a/solution.py
+++ b/solution.py
@@ -25,6 +25,7 @@
 DU_CUT = (-48.0 * CUT6 * CUT6 + 24.0 * CUT6) / RCUT
 DELTAS = [(d >> 2 & 1, d >> 1 & 1, d & 1) for d in range(1, 8)]
 SEND_ORDER = [(1, 1, 0), (1, 1, 1), (0, 1, 0), (1, 0, 0), (0, 1, 1), (1, 0, 1), (0, 0, 1)]
+POS_ORDER = [(1, 1, 0), (0, 1, 0), (1, 1, 1), (0, 1, 1), (1, 0, 0), (1, 0, 1), (0, 0, 1)]
 SHIFTS = [(dx, dy) for dy in range(-2, 3) for dx in range(-2, 3)]
 NF = 7
 
@@ -162,20 +163,20 @@
 
 def kernel(pos_hbm, vel_hbm, frc_hbm, id_hbm, val_hbm, opos_ref, ovel_ref, ofrc_ref, oid_ref, oval_ref, oen_ref, *scratch):
     psend, precv, vsend, vrecv, pos_ref, vel_ref, frc_ref, id_ref, val_ref, in_sem, atom_ref, g_ref, t_ref, q_ref, p_ref, ebuf, psend_sem, precv_sem, pabove_sem, vsend_sem, vrecv_sem, esend_sem, erecv_sem = scratch
+    bz, by, bx = lax.axis_index("bz"), lax.axis_index("by"), lax.axis_index("bx")
+
+    true = bz >= 0
+
+    def partner(delta):
+        return (lax.rem(bz + delta[0], 2), lax.rem(by + delta[1], 2), lax.rem(bx + delta[2], 2))
+
+    barrier = pltpu.get_barrier_semaphore()
+    for delta in SEND_ORDER:
+        pl.semaphore_signal(barrier, inc=1, device_id=partner(delta), device_id_type=MESH_ID)
+
     loads = [pltpu.make_async_copy(src, dst, in_sem.at[i]) for i, (src, dst) in enumerate(((vel_hbm, vel_ref), (frc_hbm, frc_ref), (pos_hbm, pos_ref), (val_hbm, val_ref), (id_hbm, id_ref)))]
     for copy in loads:
         copy.start()
-    bz, by, bx = lax.axis_index("bz"), lax.axis_index("by"), lax.axis_index("bx")
-
-    true = bz >= 0
-
-    def partner(delta):
-        return (lax.rem(bz + delta[0], 2), lax.rem(by + delta[1], 2), lax.rem(bx + delta[2], 2))
-
-    barrier = pltpu.get_barrier_semaphore()
-    for delta in DELTAS:
-        pl.semaphore_signal(barrier, inc=1, device_id=partner(delta), device_id_type=MESH_ID)
-
     for f in range(NF):
         for h in range(2):
             g_ref[h, 24 * f:24 * f + 4, :] = jnp.zeros((4, 128), F32)
@@ -217,7 +218,7 @@
         starts, total = offsets_of(arrays)
         shift = 8 if arrays is pos_arrays else 0
         cut = starts[(1, 0, 0)]
-        for delta in SEND_ORDER:
+        for delta in POS_ORDER:
             rz, lanes = tile_of(delta)
             part = pl.ds(starts[delta], part_rows(arrays, delta))
             pltpu.make_async_remote_copy(src_ref=src.at[part], dst_ref=dst.at[pl.ds(starts[delta] + shift, part_rows(arrays, delta))], send_sem=ssem, recv_sem=rsem[delta[0]], device_id=partner(delta), device_id_type=MESH_ID).start()

time: 12.6 us -> 12.5 us (level)
  no operation moved by 1% of the time
where the time goes in v8:
time: 12.5 us; the launch traced here: 12.3 us
  Pallas kernels  11.7 us (94%)
  between operations  0.64 us (5%)
    pallas_call x1, Pallas kernels, local_step(): pl.pallas_call(kernel, out_shape=(pltpu.VMEM((3, CAP), F32),) * 3 + (pltp...  11.1 us
    pallas_call x1, Pallas kernels, local_step(): pl.pallas_call(finish, out_shape=(f3, f3, f3, i1, i1, jax.ShapeDtypeStruc...  0.64 us

profile of v8, /device:TPU:0, one launch (start us, length us, event | category | flops | bytes accessed | tf_op | source)
XLA Modules:
  0.0 12.3 jit_solution(15941003521982903609)
XLA Ops:
  0.6 11.1 %shard_map.100 = (f32[3,1728]{1,0:T(4,128)S(1)}, f32[3,1728]{1,0:T(4,128)S(1)}, f32[3,1728]{1,0:T(4,128)S(1)}, s32[1,1728]{1,0:T(1,128)S(1)}, s32[1,1728]{1,0:T(1,128)S(1)}, /*index=5*/f32[8,128]{1,0:T(8,128)S(1)}) custom-call(f32[3,1728]{1,0:T(4,128)} %bitcast.7, f32[3,1728]{1,0:T(4,128)} %bitcast.8, f32[3,1728]{1,0:T(4,128)} %bitcast.9, s32[1728]{0:T(1024)} %id_hbm.1, ...), custom_call_target="tpu_custom_call" | custom-call | tf_op jit(solution)/shard_map/pallas_call | solution.py:539
  11.7 0.6 %shard_map.101 = (f32[3,1728]{1,0:T(4,128)}, f32[3,1728]{1,0:T(4,128)}, f32[3,1728]{1,0:T(4,128)}, s32[1728]{0:T(1024)}, s32[1728]{0:T(1024)}, /*index=5*/f32[1,1]{1,0:T(1,128)}) custom-call(f32[3,1728]{1,0:T(4,128)S(1)} %get-tuple-element.18.pos_ref, f32[3,1728]{1,0:T(4,128)S(1)} %get-tuple-element.19.vel_ref, f32[3,1728]{1,0:T(4,128)S(1)} %get-tuple-element.20.frc_ref, ...), custom_call_target="tpu_custom_call" | custom-call | tf_op jit(solution)/shard_map/pallas_call | solution.py:567

commit v9 on v8

--- a/solution.py
+++ b/solution.py
@@ -77,7 +77,7 @@
 def part_rows(arrays, delta):
     rz, lanes = tile_of(delta)
     if arrays is pos_arrays:
-        rz = 6 if delta[0] else 14
+        rz = 6 if delta[0] else 8 if delta == (0, 1, 1) else 14
     return arrays(delta) * rz * lanes // 128
 
 
@@ -102,6 +102,19 @@
         group = lane >> 4
         return [jnp.where((group == 4) | (group == 5), along_x(halves[0], 64), jnp.where((group == 1) | (group == 2), 0.0, along_x(halves[1], 64)))]
     return [along_x(x, 0) for x in halves]
+
+
+def folded(g_ref, f):
+    first = 24 * f + 4
+    row, moved = iota((8, 128), 0), (iota((8, 128), 1) - 6) & 127
+    xf, group = moved & 15, moved >> 4
+    outer = [jnp.where(row < 3, g_ref[h, first + 8:first + 16, :], g_ref[h, first + 10:first + 18, :]) for h in range(2)]
+
+    def along_x(x):
+        return jnp.where(xf < 3, pltpu.roll(x, 58, 1), jnp.where(xf >= 13, pltpu.roll(x, 82, 1), 0.0))
+
+    out = jnp.where((group == 4) | (group == 5), along_x(outer[0]), jnp.where((group == 1) | (group == 2), 0.0, along_x(outer[1])))
+    return to_delta(g_ref, f, (0, 1, 1))[0][0:8] + jnp.where(row < 6, out, 0.0)
 
 
 def wide(b):
@@ -233,6 +246,10 @@
         for delta in DELTAS:
             rz, lanes = tile_of(delta)
             row = starts[delta]
+            if arrays is pos_arrays and delta == (0, 1, 1):
+                for f in fields:
+                    buf[row + 8 * f:row + 8 * f + 8, :] = folded(g_ref, f)
+                continue
             for arr in pack([to_delta(g_ref, f, delta) for f in fields], delta):
                 for piece in arr:
                     if arrays is not pos_arrays:
@@ -254,13 +271,19 @@
         row8 = iota((8, 128), 0)
         parts = [{} for _ in range(3)]
         for delta in deltas:
-            rows = 6 if delta[0] else 14
+            rows = 6 if delta[0] else 8 if delta == (0, 1, 1) else 14
             row = starts[delta] + 8
             for c in range(3):
                 parts[c][delta] = []
                 for _ in range(tile_of(delta)[1] // 128):
                     if delta[0]:
                         x = jnp.where((row8 >= 1) & (row8 < 7), precv[row - 1:row + 7, :], 0.0)
+                    elif delta == (0, 1, 1):
+                        xf = iota((8, 128), 1) & 15
+                        x = precv[row:row + 8, :]
+                        if not inner:
+                            x = pltpu.roll(jnp.where(row8 < 3, x, precv[row - 2:row + 6, :]), 122, 1)
+                        x = jnp.where(((xf < 3) | (xf >= 13)) & (inner | (row8 < 3) | (row8 >= 5)), x, 0.0)
                     elif inner:
                         x = precv[row:row + 8, :]
                     else:
@@ -347,9 +370,12 @@
             put_rows(q_ref, f, h, outer_rows[h], False)
 
     span = [4, 24]
+    row8 = iota((8, 128), 0)
 
     def load(dx, dy, dz):
         s = SHIFTS.index((dx, dy))
+        if span[0] is None:
+            return [jnp.where(row8 < 4, t_ref[3 * s + c, 4 + 2 * dz:12 + 2 * dz, :], t_ref[3 * s + c, 20 + 2 * dz:28 + 2 * dz, :]) for c in range(3)]
         return [t_ref[3 * s + c, span[0] + 2 * dz:span[0] + 2 * dz + span[1], :] for c in range(3)]
 
     def low_x():
@@ -359,7 +385,7 @@
         return ((iota((span[1], 128), 0) & 1) == 0) & (iota((span[1], 128), 1) < 96)
 
     def low_z():
-        return iota((span[1], 128), 0) + span[0] < 16
+        return row8 < 4 if span[0] is None else iota((span[1], 128), 0) + span[0] < 16
 
     def pick(mask, p, q):
         m = mask()
@@ -397,8 +423,6 @@
             i6 = i2 * i2 * i2
             sw = sw + i6 * (i6 - 1.0)
             sr = sr + r2 * inv
-            for k, x in enumerate((ex, ey, ez, inv)):
-                p_ref[4 * i + k, row - 4:row + 4, :] = x
         return 4.0 * sw - DU_CUT * sr + (RCUT * DU_CUT - U_CUT) * len(first)
 
     early = [s for s, (dx, dy) in enumerate(SHIFTS) if dy > 0 or (dy == 0 and dx >= 0)]
@@ -409,20 +433,25 @@
     inner_local = localise(inner, 0)
     for s in early:
         shift_in(s, inner_local, True)
-    e_mid = pair_energy(12)
-    pos_all[1].wait_recv()
-    parts = pos_parts(False, DELTAS)
-    outer = [merge_above(merge_level(own_rows(c, 8, 8), parts[c]), parts[c]) for c in range(3)]
+    parts = pos_parts(False, DELTAS[:3])
+    outer = [merge_level(own_rows(c, 8, 8), parts[c]) for c in range(3)]
     outer_local = localise(outer, 8)
     for s in early:
         shift_in(s, outer_local, False)
-    e_low, e_high = pair_energy(4), pair_energy(20)
+    middle = [pair_energy(8), pair_energy(16)]
+    pos_all[1].wait_recv()
+    parts = pos_parts(False, DELTAS[3:])
+    outer = [merge_above(outer[c], parts[c]) for c in range(3)]
+    outer_local = localise(outer, 8)
+    for s in early:
+        shift_in(s, outer_local, False)
+    edges = pair_energy(None)
     span[:] = [4, 24]
     keep(0, inner[0], outer[0])
     lane24 = iota((24, 128), 1)
     x24 = lane24 & 15
     own = (((iota((24, 128), 0) & 1) == 0) | (lane24 < 64)) & (x24 >= 2) & (x24 < 14) & (q_ref[0, 4:28, :] != 0.0)
-    energy = jnp.where(own, jnp.concatenate([e_low, e_mid, e_high], axis=0), 0.0)
+    energy = jnp.where(own, jnp.concatenate([edges[0:4]] + middle + [edges[4:8]], axis=0), 0.0)
     me = bz * 4 + by * 2 + bx
     ebuf[me, :, :] = energy[0:8] + energy[8:16] + energy[16:24]
     for delta in SEND_ORDER:
@@ -447,9 +476,7 @@
         return (acc[0] + fr * ex, acc[1] + fr * ey, acc[2] + fr * ez)
 
     acc = tuple(jnp.zeros((24, 128), F32) for _ in range(3))
-    for i in range(len(first)):
-        acc = push(acc, *(p_ref[4 * i + k] for k in range(4)))
-    for nbr in second:
+    for nbr in first + second:
         ex, ey, ez, r2, inv = apart(mine, nbr())
         acc = push(acc, ex, ey, ez, inv)
     force = [48.0 * acc[c] for c in range(3)]
@@ -552,7 +579,7 @@
                 pltpu.VMEM((2, 168, 128), F32),
                 pltpu.VMEM((75, 32, 128), F32),
                 pltpu.VMEM((NF, 32, 128), F32),
-                pltpu.VMEM((192, 24, 128), F32),
+                pltpu.VMEM((8, 24, 128), F32),
                 pltpu.VMEM((8, 8, 128), F32),
                 pltpu.SemaphoreType.DMA,
                 pltpu.SemaphoreType.DMA,

time: 12.5 us -> 12.3 us (0.984)
  Pallas kernels: 11.7 us -> 11.5 us
    pallas_call x1, Pallas kernels: 11.1 us -> 10.9 us  [local_step(): pl.pallas_call(kernel, out_shape=(pltpu.VMEM((3, CAP), F32),) * 3 + (pltp...]
where the time goes in v9:
time: 12.3 us; the launch traced here: 12.1 us
  Pallas kernels  11.5 us (93%)
  between operations  0.64 us (5%)
    pallas_call x1, Pallas kernels, local_step(): pl.pallas_call(kernel, out_shape=(pltpu.VMEM((3, CAP), F32),) * 3 + (pltp...  10.9 us
    pallas_call x1, Pallas kernels, local_step(): pl.pallas_call(finish, out_shape=(f3, f3, f3, i1, i1, jax.ShapeDtypeStruc...  0.64 us

profile of v9, /device:TPU:0, one launch (start us, length us, event | category | flops | bytes accessed | tf_op | source)
XLA Modules:
  0.0 12.1 jit_solution(17358354379526659638)
XLA Ops:
  0.6 10.9 %shard_map.100 = (f32[3,1728]{1,0:T(4,128)S(1)}, f32[3,1728]{1,0:T(4,128)S(1)}, f32[3,1728]{1,0:T(4,128)S(1)}, s32[1,1728]{1,0:T(1,128)S(1)}, s32[1,1728]{1,0:T(1,128)S(1)}, /*index=5*/f32[8,128]{1,0:T(8,128)S(1)}) custom-call(f32[3,1728]{1,0:T(4,128)} %bitcast.7, f32[3,1728]{1,0:T(4,128)} %bitcast.8, f32[3,1728]{1,0:T(4,128)} %bitcast.9, s32[1728]{0:T(1024)} %id_hbm.1, ...), custom_call_target="tpu_custom_call" | custom-call | tf_op jit(solution)/shard_map/pallas_call | solution.py:566
  11.5 0.6 %shard_map.101 = (f32[3,1728]{1,0:T(4,128)}, f32[3,1728]{1,0:T(4,128)}, f32[3,1728]{1,0:T(4,128)}, s32[1728]{0:T(1024)}, s32[1728]{0:T(1024)}, /*index=5*/f32[1,1]{1,0:T(1,128)}) custom-call(f32[3,1728]{1,0:T(4,128)S(1)} %get-tuple-element.18.pos_ref, f32[3,1728]{1,0:T(4,128)S(1)} %get-tuple-element.19.vel_ref, f32[3,1728]{1,0:T(4,128)S(1)} %get-tuple-element.20.frc_ref, ...), custom_call_target="tpu_custom_call" | custom-call | tf_op jit(solution)/shard_map/pallas_call | solution.py:594

commit v10 on v9

--- a/solution.py
+++ b/solution.py
@@ -175,7 +175,10 @@
 
 
 def kernel(pos_hbm, vel_hbm, frc_hbm, id_hbm, val_hbm, opos_ref, ovel_ref, ofrc_ref, oid_ref, oval_ref, oen_ref, *scratch):
-    psend, precv, vsend, vrecv, pos_ref, vel_ref, frc_ref, id_ref, val_ref, in_sem, atom_ref, g_ref, t_ref, q_ref, p_ref, ebuf, psend_sem, precv_sem, pabove_sem, vsend_sem, vrecv_sem, esend_sem, erecv_sem = scratch
+    send_ref, precv, vrecv, in_ref, id_ref, val_ref, in_sem, atom_ref, g_ref, t_ref, q_ref, p_ref, ebuf, send_sem, precv_sem, pabove_sem, vrecv_sem, erecv_sem = scratch
+    pos_rows, vel_rows = offsets_of(pos_arrays)[1], offsets_of(vel_arrays)[1]
+    psend, vsend = send_ref.at[pl.ds(0, pos_rows)], send_ref.at[pl.ds(pos_rows, vel_rows)]
+    vel_ref, frc_ref, pos_ref = (in_ref.at[k] for k in range(3))
     bz, by, bx = lax.axis_index("bz"), lax.axis_index("by"), lax.axis_index("bx")
 
     true = bz >= 0
@@ -187,7 +190,7 @@
     for delta in SEND_ORDER:
         pl.semaphore_signal(barrier, inc=1, device_id=partner(delta), device_id_type=MESH_ID)
 
-    loads = [pltpu.make_async_copy(src, dst, in_sem.at[i]) for i, (src, dst) in enumerate(((vel_hbm, vel_ref), (frc_hbm, frc_ref), (pos_hbm, pos_ref), (val_hbm, val_ref), (id_hbm, id_ref)))]
+    loads = [pltpu.make_async_copy(src, dst, in_sem.at[max(i - 2, 0)]) for i, (src, dst) in enumerate(((vel_hbm, vel_ref), (frc_hbm, frc_ref), (pos_hbm, pos_ref), (val_hbm, val_ref), (id_hbm, id_ref)))]
     for copy in loads:
         copy.start()
     for f in range(NF):
@@ -195,7 +198,7 @@
             g_ref[h, 24 * f:24 * f + 4, :] = jnp.zeros((4, 128), F32)
             g_ref[h, 24 * f + 20:24 * f + 24, :] = jnp.zeros((4, 128), F32)
 
-    for copy in loads:
+    for copy in [pltpu.make_async_copy(in_ref, in_ref, in_sem.at[0])] + loads[3:]:
         copy.wait()
     v_half = vel_ref[...] + (0.5 * TIME_STEP) * frc_ref[...]
     moved = pos_ref[...] + TIME_STEP * v_half
@@ -318,7 +321,7 @@
         keep_own(c, pos_own[c])
     fill(psend, range(3), same, pos_arrays)
     pl.semaphore_wait(barrier, 7)
-    pos_all = exchange(psend, precv, psend_sem, (precv_sem, pabove_sem), pos_arrays)
+    pos_all = exchange(psend, precv, send_sem, (precv_sem, pabove_sem), pos_arrays)
 
     lhs = jnp.concatenate([spread(8 * k + c) for k in range(3, 6) for c in range(3)] + [spread(48), spread(49)], axis=0)
     binned = dot_split(lhs, onehot, true)
@@ -327,7 +330,7 @@
     for c in range(4):
         keep_own(3 + c, vel_own[c])
     fill(vsend, range(3, 7), pack_vel, vel_arrays)
-    vel_all = exchange(vsend, vrecv, vsend_sem, (vrecv_sem, vrecv_sem), vel_arrays)
+    vel_all = exchange(vsend, vrecv, send_sem, (vrecv_sem, vrecv_sem), vel_arrays)
 
     los = [bx, by, bz]
 
@@ -455,8 +458,8 @@
     me = bz * 4 + by * 2 + bx
     ebuf[me, :, :] = energy[0:8] + energy[8:16] + energy[16:24]
     for delta in SEND_ORDER:
-        pltpu.make_async_remote_copy(src_ref=ebuf.at[me], dst_ref=ebuf.at[me], send_sem=esend_sem, recv_sem=erecv_sem, device_id=partner(delta), device_id_type=MESH_ID).start()
-    energy_all = pltpu.make_async_remote_copy(src_ref=ebuf.at[pl.ds(0, 7)], dst_ref=ebuf.at[pl.ds(0, 7)], send_sem=esend_sem, recv_sem=erecv_sem, device_id=partner(DELTAS[0]), device_id_type=MESH_ID)
+        pltpu.make_async_remote_copy(src_ref=ebuf.at[me], dst_ref=ebuf.at[me], send_sem=send_sem, recv_sem=erecv_sem, device_id=partner(delta), device_id_type=MESH_ID).start()
+    energy_all = pltpu.make_async_remote_copy(src_ref=ebuf.at[pl.ds(0, 7)], dst_ref=ebuf.at[pl.ds(0, 7)], send_sem=send_sem, recv_sem=erecv_sem, device_id=partner(DELTAS[0]), device_id_type=MESH_ID)
 
     vel_all[2].wait_recv()
     for f, (a, b) in enumerate(vel_fields()):
@@ -537,8 +540,7 @@
     put(oid_ref, 0, field(27) * 128.0 + field(28))
     put(oval_ref, 0, field(29))
 
-    for copy in (pos_all[2], vel_all[2], energy_all):
-        copy.wait_send()
+    pltpu.make_async_remote_copy(src_ref=send_ref, dst_ref=send_ref, send_sem=send_sem, recv_sem=precv_sem, device_id=partner(DELTAS[0]), device_id_type=MESH_ID).wait_send()
     energy_all.wait_recv()
     acc = ebuf[0]
     for k in range(1, 8):
@@ -568,21 +570,17 @@
             out_shape=(pltpu.VMEM((3, CAP), F32),) * 3 + (pltpu.VMEM((1, CAP), jnp.int32),) * 2 + (pltpu.VMEM((8, 128), F32),),
             in_specs=[pl.BlockSpec(memory_space=pltpu.HBM)] * 5,
             out_specs=(vmem,) * 6,
-            scratch_shapes=[pltpu.VMEM((offsets_of(pos_arrays)[1], 128), F32), pltpu.VMEM((offsets_of(pos_arrays)[1] + 16, 128), F32)] + [pltpu.VMEM((offsets_of(vel_arrays)[1], 128), F32)] * 2 + [
-                pltpu.VMEM((3, CAP), F32),
-                pltpu.VMEM((3, CAP), F32),
-                pltpu.VMEM((3, CAP), F32),
+            scratch_shapes=[pltpu.VMEM((offsets_of(pos_arrays)[1] + offsets_of(vel_arrays)[1] + 56, 128), F32), pltpu.VMEM((offsets_of(pos_arrays)[1] + 16, 128), F32), pltpu.VMEM((offsets_of(vel_arrays)[1], 128), F32)] + [
+                pltpu.VMEM((3, 3, CAP), F32),
                 pltpu.VMEM((CAP,), jnp.int32),
                 pltpu.VMEM((CAP,), jnp.int32),
-                pltpu.SemaphoreType.DMA((5,)),
+                pltpu.SemaphoreType.DMA((3,)),
                 pltpu.VMEM((56, KPAD), F32),
                 pltpu.VMEM((2, 168, 128), F32),
                 pltpu.VMEM((75, 32, 128), F32),
                 pltpu.VMEM((NF, 32, 128), F32),
                 pltpu.VMEM((8, 24, 128), F32),
                 pltpu.VMEM((8, 8, 128), F32),
-                pltpu.SemaphoreType.DMA,
-                pltpu.SemaphoreType.DMA,
                 pltpu.SemaphoreType.DMA,
                 pltpu.SemaphoreType.DMA,
                 pltpu.SemaphoreType.DMA,

time: 12.3 us -> 12.3 us (level)
  no operation moved by 1% of the time
where the time goes in v10:
time: 12.3 us; the launch traced here: 12.1 us
  Pallas kernels  11.5 us (93%)
  between operations  0.64 us (5%)
    pallas_call x1, Pallas kernels, local_step(): pl.pallas_call(kernel, out_shape=(pltpu.VMEM((3, CAP), F32),) * 3 + (pltp...  10.8 us
    pallas_call x1, Pallas kernels, local_step(): pl.pallas_call(finish, out_shape=(f3, f3, f3, i1, i1, jax.ShapeDtypeStruc...  0.64 us

profile of v10, /device:TPU:0, one launch (start us, length us, event | category | flops | bytes accessed | tf_op | source)
XLA Modules:
  0.0 12.1 jit_solution(15314845429355397703)
XLA Ops:
  0.6 10.8 %shard_map.100 = (f32[3,1728]{1,0:T(4,128)S(1)}, f32[3,1728]{1,0:T(4,128)S(1)}, f32[3,1728]{1,0:T(4,128)S(1)}, s32[1,1728]{1,0:T(1,128)S(1)}, s32[1,1728]{1,0:T(1,128)S(1)}, /*index=5*/f32[8,128]{1,0:T(8,128)S(1)}) custom-call(f32[3,1728]{1,0:T(4,128)} %bitcast.7, f32[3,1728]{1,0:T(4,128)} %bitcast.8, f32[3,1728]{1,0:T(4,128)} %bitcast.9, s32[1728]{0:T(1024)} %id_hbm.1, ...), custom_call_target="tpu_custom_call" | custom-call | tf_op jit(solution)/shard_map/pallas_call | solution.py:568
  11.5 0.6 %shard_map.101 = (f32[3,1728]{1,0:T(4,128)}, f32[3,1728]{1,0:T(4,128)}, f32[3,1728]{1,0:T(4,128)}, s32[1728]{0:T(1024)}, s32[1728]{0:T(1024)}, /*index=5*/f32[1,1]{1,0:T(1,128)}) custom-call(f32[3,1728]{1,0:T(4,128)S(1)} %get-tuple-element.18.pos_ref, f32[3,1728]{1,0:T(4,128)S(1)} %get-tuple-element.19.vel_ref, f32[3,1728]{1,0:T(4,128)S(1)} %get-tuple-element.20.frc_ref, ...), custom_call_target="tpu_custom_call" | custom-call | tf_op jit(solution)/shard_map/pallas_call | solution.py:592
